TPU v7x, 32 devices: a whole 2x2x4 slice. The times are simulated.
32 devices in a mesh: replica: 16 (over z, x, core), group: 2 (over y).
Axes of the slice: x: 2, y: 2, z: 4, core: 2. Of those that a mesh axis runs over, the one named last changes fastest.
Arguments:
- inputs: bfloat16 [640, 197, 384], P(('replica', 'group')), may hold values from -6 to 6
- cotangent: bfloat16 [640, 197, 384], P(('replica', 'group')), may hold values from -6 to 6
- gain_one: bfloat16 [384], P('group'), may hold values from 0.5 to 1.5
- shift_one: bfloat16 [384], P('group'), may hold values from -3 to 3
- w_qkv: bfloat16 [384, 1152], P('group'), may hold values from -2 to 2
- b_query: bfloat16 [384], P('group'), may hold values from -3 to 3
- b_value: bfloat16 [384], P('group'), may hold values from -3 to 3
- w_proj: bfloat16 [384, 384], P('group'), may hold values from -0.875 to 0.875
- b_proj: bfloat16 [384], P('group'), may hold values from -3 to 3
- gain_two: bfloat16 [384], P('group'), may hold values from 0.5 to 1.5
- shift_two: bfloat16 [384], P('group'), may hold values from -3 to 3
- w_fc1: bfloat16 [384, 1536], P('group'), may hold values from -0.3125 to 0.3125
- b_fc1: bfloat16 [1536], P('group'), may hold values from -3 to 3
- w_fc2: bfloat16 [1536, 384], P('group'), may hold values from -0.15625 to 0.15625
- b_fc2: bfloat16 [384], P('group'), may hold values from -3 to 3
Outputs:
- outputs: bfloat16 [640, 197, 384], P(('replica', 'group'))
- grad_inputs: float32 [640, 197, 384], P(('replica', 'group'))
- grad_gain_one: float32 [384], P('group')
- grad_shift_one: float32 [384], P('group')
- grad_w_qkv: float32 [384, 1152], P('group')
- grad_b_query: float32 [384], P('group')
- grad_b_value: float32 [384], P('group')
- grad_w_proj: float32 [384, 384], P('group')
- grad_b_proj: float32 [384], P('group')
- grad_gain_two: float32 [384], P('group')
- grad_shift_two: float32 [384], P('group')
- grad_w_fc1: float32 [384, 1536], P('group')
- grad_b_fc1: float32 [1536], P('group')
- grad_w_fc2: float32 [1536, 384], P('group')
- grad_b_fc2: float32 [384], P('group')
All inputs are finite; a program needn't handle non-finite values.
Results may differ from a plain program's by a relative error of at most 0.012.
Values may be sent and summed in bfloat16 or wider, within the bound.
A program may use at most 256 MiB of HBM per device.

v0:
```python
import jax
import jax.numpy as jnp
from jax import lax
from jax.sharding import PartitionSpec as P

HEADS = 6


epsilon = 1e-06


def product(left, right):
    return jnp.dot(left, right, preferred_element_type=jnp.float32)


def product_left_t(left, right):
    return lax.dot_general(
        left, right, (((0,), (0,)), ((), ())), preferred_element_type=jnp.float32
    )


def product_right_t(left, right):
    return lax.dot_general(
        left, right, (((1,), (1,)), ((), ())), preferred_element_type=jnp.float32
    )


def layer_norm(token_rows, gain_row, shift_row):
    centre = jnp.mean(token_rows, axis=-1, keepdims=True)
    centered = token_rows - centre
    inverse = lax.rsqrt(jnp.mean(centered * centered, axis=-1, keepdims=True) + epsilon)
    normed = centered * inverse
    hidden = (normed * gain_row.astype(jnp.float32) + shift_row.astype(jnp.float32)).astype(
        jnp.bfloat16
    )
    return (normed, inverse, hidden)


def norm_backward(grad_hidden, normed, inverse, gain_row):
    grad_normed = grad_hidden * gain_row.astype(jnp.float32)
    average_one = jnp.mean(grad_normed, axis=-1, keepdims=True)
    average_two = jnp.mean(grad_normed * normed, axis=-1, keepdims=True)
    grad_rows = inverse * (grad_normed - average_one - normed * average_two)
    return (grad_rows, jnp.sum(grad_hidden * normed, axis=0), jnp.sum(grad_hidden, axis=0))


def gelu_slope(values):
    return (
        0.5 * (1.0 + lax.erf(values * 0.7071067811865476))
        + values * jnp.exp(-0.5 * values * values) * 0.3989422804014327
    )


def attention_scores(query, keys, scaling):
    return jnp.einsum("bshe,bthe->bhst", query, keys, preferred_element_type=jnp.float32) * scaling


def forward_pass(inputs, params):
    (
        gain_one,
        shift_one,
        w_qkv,
        b_query,
        b_value,
        w_proj,
        b_proj,
        gain_two,
        shift_two,
        w_fc1,
        b_fc1,
        w_fc2,
        b_fc2,
    ) = params
    images, length, width = inputs.shape
    head_dim = width // HEADS
    scaling = head_dim ** (-0.5)
    row_count = images * length
    token_rows = inputs.reshape(row_count, width).astype(jnp.float32)
    normed_one, inverse_one, hidden_one = layer_norm(token_rows, gain_one, shift_one)
    bias_full = jnp.concatenate([b_query, jnp.zeros_like(b_query), b_value]).astype(jnp.float32)
    packed = (product(hidden_one, w_qkv) + bias_full).astype(jnp.bfloat16)
    packed = packed.reshape(images, length, 3, HEADS, head_dim)
    query = packed[:, :, 0]
    keys = packed[:, :, 1]
    values = packed[:, :, 2]
    scores = attention_scores(query, keys, scaling)
    log_total = jax.nn.logsumexp(scores, axis=-1, keepdims=True)
    probs_b = jnp.exp(scores - log_total).astype(jnp.bfloat16)
    attended = jnp.einsum("bhst,bthe->bshe", probs_b, values, preferred_element_type=jnp.float32)
    attended = attended.astype(jnp.bfloat16).reshape(row_count, width)
    resid = token_rows + product(attended, w_proj) + b_proj.astype(jnp.float32)
    normed_two, inverse_two, hidden_two = layer_norm(resid, gain_two, shift_two)
    pre_act = product(hidden_two, w_fc1) + b_fc1.astype(jnp.float32)
    act_b = jax.nn.gelu(pre_act, approximate=False).astype(jnp.bfloat16)
    outputs = (resid + product(act_b, w_fc2) + b_fc2.astype(jnp.float32)).astype(jnp.bfloat16)
    saved = (
        normed_one,
        inverse_one,
        hidden_one,
        query,
        keys,
        values,
        log_total,
        attended,
        normed_two,
        inverse_two,
        hidden_two,
        pre_act,
        act_b,
    )
    return (outputs.reshape(images, length, width), saved)


def backward_pass(cotangent, saved, params):
    (
        gain_one,
        shift_one,
        w_qkv,
        b_query,
        b_value,
        w_proj,
        b_proj,
        gain_two,
        shift_two,
        w_fc1,
        b_fc1,
        w_fc2,
        b_fc2,
    ) = params
    (
        normed_one,
        inverse_one,
        hidden_one,
        query,
        keys,
        values,
        log_total,
        attended,
        normed_two,
        inverse_two,
        hidden_two,
        pre_act,
        act_b,
    ) = saved
    images, length, width = cotangent.shape
    head_dim = width // HEADS
    scaling = head_dim ** (-0.5)
    row_count = images * length
    grad_out = cotangent.reshape(row_count, width)
    grad_top = grad_out.astype(jnp.float32)
    grad_b_fc2 = jnp.sum(grad_top, axis=0)
    grad_w_fc2 = product_left_t(act_b, grad_out)
    grad_pre = product_right_t(grad_out, w_fc2) * gelu_slope(pre_act)
    grad_b_fc1 = jnp.sum(grad_pre, axis=0)
    grad_pre_b = grad_pre.astype(jnp.bfloat16)
    grad_w_fc1 = product_left_t(hidden_two, grad_pre_b)
    grad_hidden_two = product_right_t(grad_pre_b, w_fc1)
    grad_part, grad_gain_two, grad_shift_two = norm_backward(
        grad_hidden_two, normed_two, inverse_two, gain_two
    )
    grad_resid = grad_top + grad_part
    grad_b_proj = jnp.sum(grad_resid, axis=0)
    grad_resid_b = grad_resid.astype(jnp.bfloat16)
    grad_w_proj = product_left_t(attended, grad_resid_b)
    grad_attended = product_right_t(grad_resid_b, w_proj).astype(jnp.bfloat16)
    grad_attended = grad_attended.reshape(images, length, HEADS, head_dim)
    probs = jnp.exp(attention_scores(query, keys, scaling) - log_total)
    probs_b = probs.astype(jnp.bfloat16)
    grad_values = jnp.einsum(
        "bhst,bshe->bthe", probs_b, grad_attended, preferred_element_type=jnp.float32
    )
    grad_probs = jnp.einsum(
        "bshe,bthe->bhst", grad_attended, values, preferred_element_type=jnp.float32
    )
    delta_rows = jnp.sum(probs * grad_probs, axis=-1, keepdims=True)
    grad_scores = (probs * (grad_probs - delta_rows) * scaling).astype(jnp.bfloat16)
    grad_query = jnp.einsum(
        "bhst,bthe->bshe", grad_scores, keys, preferred_element_type=jnp.float32
    )
    grad_keys = jnp.einsum(
        "bhst,bshe->bthe", grad_scores, query, preferred_element_type=jnp.float32
    )
    grad_b_query = jnp.sum(grad_query.reshape(row_count, width), axis=0)
    grad_b_value = jnp.sum(grad_values.reshape(row_count, width), axis=0)
    grad_packed_b = (
        jnp.stack([grad_query, grad_keys, grad_values], axis=2)
        .reshape(row_count, 3 * width)
        .astype(jnp.bfloat16)
    )
    grad_w_qkv = product_left_t(hidden_one, grad_packed_b)
    grad_hidden_one = product_right_t(grad_packed_b, w_qkv)
    grad_first, grad_gain_one, grad_shift_one = norm_backward(
        grad_hidden_one, normed_one, inverse_one, gain_one
    )
    grad_inputs = (grad_resid + grad_first).reshape(images, length, width)
    grads = (
        grad_gain_one,
        grad_shift_one,
        grad_w_qkv,
        grad_b_query,
        grad_b_value,
        grad_w_proj,
        grad_b_proj,
        grad_gain_two,
        grad_shift_two,
        grad_w_fc1,
        grad_b_fc1,
        grad_w_fc2,
        grad_b_fc2,
    )
    return (grad_inputs, grads)


def owned_rows(whole, position, members):
    share = whole.shape[0] // members
    return lax.dynamic_slice_in_dim(whole, position * share, share, 0)


def local(
    inputs,
    cotangent,
    gain_one,
    shift_one,
    w_qkv,
    b_query,
    b_value,
    w_proj,
    b_proj,
    gain_two,
    shift_two,
    w_fc1,
    b_fc1,
    w_fc2,
    b_fc2,
):
    gathered = (
        lax.all_gather(gain_one, "group", axis=0, tiled=True),
        lax.all_gather(shift_one, "group", axis=0, tiled=True),
        lax.all_gather(w_qkv, "group", axis=0, tiled=True),
        lax.all_gather(b_query, "group", axis=0, tiled=True),
        lax.all_gather(b_value, "group", axis=0, tiled=True),
        lax.all_gather(w_proj, "group", axis=0, tiled=True),
        lax.all_gather(b_proj, "group", axis=0, tiled=True),
        lax.all_gather(gain_two, "group", axis=0, tiled=True),
        lax.all_gather(shift_two, "group", axis=0, tiled=True),
        lax.all_gather(w_fc1, "group", axis=0, tiled=True),
        lax.all_gather(b_fc1, "group", axis=0, tiled=True),
        lax.all_gather(w_fc2, "group", axis=0, tiled=True),
        lax.all_gather(b_fc2, "group", axis=0, tiled=True),
    )
    outputs, saved = forward_pass(inputs, gathered)
    params_back = (
        lax.all_gather(gain_one, "group", axis=0, tiled=True),
        lax.all_gather(shift_one, "group", axis=0, tiled=True),
        lax.all_gather(w_qkv, "group", axis=0, tiled=True),
        lax.all_gather(b_query, "group", axis=0, tiled=True),
        lax.all_gather(b_value, "group", axis=0, tiled=True),
        lax.all_gather(w_proj, "group", axis=0, tiled=True),
        lax.all_gather(b_proj, "group", axis=0, tiled=True),
        lax.all_gather(gain_two, "group", axis=0, tiled=True),
        lax.all_gather(shift_two, "group", axis=0, tiled=True),
        lax.all_gather(w_fc1, "group", axis=0, tiled=True),
        lax.all_gather(b_fc1, "group", axis=0, tiled=True),
        lax.all_gather(w_fc2, "group", axis=0, tiled=True),
        lax.all_gather(b_fc2, "group", axis=0, tiled=True),
    )
    grad_inputs, grads = backward_pass(cotangent, saved, params_back)
    (
        term_gain_one,
        term_shift_one,
        term_w_qkv,
        term_b_query,
        term_b_value,
        term_w_proj,
        term_b_proj,
        term_gain_two,
        term_shift_two,
        term_w_fc1,
        term_b_fc1,
        term_w_fc2,
        term_b_fc2,
    ) = grads
    wholes = lax.psum(
        (
            term_gain_one,
            term_shift_one,
            term_w_qkv,
            term_b_query,
            term_b_value,
            term_w_proj,
            term_b_proj,
            term_gain_two,
            term_shift_two,
            term_w_fc1,
            term_b_fc1,
            term_w_fc2,
            term_b_fc2,
        ),
        ("replica", "group"),
    )
    position = lax.axis_index("group")
    members = lax.axis_size("group")
    totals = tuple((owned_rows(whole, position, members) for whole in wholes))
    token_total = (
        inputs.shape[0] * inputs.shape[1] * lax.axis_size("replica") * lax.axis_size("group")
    )
    factor = float(token_total) ** (-0.5)
    return (outputs, grad_inputs) + tuple((total * factor for total in totals))


def solution(mesh):
    return jax.shard_map(
        local,
        mesh=mesh,
        in_specs=(
            P(("replica", "group"), None, None),
            P(("replica", "group"), None, None),
            P("group"),
            P("group"),
            P("group", None),
            P("group"),
            P("group"),
            P("group", None),
            P("group"),
            P("group"),
            P("group"),
            P("group", None),
            P("group"),
            P("group", None),
            P("group"),
        ),
        out_specs=(
            P(("replica", "group"), None, None),
            P(("replica", "group"), None, None),
            P("group"),
            P("group"),
            P("group", None),
            P("group"),
            P("group"),
            P("group", None),
            P("group"),
            P("group"),
            P("group"),
            P("group", None),
            P("group"),
            P("group", None),
            P("group"),
        ),
        check_vma=False,
    )
```

profile of v0, /device:TPU:0, one launch (start us, length us, event | category | flops | bytes accessed | tf_op | source)
XLA Modules:
  0.0 717.0 jit_solution(14712015260770157017)
XLA Ops:
  41.6 6.7 all-reduce.10
  53.7 15.1 %all_gather.47 = bf16[384,1152]{1,0:T(8,128)(2,1)S(1)} all-gather(bf16[192,1152]{1,0:T(8,128)(2,1)S(1)} %copy-done.18), channel_id=1, replica_groups=mesh['replica'=16,'group'=2] {'group'}, dimensions={0}, use_global_device_ids=true | all-gather | bytes 1327104 | tf_op jit(solution)/shard_map/all_gather | solution.py:239
  72.2 8.7 %fusion.17 = bf16[3940,1152]{1,0:T(8,128)(2,1)} fusion(bf16[384,1152]{1,0:T(8,128)(2,1)S(1)} %all_gather.47, f32[1152]{0:T(1024)S(1)} %maximum_convert_fusion.1, f32[3940,384]{1,0:T(8,128)S(1)} %copy-done.1, f32[384]{0:T(512)S(1)} %copy-done.27, f32[384]{0:T(512)S(1)} %copy-done.25, f32[3940]{0:T(1024)S(1)} %copy-done.23, f32[3940]{0:T(1024)S(1)} %div.27), kind=kOutput, calls=%fused_computation.34 | convolution fusion | flops 3502502400 | bytes 16053536 | tf_op jit(solution)/shard_map/dot_general | solution.py:13
  80.9 27.6 %reshape.236 = bf16[20,197,3,6,64]{4,3,2,1,0:T(8,128)(2,1)} reshape(bf16[3940,1152]{1,0:T(8,128)(2,1)} %fusion.17) | data formatting | bytes 18155520 | tf_op jit(solution)/shard_map/reshape | solution.py:82
  108.5 16.3 %fusion.67 = (bf16[20,197,1,6,64]{4,3,2,1,0:T(8,128)(2,1)}, bf16[20,197,1,6,64]{4,3,2,1,0:T(8,128)(2,1)}, bf16[20,197,1,6,64]{4,3,2,1,0:T(8,128)(2,1)}) fusion(bf16[20,197,3,6,64]{4,3,2,1,0:T(8,128)(2,1)} %reshape.236), kind=kLoop, calls=%fused_computation.116 | loop fusion | bytes 18155520 | tf_op jit(solution)/shard_map/slice | solution.py:83
  124.8 9.7 %copy.74 = bf16[20,197,1,6,64]{1,4,3,0,2:T(8,128)(2,1)} copy(bf16[20,197,1,6,64]{4,3,2,1,0:T(8,128)(2,1)} %get-tuple-element.46) | data formatting | bytes 6051840
  134.5 9.7 %copy.75 = bf16[20,197,1,6,64]{1,4,3,0,2:T(8,128)(2,1)} copy(bf16[20,197,1,6,64]{4,3,2,1,0:T(8,128)(2,1)} %get-tuple-element.48) | data formatting | bytes 6051840
  144.2 14.9 %multiply_reduce_fusion.1 = (f32[20,6,197]{2,1,0:T(8,128)S(1)}, f32[20,6,197,197]{2,3,1,0:T(8,128)}) fusion(bf16[20,197,1,6,64]{1,4,3,0,2:T(8,128)(2,1)} %copy.75, bf16[20,197,1,6,64]{1,4,3,0,2:T(8,128)(2,1)} %copy.74), kind=kOutput, calls=%fused_computation.32 | convolution fusion | flops 605396736 | bytes 24774720 | tf_op jit(solution)/shard_map/bshe,bthe->bhst/dot_general | solution.py:55
  159.2 10.6 %exponential_reduce_fusion = f32[20,6,197]{2,1,0:T(8,128)S(1)} fusion(f32[20,6,197,197]{2,3,1,0:T(8,128)} %get-tuple-element.50, f32[20,6,197]{2,1,0:T(8,128)S(1)} %is-finite_select_fusion), kind=kLoop, calls=%fused_computation.7 | loop fusion | flops 13947600 | bytes 18817440 | tf_op jit(solution)/shard_map/reduce_sum | solution.py:87
  169.8 9.9 %copy.73 = bf16[20,197,1,6,64]{1,4,3,0,2:T(8,128)(2,1)} copy(bf16[20,197,1,6,64]{4,3,2,1,0:T(8,128)(2,1)} %get-tuple-element.47) | data formatting | bytes 6051840
  179.8 15.8 %convert_bitcast_fusion = bf16[20,197,6,64]{1,3,2,0:T(8,128)(2,1)} fusion(bf16[20,197,1,6,64]{1,4,3,0,2:T(8,128)(2,1)} %copy.73, f32[20,6,197]{2,1,0:T(8,128)S(1)} %log_add_fusion, f32[20,6,197,197]{2,3,1,0:T(8,128)} %get-tuple-element.50), kind=kOutput, calls=%fused_computation.73 | convolution fusion | flops 611590464 | bytes 24774720 | tf_op jit(solution)/shard_map/bhst,bthe->bshe/dot_general | solution.py:89
  195.6 6.8 copy.57
  202.4 6.6 reshape.187
  232.4 62.4 %fusion.4 = (bf16[3940,1536]{1,0:T(8,128)(2,1)}, f32[3940,1536]{1,0:T(8,128)}) fusion(f32[1536]{0:T(1024)S(1)} %reshape.219, bf16[384,1536]{1,0:T(8,128)(2,1)} %all-gather.4.cloned.1.call-done, f32[3940,384]{1,0:T(8,128)} %copy-done.2, f32[384]{0:T(512)S(1)} %convert_element_type.115, f32[384]{0:T(512)S(1)} %convert_element_type.114, ...), kind=kOutput, calls=%fused_computation.10 | convolution fusion | flops 5054799360 | bytes 43583264 | tf_op jit(solution)/shard_map/dot_general | solution.py:13
  294.8 20.8 %fusion.71 = (f32[1536]{0:T(1024)}, bf16[3940,1536]{1,0:T(8,128)(2,1)}) fusion(f32[3940,1536]{1,0:T(8,128)} %get-tuple-element.54, f32[1536]{0:T(1024)S(1)} %reshape.219, bf16[3940,384]{1,0:T(8,128)(2,1)S(1)} %copy-done.8, bf16[1536,384]{1,0:T(8,128)(2,1)} %all-gather.6.cloned.1.call-done), kind=kOutput, calls=%fused_computation.118 | convolution fusion | flops 4720433664 | bytes 40528896 | tf_op jit(solution)/shard_map/dot_general | solution.py:23
  315.5 11.3 %fusion.27 = f32[384,1536]{1,0:T(8,128)} fusion(bf16[3940,1536]{1,0:T(8,128)(2,1)} %get-tuple-element.62, f32[3940,384]{1,0:T(8,128)S(1)} %copy-done.3, f32[384]{0:T(512)S(1)} %convert_element_type.115, f32[384]{0:T(512)S(1)} %convert_element_type.114, f32[3940]{0:T(1024)S(1)} %add_rsqrt_fusion.1, f32[3940]{0:T(1024)S(1)} %broadcast_multiply_fusion.5), kind=kOutput, calls=%fused_computation.49 | convolution fusion | flops 4655377920 | bytes 20549408 | tf_op jit(solution)/shard_map/dot_general | solution.py:17
  326.9 10.6 %multiply_reduce_fusion.3 = (f32[384]{0:T(512)S(1)}, f32[3940]{0:T(1024)S(1)}, f32[3940]{0:T(1024)S(1)}, f32[384]{0:T(512)S(1)}, f32[3940,384]{1,0:T(8,128)S(1)}) fusion(f32[3940,384]{1,0:T(8,128)S(1)} %copy-done.3, f32[3940]{0:T(1024)S(1)} %add_rsqrt_fusion.1, f32[3940]{0:T(1024)S(1)} %broadcast_multiply_fusion.5, f32[384]{0:T(512)S(1)} %convert_element_type.114, ...), kind=kOutput, calls=%fused_computation.43 | convolution fusion | flops 4661420544 | bytes 25454656 | tf_op jit(solution)/shard_map/dot_general | solution.py:23
  346.5 7.4 %reshape.237 = bf16[20,197,6,64]{3,2,1,0:T(8,128)(2,1)} reshape(bf16[3940,384]{1,0:T(8,128)(2,1)S(1)} %convolution_convert_fusion) | data formatting | bytes 6051840 | tf_op jit(solution)/shard_map/reshape | solution.py:166
  353.9 9.9 %copy.59 = bf16[20,197,6,64]{1,3,2,0:T(8,128)(2,1)} copy(bf16[20,197,6,64]{3,2,1,0:T(8,128)(2,1)} %reshape.237) | data formatting | bytes 6051840 | tf_op jit(solution)/shard_map/reshape | solution.py:166
  363.8 14.9 %fusion.36 = f32[20,6,197,197]{2,3,1,0:T(8,128)} fusion(bf16[20,197,6,64]{1,3,2,0:T(8,128)(2,1)} %copy.59, bf16[20,197,1,6,64]{1,4,3,0,2:T(8,128)(2,1)} %copy.73), kind=kOutput, calls=%fused_computation.69 | convolution fusion | flops 596106240 | bytes 24680160 | tf_op jit(solution)/shard_map/bshe,bthe->bhst/dot_general | solution.py:172
  378.8 36.2 %bitcast_reduce_fusion.1 = (f32[6,64]{1,0:T(8,128)S(1)}, bf16[20,6,64,197]{3,2,1,0:T(8,128)(2,1)}) fusion(f32[20,6,197,197]{2,3,1,0:T(8,128)} %fusion.36, f32[20,6,197]{2,1,0:T(8,128)S(1)} %copy-done.15, f32[20,6,197,197]{2,3,1,0:T(8,128)} %get-tuple-element.50, bf16[20,197,1,6,64]{1,4,3,0,2:T(8,128)(2,1)} %copy.75), kind=kOutput, calls=%fused_computation.39 | convolution fusion | flops 641069312 | bytes 43404576 | tf_op jit(solution)/shard_map/bhst,bthe->bshe/dot_general | solution.py:177
  415.0 41.0 %fusion.40 = bf16[20,197,1,6,64]{1,4,3,0,2:T(8,128)(2,1)} fusion(f32[20,6,197,197]{2,3,1,0:T(8,128)} %fusion.36, f32[20,6,197]{2,1,0:T(8,128)S(1)} %copy-done.15, f32[20,6,197,197]{2,3,1,0:T(8,128)} %get-tuple-element.50, bf16[20,197,1,6,64]{1,4,3,0,2:T(8,128)(2,1)} %copy.74), kind=kOutput, calls=%fused_computation.74 | convolution fusion | flops 638043776 | bytes 43403040 | tf_op jit(solution)/shard_map/bhst,bshe->bthe/dot_general | solution.py:180
  456.0 13.8 %bitcast_reduce_fusion = (f32[6,64]{1,0:T(8,128)S(1)}, bf16[20,6,64,197]{3,2,1,0:T(8,128)(2,1)}) fusion(bf16[20,197,6,64]{1,3,2,0:T(8,128)(2,1)} %copy.59, f32[20,6,197]{2,1,0:T(8,128)S(1)} %copy-done.15, f32[20,6,197,197]{2,3,1,0:T(8,128)} %get-tuple-element.50), kind=kOutput, calls=%fused_computation.38 | convolution fusion | flops 613103040 | bytes 24776256 | tf_op jit(solution)/shard_map/bhst,bshe->bthe/dot_general | solution.py:169
  469.8 6.9 maximum_convert_fusion
  476.8 9.9 %copy.64 = bf16[20,197,3,6,64]{1,0,4,3,2:T(8,128)(2,1)} copy(bf16[20,197,3,6,64]{1,4,3,0,2:T(8,128)(2,1)S(1)} %maximum_convert_fusion) | data formatting | bytes 18155520 | tf_op jit(solution)/shard_map/convert_element_type | solution.py:188
  486.6 20.8 %convert_element_type.127 = bf16[3940,1152]{0,1:T(8,128)(2,1)} reshape(bf16[20,197,3,6,64]{1,0,4,3,2:T(8,128)(2,1)} %copy.64) | data formatting | bytes 18155520 | tf_op jit(solution)/shard_map/convert_element_type | solution.py:188
  507.5 13.7 %multiply_reduce_fusion.4 = (f32[384]{0:T(512)S(1)}, f32[3940]{0:T(1024)S(1)}, f32[3940]{0:T(1024)S(1)}, f32[384]{0:T(512)S(1)}, f32[3940,384]{1,0:T(8,128)}) fusion(f32[3940,384]{1,0:T(8,128)} %reshape.192, f32[3940]{0:T(1024)S(1)} %copy-done.24, f32[3940]{0:T(1024)S(1)} %copy-done.22, f32[384]{0:T(512)S(1)} %copy-done.26, ...), kind=kOutput, calls=%fused_computation.44 | convolution fusion | flops 3499467776 | bytes 22133824 | tf_op jit(solution)/shard_map/dot_general | solution.py:23
  526.8 10.8 %fusion.73 = f32[1536,384]{1,0:T(8,128)} fusion(bf16[3940,1536]{1,0:T(8,128)(2,1)} %get-tuple-element.53, bf16[3940,384]{1,0:T(8,128)(2,1)S(1)} %copy-done.9), kind=kOutput, calls=%fused_computation.120 | convolution fusion | flops 4647813120 | bytes 17488896 | tf_op jit(solution)/shard_map/dot_general | solution.py:17
  537.7 11.0 %multiply_add_fusion = f32[3940,384]{1,0:T(8,128)} fusion(f32[3940,384]{1,0:T(8,128)} %copy-done, f32[3940,384]{1,0:T(8,128)} %get-tuple-element.56, f32[3940,384]{1,0:T(8,128)} %reshape.192, f32[3940]{0:T(1024)S(1)} %broadcast_multiply_fusion.1, f32[3940]{0:T(1024)S(1)} %broadcast_multiply_fusion.2, f32[384]{0:T(512)S(1)} %copy-done.26, ...), kind=kLoop, calls=%fused_computation.45 | loop fusion | flops 12103680 | bytes 24271936 | tf_op jit(solution)/shard_map/add | solution.py:195
  554.4 10.8 %add_convert_fusion.1 = bf16[3940,384]{1,0:T(8,128)(2,1)S(1)} fusion(f32[3940,384]{1,0:T(8,128)} %copy-done.2, bf16[3940,1536]{1,0:T(8,128)(2,1)} %get-tuple-element.53, bf16[1536,384]{1,0:T(8,128)(2,1)} %all-gather.6.cloned.1.call-done, f32[384]{0:T(512)S(1)} %copy-done.30), kind=kOutput, calls=%fused_computation.53 | convolution fusion | flops 4652352000 | bytes 22362624 | tf_op jit(solution)/shard_map/dot_general | solution.py:13
  567.6 39.7 %all-reduce.8 = (f32[384]{0:T(512)S(1)}, f32[384]{0:T(512)S(1)}, f32[384]{0:T(512)S(1)}, f32[384]{0:T(512)S(1)}, f32[384]{0:T(512)S(1)}, /*index=5*/f32[384]{0:T...) all-reduce(f32[384]{0:T(512)S(1)} %get-tuple-element.17, ...), channel_id=1, replica_groups=mesh['replica'=16,'group'=2] {'replica','group'}, use_global_device_ids=true, to_apply=%region_12.0 | all-reduce | flops 4608 | bytes 36864 | tf_op jit(solution)/shard_map/psum | solution.py:283
  613.0 89.3 %all-reduce.13.cloned.1.call-done = (f32[384,1152]{1,0:T(8,128)}, f32[384,384]{1,0:T(8,128)}, f32[384,1536]{1,0:T(8,128)}, f32[1536,384]{1,0:T(8,128)}) async-done(((f32[384,1152]{1,0:T(8,128)}, f32[384,384]{1,0:T(8,128)}, f32[384,1536]{1,0:T(8,128)}, f32[1536,384]{1,0:T(8,128)}), (f32[384,1152]{1,0:T(8,128)}, f32[384,384]{1,0:T(8,128)}, f32[384,1536]{1,0:T(8,128)}, ...) | async-done | bytes 7077904 | tf_op jit(solution)/shard_map/psum | solution.py:283
  (157 shorter events, 102.0 us)
Async XLA Ops:
  7.2 225.2 %all-gather.4.cloned.1.call-start = ((), (), s32[]{:S(2)}) async-start(), calls=%async_computation | async-start | bytes 1769472 | tf_op jit(solution)/shard_map/all_gather | solution.py:246
  7.9 286.8 %all-gather.6.cloned.1.call-start = ((), (), s32[]{:S(2)}) async-start(), calls=%async_computation.1 | async-start | bytes 1769472 | tf_op jit(solution)/shard_map/all_gather | solution.py:248
  8.7 693.6 %all-reduce.13.cloned.1.call-start = ((), (), s32[]{:S(2)}) async-start(), calls=%async_computation.2 | async-start | bytes 14155776 | tf_op jit(solution)/shard_map/psum | solution.py:283
  13.7 58.4 %copy-start.21 = (f32[3940]{0:T(1024)}, f32[3940]{0:T(1024)S(1)}, u32[]{:S(2)}) copy-start(f32[3940]{0:T(1024)S(1)} %div.27) | copy-start | bytes 47284
  17.1 36.6 %copy-start.18 = (bf16[192,1152]{1,0:T(8,128)(2,1)S(1)}, bf16[192,1152]{1,0:T(8,128)(2,1)}, u32[]{:S(2)}) copy-start(bf16[192,1152]{1,0:T(8,128)(2,1)} %param.19) | copy-start | bytes 1327108
  53.7 18.4 %copy-start.36 = (bf16[384]{0:T(512)(128)(2,1)S(1)}, bf16[384]{0:T(512)(128)(2,1)}, u32[]{:S(2)}) copy-start(bf16[384]{0:T(512)(128)(2,1)} %get-tuple-element.36) | copy-start | bytes 2308
  53.7 18.4 %copy-start.37 = (bf16[384]{0:T(512)(128)(2,1)S(1)}, bf16[384]{0:T(512)(128)(2,1)}, u32[]{:S(2)}) copy-start(bf16[384]{0:T(512)(128)(2,1)} %get-tuple-element.37) | copy-start | bytes 2308
  53.7 18.5 %copy-start.1 = (f32[3940,384]{1,0:T(8,128)S(1)}, f32[3940,384]{1,0:T(8,128)}, u32[]{:S(2)}) copy-start(f32[3940,384]{1,0:T(8,128)} %reshape.192) | copy-start | bytes 18155524
  53.7 18.5 %copy-start.23 = (f32[3940]{0:T(1024)S(1)}, f32[3940]{0:T(1024)}, u32[]{:S(2)}) copy-start(f32[3940]{0:T(1024)} %rsqrt.21) | copy-start | bytes 47284
  53.7 18.5 %copy-start.25 = (f32[384]{0:T(512)S(1)}, f32[384]{0:T(512)}, u32[]{:S(2)}) copy-start(f32[384]{0:T(512)} %convert_element_type.105) | copy-start | bytes 4612
  53.7 18.5 %copy-start.27 = (f32[384]{0:T(512)S(1)}, f32[384]{0:T(512)}, u32[]{:S(2)}) copy-start(f32[384]{0:T(512)} %convert_element_type.106) | copy-start | bytes 4612
  169.8 25.8 %copy-start.14 = (f32[20,6,197]{2,1,0:T(8,128)}, f32[20,6,197]{2,1,0:T(8,128)S(1)}, u32[]{:S(2)}) copy-start(f32[20,6,197]{2,1,0:T(8,128)S(1)} %log_add_fusion) | copy-start | bytes 283684
  195.6 13.4 %copy-start.35 = (bf16[384]{0:T(512)(128)(2,1)S(1)}, bf16[384]{0:T(512)(128)(2,1)}, u32[]{:S(2)}) copy-start(bf16[384]{0:T(512)(128)(2,1)} %get-tuple-element.40) | copy-start | bytes 2308
  195.6 13.4 %copy-start.19 = (bf16[192,384]{1,0:T(8,128)(2,1)S(1)}, bf16[192,384]{1,0:T(8,128)(2,1)}, u32[]{:S(2)}) copy-start(bf16[192,384]{1,0:T(8,128)(2,1)} %param.22) | copy-start | bytes 442372
  209.0 11.4 %copy-start.5 = (bf16[3940,384]{0,1:T(8,128)(2,1)}, bf16[3940,384]{0,1:T(8,128)(2,1)S(1)}, u32[]{:S(2)}) copy-start(bf16[3940,384]{0,1:T(8,128)(2,1)S(1)} %reshape.187) | copy-start | bytes 9077764
  220.5 8.9 %copy-start.7 = (bf16[20,197,384]{2,1,0:T(8,128)(2,1)S(1)}, bf16[20,197,384]{2,1,0:T(8,128)(2,1)}, u32[]{:S(2)}) copy-start(bf16[20,197,384]{2,1,0:T(8,128)(2,1)} %add_convert_fusion) | copy-start | bytes 9077764
  223.5 8.3 %copy-start.32 = (bf16[384]{0:T(512)(128)(2,1)S(1)}, bf16[384]{0:T(512)(128)(2,1)}, u32[]{:S(2)}) copy-start(bf16[384]{0:T(512)(128)(2,1)} %get-tuple-element.43) | copy-start | bytes 2308
  232.4 62.4 %copy-start.8 = (bf16[3940,384]{1,0:T(8,128)(2,1)S(1)}, bf16[3940,384]{1,0:T(8,128)(2,1)}, u32[]{:S(2)}) copy-start(bf16[3940,384]{1,0:T(8,128)(2,1)} %reshape.189) | copy-start | bytes 9077764
  294.8 20.8 %copy-start.3 = (f32[3940,384]{1,0:T(8,128)S(1)}, f32[3940,384]{1,0:T(8,128)}, u32[]{:S(2)}) copy-start(f32[3940,384]{1,0:T(8,128)} %copy-done.2) | copy-start | bytes 18155524
  315.5 11.3 %copy-start.38 = (bf16[384,1536]{1,0:T(8,128)(2,1)S(1)}, bf16[384,1536]{1,0:T(8,128)(2,1)}, u32[]{:S(2)}) copy-start(bf16[384,1536]{1,0:T(8,128)(2,1)} %all-gather.4.cloned.1.call-done) | copy-start | bytes 3538948
  363.8 14.9 %copy-start.15 = (f32[20,6,197]{2,1,0:T(8,128)S(1)}, f32[20,6,197]{2,1,0:T(8,128)}, u32[]{:S(2)}) copy-start(f32[20,6,197]{2,1,0:T(8,128)} %copy-done.14) | copy-start | bytes 283684
  486.6 20.8 %copy-start.17 = (bf16[384,1152]{1,0:T(8,128)(2,1)S(1)}, bf16[384,1152]{1,0:T(8,128)(2,1)}, u32[]{:S(2)}) copy-start(bf16[384,1152]{1,0:T(8,128)(2,1)} %copy-done.16) | copy-start | bytes 2654212
  486.6 20.8 %copy-start.22 = (f32[3940]{0:T(1024)S(1)}, f32[3940]{0:T(1024)}, u32[]{:S(2)}) copy-start(f32[3940]{0:T(1024)} %copy-done.21) | copy-start | bytes 47284
  486.6 20.8 %copy-start.24 = (f32[3940]{0:T(1024)S(1)}, f32[3940]{0:T(1024)}, u32[]{:S(2)}) copy-start(f32[3940]{0:T(1024)} %rsqrt.21) | copy-start | bytes 47284
  486.6 20.8 %copy-start.26 = (f32[384]{0:T(512)S(1)}, f32[384]{0:T(512)}, u32[]{:S(2)}) copy-start(f32[384]{0:T(512)} %convert_element_type.105) | copy-start | bytes 4612
  507.5 13.7 %copy-start.10 = (bf16[3940,1152]{0,1:T(8,128)(2,1)S(1)}, bf16[3940,1152]{0,1:T(8,128)(2,1)}, u32[]{:S(2)}) copy-start(bf16[3940,1152]{0,1:T(8,128)(2,1)} %convert_element_type.127) | copy-start | bytes 27233284
  507.5 13.7 %copy-start.11 = (bf16[3940,384]{1,0:T(8,128)(2,1)S(1)}, bf16[3940,384]{1,0:T(8,128)(2,1)}, u32[]{:S(2)}) copy-start(bf16[3940,384]{1,0:T(8,128)(2,1)} %convert_element_type.129) | copy-start | bytes 9077764
  521.2 5.6 copy-start.9
  548.7 5.7 copy-start.30
  554.4 13.2 %copy-start.28 = (f32[1536]{0:T(1024)S(1)}, f32[1536]{0:T(1024)}, u32[]{:S(2)}) copy-start(f32[1536]{0:T(1024)} %get-tuple-element.61) | copy-start | bytes 18436
  554.4 13.2 %copy-start.29 = (f32[384]{0:T(512)S(1)}, f32[384]{0:T(512)}, u32[]{:S(2)}) copy-start(f32[384]{0:T(512)} %convert_reduce_fusion) | copy-start | bytes 4612
  702.3 7.0 copy-start.20
  (10 other events, 38.8 us)
Sparse Core Ops, SparseCore 0:
  9.5 25.4 all-gather.3
  36.6 24.6 all-gather.5
  537.8 164.4 all-reduce.12
where the time goes:
time: 724 us; the launch traced here: 717 us
  matrix products  302 us (42%)
  local copies, waits for them, and re-layouts  174 us (24%)
  waiting for transfers between devices  90.7 us (13%)
  blocking collectives  71.8 us (10%)
  other arithmetic  62.9 us (9%)
  between operations  15.4 us (2%)
    psum x1, waiting for transfers between devices, local(): lax.psum((term_gain_one, term_shift_one, term_w_qkv, term_b_query, term_b...  89.3 us
    dot_general x4, matrix products, product(): return jnp.dot(left, right, preferred_element_type=jnp.float32)  87.2 us
    unnamed x100, local copies, waits for them, and re-layouts  49 us
    dot_general x4, matrix products, product_right_t(): lax.dot_general(left, right, (((1,), (1,)), ((), ())), preferred_element_...  47.4 us
    dot_general x1, matrix products, backward_pass(): jnp.einsum('bhst,bshe->bthe', grad_scores, query, preferred_element_type=...  41 us
    psum x1, blocking collectives, local(): lax.psum((term_gain_one, term_shift_one, term_w_qkv, term_b_query, term_b...  39.7 us
    dot_general x1, matrix products, backward_pass(): jnp.einsum('bhst,bthe->bshe', grad_scores, keys, preferred_element_type=j...  36.2 us
    convert_element_type x2, local copies, waits for them, and re-layouts, backward_pass(): grad_packed_b = jnp.stack([grad_query, grad_keys, grad_values], axis=2).r...  30.7 us
  transfers between devices with their start and end apart: 3, of which 1 were waited for; matrix products, arithmetic and copies ran while one was open for 40% of the time, Pallas kernels for 0%

commit v1 on v0

v1 whole, which is shorter than its diff:
```python
import functools

import jax
import jax.numpy as jnp
from jax import lax
from jax.experimental import pallas as pl
from jax.experimental.pallas import tpu as pltpu
from jax.sharding import PartitionSpec as P

HEADS = 6
EPS = 1e-06
BF = jnp.bfloat16
F32 = jnp.float32
LOG2E = 1.4426950408889634
VMEM_LIMIT = 60 * 1024 * 1024


def dot(left, right):
    return jnp.dot(left, right, preferred_element_type=F32)


def dot_lt(left, right):
    return lax.dot_general(left, right, (((0,), (0,)), ((), ())), preferred_element_type=F32)


def dot_rt(left, right):
    return lax.dot_general(left, right, (((1,), (1,)), ((), ())), preferred_element_type=F32)


def row_stats(rows):
    centre = jnp.mean(rows, axis=-1, keepdims=True)
    centered = rows - centre
    inverse = lax.rsqrt(jnp.mean(centered * centered, axis=-1, keepdims=True) + EPS)
    return centered * inverse, inverse


def norm_back(grad_hidden, normed, inverse, gain):
    grad_normed = grad_hidden * gain
    one = jnp.mean(grad_normed, axis=-1, keepdims=True)
    two = jnp.mean(grad_normed * normed, axis=-1, keepdims=True)
    return inverse * (grad_normed - one - normed * two)


def col_sum(rows):
    return jnp.sum(rows, axis=0, keepdims=True)


def attention_forward(length, pitch, count, x_ref, w_ref, vec_ref, bias_ref, packed_ref, probs_ref, att_ref, pad_ref):
    width = x_ref.shape[2]
    head_dim = width // HEADS
    pair = 2 * head_dim
    factor = head_dim ** (-0.5) * LOG2E

    @pl.when(pl.program_id(0) == 0)
    def _():
        pad_ref[...] = jnp.zeros_like(pad_ref)

    gain = vec_ref[0:1, :].astype(F32)
    shift = vec_ref[1:2, :].astype(F32)
    for image in range(count):
        pad_ref[image * pitch : image * pitch + length, :] = x_ref[image]
    normed, _ = row_stats(pad_ref[...].astype(F32))
    hidden = (normed * gain + shift).astype(BF)
    packed = (dot(hidden, w_ref[...]) + bias_ref[...].astype(F32)).astype(BF)
    for image in range(count):
        packed_ref[image] = packed[image * pitch : (image + 1) * pitch]
    lane = lax.broadcasted_iota(jnp.int32, (pitch, pair), 1)
    tail = length // 8 * 8
    row = lax.broadcasted_iota(jnp.int32, (pitch - tail, pitch), 0) + tail
    for image in range(count):
        for two in range(HEADS // 2):
            cols = slice(two * pair, (two + 1) * pair)
            query = packed_ref[image, :, two * pair : (two + 1) * pair]
            keys = packed_ref[image, :, width + two * pair : width + (two + 1) * pair]
            values = packed_ref[image, :, 2 * width + two * pair : 2 * width + (two + 1) * pair]
            values_t = values.T
            parts = []
            for side in range(2):
                own = (lane < head_dim) if side == 0 else (lane >= head_dim)
                scores = dot_rt(keys, jnp.where(own, query, jnp.zeros_like(query)))
                low = jnp.where(row < length, scores[tail:], -1e30)
                scores = jnp.concatenate([scores[:tail], low], axis=0)
                top = jnp.max(scores, axis=0, keepdims=True)
                raised = jnp.exp2((scores - top) * factor)
                total = jnp.sum(raised, axis=0, keepdims=True)
                probs = (raised * (1.0 / total)).astype(BF)
                probs_ref[image, 2 * two + side] = probs
                parts.append(dot(values_t[side * head_dim : (side + 1) * head_dim], probs))
            mixed = jnp.concatenate(parts, axis=0)
            att_ref[image, :, cols] = mixed.T.astype(BF)


def gelu_parts(values):
    half = 0.5 * (1.0 + lax.erf(values * 0.7071067811865476))
    slope = half + values * jnp.exp(-0.5 * values * values) * 0.3989422804014327
    return half, slope


def mlp_both(
    length, pitch, count, chunk,
    x_ref, ct_ref, att_ref, wp_ref, w1_ref, w2_ref, vec_ref, b1_ref,
    y_ref, gr_ref, dw1_ref, dw2t_ref, dwp_ref, dvec_ref, db1_ref,
    xpad, ctpad, act_ref, gp_ref, acc1, acc2, accp, accv, accb,
):
    step = pl.program_id(0)
    hidden_units = w1_ref.shape[1]

    @pl.when(step == 0)
    def _():
        for ref in (xpad, ctpad, acc1, acc2, accp, accv, accb):
            ref[...] = jnp.zeros_like(ref)

    for image in range(count):
        xpad[image * pitch : image * pitch + length, :] = x_ref[image]
        ctpad[image * pitch : image * pitch + length, :] = ct_ref[image]
    bias_p = vec_ref[4:5, :].astype(F32)
    gain = vec_ref[5:6, :].astype(F32)
    shift = vec_ref[6:7, :].astype(F32)
    bias_2 = vec_ref[7:8, :].astype(F32)
    ct = ctpad[...]
    att = att_ref[...].reshape(count * pitch, att_ref.shape[2])
    resid = xpad[...].astype(F32) + dot(att, wp_ref[...]) + bias_p
    normed, inverse = row_stats(resid)
    hidden = (normed * gain + shift).astype(BF)
    for start in range(0, hidden_units, chunk):
        cols = slice(start, start + chunk)
        pre = dot(hidden, w1_ref[:, cols]) + b1_ref[:, cols].astype(F32)
        half, slope = gelu_parts(pre)
        act_ref[:, cols] = (pre * half).astype(BF)
        grad_pre = dot_rt(ct, w2_ref[cols, :]) * slope
        accb[:, cols] += col_sum(grad_pre)
        gp_ref[:, cols] = grad_pre.astype(BF)
    out = resid + dot(act_ref[...], w2_ref[...]) + bias_2
    for image in range(count):
        y_ref[image] = out[image * pitch : image * pitch + length].astype(BF)
    grad_hidden = dot_rt(gp_ref[...], w1_ref[...])
    top = ct.astype(F32)
    grad_resid = top + norm_back(grad_hidden, normed, inverse, gain)
    accv[0:1, :] += col_sum(grad_resid)
    accv[1:2, :] += col_sum(grad_hidden * normed)
    accv[2:3, :] += col_sum(grad_hidden)
    accv[3:4, :] += col_sum(top)
    gr_ref[...] = grad_resid.reshape(gr_ref.shape)
    acc1[...] += dot_lt(hidden, gp_ref[...])
    acc2[...] += dot_lt(ct, act_ref[...])
    accp[...] += dot_lt(att, grad_resid.astype(BF))

    @pl.when(step == pl.num_programs(0) - 1)
    def _():
        dw1_ref[...] = acc1[...].astype(BF)
        dw2t_ref[...] = acc2[...].astype(BF)
        dwp_ref[...] = accp[...].astype(BF)
        dvec_ref[...] = accv[...]
        db1_ref[...] = accb[...]


def attention_backward(
    length, pitch, count,
    x_ref, gr_ref, packed_ref, probs_ref, wp_ref, w_ref, vec_ref,
    gx_ref, dw_ref, dvec_ref,
    pad_ref, gp_ref, acc, accv,
):
    step = pl.program_id(0)
    width = x_ref.shape[2]
    head_dim = width // HEADS
    pair = 2 * head_dim
    factor = head_dim ** (-0.5)

    @pl.when(step == 0)
    def _():
        for ref in (pad_ref, acc, accv):
            ref[...] = jnp.zeros_like(ref)

    gain = vec_ref[0:1, :].astype(F32)
    shift = vec_ref[1:2, :].astype(F32)
    for image in range(count):
        pad_ref[image * pitch : image * pitch + length, :] = x_ref[image]
    grad_resid = gr_ref[...].reshape(count * pitch, width)
    grad_att = dot_rt(grad_resid.astype(BF), wp_ref[...]).astype(BF)
    lane = lax.broadcasted_iota(jnp.int32, (pitch, pair), 1)
    for image in range(count):
        rows = slice(image * pitch, (image + 1) * pitch)
        for two in range(HEADS // 2):
            cols = slice(two * pair, (two + 1) * pair)
            query = packed_ref[image, :, two * pair : (two + 1) * pair]
            keys = packed_ref[image, :, width + two * pair : width + (two + 1) * pair]
            values = packed_ref[image, :, 2 * width + two * pair : 2 * width + (two + 1) * pair]
            grad_out = grad_att[rows, cols]
            keys_t = keys.T
            grad_values = None
            grad_keys = None
            parts = []
            for side in range(2):
                own = (lane < head_dim) if side == 0 else (lane >= head_dim)
                zero = jnp.zeros_like(query)
                grad_side = jnp.where(own, grad_out, zero)
                probs_b = probs_ref[image, 2 * two + side]
                probs = probs_b.astype(F32)
                grad_probs = dot_rt(values, grad_side)
                delta = jnp.sum(probs * grad_probs, axis=0, keepdims=True)
                grad_scores = (probs * (grad_probs - delta)).astype(BF)
                piece_v = dot(probs_b, grad_side)
                piece_k = dot(grad_scores, jnp.where(own, query, zero))
                grad_values = piece_v if grad_values is None else grad_values + piece_v
                grad_keys = piece_k if grad_keys is None else grad_keys + piece_k
                parts.append(dot(keys_t[side * head_dim : (side + 1) * head_dim], grad_scores))
            grad_query = jnp.concatenate(parts, axis=0).T * factor
            grad_keys = grad_keys * factor
            accv[0:1, cols] += col_sum(grad_query)
            accv[1:2, cols] += col_sum(grad_values)
            gp_ref[rows, two * pair : (two + 1) * pair] = grad_query.astype(BF)
            gp_ref[rows, width + two * pair : width + (two + 1) * pair] = grad_keys.astype(BF)
            gp_ref[rows, 2 * width + two * pair : 2 * width + (two + 1) * pair] = grad_values.astype(BF)
    normed, inverse = row_stats(pad_ref[...].astype(F32))
    hidden = (normed * gain + shift).astype(BF)
    acc[...] += dot_lt(hidden, gp_ref[...])
    grad_hidden = dot_rt(gp_ref[...], w_ref[...])
    accv[2:3, :] += col_sum(grad_hidden * normed)
    accv[3:4, :] += col_sum(grad_hidden)
    grad_x = grad_resid + norm_back(grad_hidden, normed, inverse, gain)
    for image in range(count):
        gx_ref[image] = grad_x[image * pitch : image * pitch + length]

    @pl.when(step == pl.num_programs(0) - 1)
    def _():
        dw_ref[...] = acc[...].astype(BF)
        dvec_ref[...] = accv[...]


def whole(array):
    return pl.BlockSpec(array.shape, lambda i: (0,) * len(array.shape))


def blocks(count, *rest):
    return pl.BlockSpec((count,) + rest, lambda i: (i,) + (0,) * len(rest))


def fixed(*shape):
    return pl.BlockSpec(shape, lambda i: (0,) * len(shape))


def compute(inputs, cotangent, w_qkv, w_proj, w_fc1, w_fc2, vecs, bias_qkv, bias_fc1):
    images, length, width = inputs.shape
    hidden_units = w_fc1.shape[1]
    pitch = (length + 15) // 16 * 16
    sds = jax.ShapeDtypeStruct
    params = pltpu.CompilerParams(vmem_limit_bytes=VMEM_LIMIT, dimension_semantics=("arbitrary",))

    count = 2
    packed, probs, attended = pl.pallas_call(
        functools.partial(attention_forward, length, pitch, count),
        grid=(images // count,),
        in_specs=[blocks(count, length, width), whole(w_qkv), whole(vecs), whole(bias_qkv)],
        out_specs=[
            blocks(count, pitch, 3 * width),
            blocks(count, HEADS, pitch, pitch),
            blocks(count, pitch, width),
        ],
        out_shape=[
            sds((images, pitch, 3 * width), BF),
            sds((images, HEADS, pitch, pitch), BF),
            sds((images, pitch, width), BF),
        ],
        scratch_shapes=[pltpu.VMEM((count * pitch, width), BF)],
        compiler_params=params,
        name="attention_forward",
    )(inputs, w_qkv, vecs, bias_qkv)

    count = 2
    rows = count * pitch
    outputs, grad_resid, d_fc1, d_fc2t, d_proj, d_vec, d_b1 = pl.pallas_call(
        functools.partial(mlp_both, length, pitch, count, 256),
        grid=(images // count,),
        in_specs=[
            blocks(count, length, width),
            blocks(count, length, width),
            blocks(count, pitch, width),
            whole(w_proj), whole(w_fc1), whole(w_fc2), whole(vecs), whole(bias_fc1),
        ],
        out_specs=[
            blocks(count, length, width),
            blocks(count, pitch, width),
            fixed(width, hidden_units), fixed(width, hidden_units), fixed(width, width),
            fixed(8, width), fixed(1, hidden_units),
        ],
        out_shape=[
            sds((images, length, width), BF),
            sds((images, pitch, width), F32),
            sds((width, hidden_units), BF), sds((width, hidden_units), BF), sds((width, width), BF),
            sds((8, width), F32), sds((1, hidden_units), F32),
        ],
        scratch_shapes=[
            pltpu.VMEM((rows, width), BF), pltpu.VMEM((rows, width), BF),
            pltpu.VMEM((rows, hidden_units), BF), pltpu.VMEM((rows, hidden_units), BF),
            pltpu.VMEM((width, hidden_units), F32), pltpu.VMEM((width, hidden_units), F32),
            pltpu.VMEM((width, width), F32), pltpu.VMEM((8, width), F32), pltpu.VMEM((1, hidden_units), F32),
        ],
        compiler_params=params,
        name="mlp_both",
    )(inputs, cotangent, attended, w_proj, w_fc1, w_fc2, vecs, bias_fc1)

    count = 2
    rows = count * pitch
    grad_inputs, d_qkv, d_vec2 = pl.pallas_call(
        functools.partial(attention_backward, length, pitch, count),
        grid=(images // count,),
        in_specs=[
            blocks(count, length, width),
            blocks(count, pitch, width),
            blocks(count, pitch, 3 * width),
            blocks(count, HEADS, pitch, pitch),
            whole(w_proj), whole(w_qkv), whole(vecs),
        ],
        out_specs=[blocks(count, length, width), fixed(width, 3 * width), fixed(8, width)],
        out_shape=[
            sds((images, length, width), F32),
            sds((width, 3 * width), BF),
            sds((8, width), F32),
        ],
        scratch_shapes=[
            pltpu.VMEM((rows, width), BF), pltpu.VMEM((rows, 3 * width), BF),
            pltpu.VMEM((width, 3 * width), F32), pltpu.VMEM((8, width), F32),
        ],
        compiler_params=params,
        name="attention_backward",
    )(inputs, grad_resid, packed, probs, w_proj, w_qkv, vecs)
    return outputs, grad_inputs, d_fc1, d_fc2t, d_proj, d_qkv, d_vec, d_vec2, d_b1


def local(
    inputs, cotangent, gain_one, shift_one, w_qkv, b_query, b_value, w_proj, b_proj,
    gain_two, shift_two, w_fc1, b_fc1, w_fc2, b_fc2,
):
    def gather(piece):
        return lax.all_gather(piece, "group", axis=0, tiled=True)

    width = inputs.shape[2]
    members = lax.axis_size("group")
    share = width // members
    small = jnp.concatenate(
        [gain_one, shift_one, b_query, b_value, b_proj, gain_two, shift_two, b_fc2, b_fc1]
    ).reshape(-1, share)
    small = lax.all_gather(small, "group", axis=0)
    vecs = small[:, :8].transpose(1, 0, 2).reshape(8, width)
    bias_fc1 = small[:, 8:].reshape(1, -1)
    bias_qkv = jnp.concatenate([vecs[2], jnp.zeros_like(vecs[2]), vecs[3]]).reshape(1, -1)
    outputs, grad_inputs, d_fc1, d_fc2t, d_proj, d_qkv, d_vec, d_vec2, d_b1 = compute(
        inputs, cotangent, gather(w_qkv), gather(w_proj), gather(w_fc1), gather(w_fc2), vecs, bias_qkv, bias_fc1
    )
    token_total = inputs.shape[0] * inputs.shape[1] * lax.axis_size("replica") * members
    factor = float(token_total) ** (-0.5)
    big = jnp.concatenate([d_qkv, d_proj, d_fc1, d_fc2t], axis=1)
    position = lax.axis_index("group")
    flat = jnp.concatenate([d_vec[:4].reshape(-1), d_vec2[:4].reshape(-1), d_b1.reshape(-1)])
    big, flat = lax.psum((big, flat), ("replica", "group"))
    big = big.astype(F32) * factor
    flat = flat * factor
    cut = [3 * width, 4 * width, 4 * width + w_fc1.shape[1]]

    def rows(block):
        return lax.dynamic_slice_in_dim(block, position * (block.shape[0] // members), block.shape[0] // members, 0)

    g_qkv, g_proj, g_fc1 = (rows(big[:, a:b]) for a, b in zip([0] + cut, cut))
    g_fc2 = rows(big[:, cut[2] :].T)
    names = ["b_proj", "gain_two", "shift_two", "b_fc2", "b_query", "b_value", "gain_one", "shift_one"]
    got = {name: rows(flat[k * width : (k + 1) * width]) for k, name in enumerate(names)}
    g_b1 = rows(flat[8 * width :])
    return (
        outputs, grad_inputs, got["gain_one"], got["shift_one"], g_qkv, got["b_query"], got["b_value"],
        g_proj, got["b_proj"], got["gain_two"], got["shift_two"], g_fc1, g_b1, g_fc2, got["b_fc2"],
    )


def solution(mesh):
    images = P(("replica", "group"), None, None)
    line, table = P("group"), P("group", None)
    params = (line, line, table, line, line, table, line, line, line, table, line, table, line)
    return jax.shard_map(
        local, mesh=mesh, in_specs=(images, images) + params, out_specs=(images, images) + params, check_vma=False
    )
```

time: 724 us -> 350 us (0.48)
  matrix products: 302 us -> 0 us
  local copies, waits for them, and re-layouts: 174 us -> 24.1 us
  Pallas kernels: 0 us -> 137 us
  other arithmetic: 62.9 us -> 5.89 us
    dot_general x18 -> x0, matrix products: 302 us -> none  [the longest x4 87.2 us: product(): return jnp.dot(left, right, preferred_element_type=jnp.float32)]
    pallas_call x0 -> x3, Pallas kernels: none -> 137 us  [the longest x1 54.3 us: compute(): pl.pallas_call(functools.partial(mlp_both, length, pitch, count, 256), gr...]
    reshape x7 -> x5, local copies, waits for them, and re-layouts: 64 us -> 1.98 us  [the longest x1 0.68 us: local(): vecs = small[:, :8].transpose(1, 0, 2).reshape(8, width)]
    unnamed x100 -> x17, local copies, waits for them, and re-layouts: 49 us -> 3.8 us
    convert_element_type x6 -> x0, local copies, waits for them, and re-layouts: 43.3 us -> none  [the longest x2 30.7 us: backward_pass(): grad_packed_b = jnp.stack([grad_query, grad_keys, grad_values], axis=2).r...]
    reduce_sum x6 -> x0, other arithmetic: 23.6 us -> none  [the longest x1 10.6 us: forward_pass(): log_total = jax.nn.logsumexp(scores, axis=-1, keepdims=True)]
    slice x1 -> x11, local copies, waits for them, and re-layouts: 16.3 us -> 2.05 us  [the longest x1 2 us: local(): g_fc2 = rows(big[:, cut[2]:].T)]
    convert_element_type x10 -> x0, other arithmetic: 13.4 us -> none  [the longest x1 6.93 us: backward_pass(): grad_packed_b = jnp.stack([grad_query, grad_keys, grad_values], axis=2).r...]
  transfers between devices with their start and end apart: 3 -> 3, of which waited for: 1 -> 1; matrix products, arithmetic and copies ran while one was open for 40% -> 4% of each run, Pallas kernels for 0% -> 11%
where the time goes in v1:
time: 350 us; the launch traced here: 349 us
  Pallas kernels  137 us (39%)
  waiting for transfers between devices  94.8 us (27%)
  blocking collectives  73.7 us (21%)
  local copies, waits for them, and re-layouts  24.1 us (7%)
  between operations  13.9 us (4%)
  other arithmetic  5.89 us (2%)
    psum x1, waiting for transfers between devices, local(): big, flat = lax.psum((big, flat), ('replica', 'group'))  93.4 us
    pallas_call x1, Pallas kernels, compute(): pl.pallas_call(functools.partial(mlp_both, length, pitch, count, 256), gr...  54.3 us
    pallas_call x1, Pallas kernels, compute(): pl.pallas_call(functools.partial(attention_backward, length, pitch, count...  45.9 us
    psum x1, blocking collectives, local(): big, flat = lax.psum((big, flat), ('replica', 'group'))  40.2 us
    pallas_call x1, Pallas kernels, compute(): pl.pallas_call(functools.partial(attention_forward, length, pitch, count)...  36.8 us
    all_gather x2, blocking collectives, gather(): return lax.all_gather(piece, 'group', axis=0, tiled=True)  28.2 us
    dynamic_slice x13, local copies, waits for them, and re-layouts, rows(): lax.dynamic_slice_in_dim(block, position * (block.shape[0] // members), b...  9.88 us
  transfers between devices with their start and end apart: 3, of which 1 were waited for; matrix products, arithmetic and copies ran while one was open for 4% of the time, Pallas kernels for 11%

profile of v1, /device:TPU:0, one launch (start us, length us, event | category | flops | bytes accessed | tf_op | source)
XLA Modules:
  0.0 349.4 jit_solution(14505835633055198855)
XLA Ops:
  7.2 0.7 all-gather.3.cloned.1.call-update
  8.0 0.7 all-gather.5.cloned.1.call-update
  8.7 6.1 %concatenate.12 = bf16[2304]{0:T(1024)(128)(2,1)S(1)} concatenate(bf16[192]{0:T(256)(128)(2,1)} %param.17, bf16[192]{0:T(256)(128)(2,1)} %param.18, bf16[192]{0:T(256)(128)(2,1)} %param.20, bf16[192]{0:T(256)(128)(2,1)} %param.21, bf16[192]{0:T(256)(128)(2,1)} %param.23, bf16[192]{0:T(256)(128)(2,1)} %param.24, bf16[192]{0:T(256)(128)(2,1)} %param.25, bf16[192]{0:T(256)(128)(2,1)} %param.29, ...), dimensions={0} | concatenate | bytes 9216 | tf_op jit(solution)/shard_map/concatenate | solution.py:340
  14.9 5.3 %all_gather.16 = bf16[2,12,192]{2,1,0:T(8,128)(2,1)S(1)} all-gather(bf16[1,12,192]{2,1,0:T(8,128)(2,1)S(1)} %all_gather_reshape.3), channel_id=1, replica_groups=mesh['replica'=16,'group'=2] {'group'}, dimensions={0}, use_global_device_ids=true | all-gather | bytes 13824 | tf_op jit(solution)/shard_map/all_gather | solution.py:343
  20.5 0.6 reshape.53.bias_ref
  21.1 0.7 reshape.52.vec_ref
  21.7 0.7 reshape.54.b1_ref
  22.4 22.0 %all_gather.15.w_ref = bf16[384,1152]{1,0:T(8,128)(2,1)} all-gather(bf16[192,1152]{1,0:T(8,128)(2,1)} %param.19), channel_id=1, replica_groups=mesh['replica'=16,'group'=2] {'group'}, dimensions={0}, use_global_device_ids=true | all-gather | bytes 1327104 | tf_op jit(solution)/shard_map/all_gather | solution.py:335
  44.4 36.8 %attention_forward.1 = (bf16[20,208,1152]{2,1,0:T(8,128)(2,1)}, bf16[20,6,208,208]{3,2,1,0:T(8,128)(2,1)}, bf16[20,208,384]{2,1,0:T(8,128)(2,1)}) custom-call(bf16[20,197,384]{2,1,0:T(8,128)(2,1)} %x_ref.5, bf16[384,1152]{1,0:T(8,128)(2,1)} %all_gather.15.w_ref, bf16[8,384]{1,0:T(8,128)(2,1)} %reshape.52.vec_ref, bf16[1,1152]{1,0:T(2,128)(2,1)} %reshape.53.bias_ref), custom_call_target="tpu_custom_call" | custom-call | tf_op jit(solution)/shard_map/attention_forward/pallas_call | solution.py:250
  81.2 6.2 %all_gather.17.wp_ref = bf16[384,384]{1,0:T(8,128)(2,1)} all-gather(bf16[192,384]{1,0:T(8,128)(2,1)S(1)} %copy-done.4), channel_id=1, replica_groups=mesh['replica'=16,'group'=2] {'group'}, dimensions={0}, use_global_device_ids=true | all-gather | bytes 442368 | tf_op jit(solution)/shard_map/all_gather | solution.py:335
  87.3 54.3 %mlp_both.1 = (bf16[20,197,384]{2,1,0:T(8,128)(2,1)}, f32[20,208,384]{2,1,0:T(8,128)}, bf16[384,1536]{1,0:T(8,128)(2,1)}, bf16[384,1536]{1,0:T(8,128)(2,1)}, bf1...) custom-call(bf16[20,197,384]{2,1,0:T(8,128)(2,1)} %x_ref.5, bf16[20,197,384]{2,1,0:T(8,128)(2,1)} %ct_ref.1, ...), custom_call_target="tpu_custom_call" | custom-call | tf_op jit(solution)/shard_map/mlp_both/pallas_call | solution.py:271
  141.6 45.9 %attention_backward.1 = (f32[20,197,384]{2,1,0:T(8,128)}, bf16[384,1152]{1,0:T(8,128)(2,1)}, f32[8,384]{1,0:T(8,128)}) custom-call(bf16[20,197,384]{2,1,0:T(8,128)(2,1)} %x_ref.5, f32[20,208,384]{2,1,0:T(8,128)} %get-tuple-element.30.gr_ref, bf16[20,208,1152]{2,1,0:T(8,128)(2,1)} %get-tuple-element.31.packed_ref, ...), custom_call_target="tpu_custom_call" | custom-call | tf_op jit(solution)/shard_map/attention_backward/pallas_call | solution.py:304
  187.5 2.9 pad_maximum_fusion
  190.5 0.7 copy-done.7
  191.3 40.2 %psum.14 = f32[4608]{0:T(1024)S(1)} all-reduce(f32[4608]{0:T(1024)S(1)} %pad_maximum_fusion.1), channel_id=1, replica_groups=mesh['replica'=16,'group'=2] {'replica','group'}, use_global_device_ids=true, to_apply=%region_0.0 | all-reduce | flops 4608 | bytes 36864 | tf_op jit(solution)/shard_map/psum | solution.py:355
  231.5 0.6 dynamic_slice.42
  232.1 0.6 dynamic_slice.43
  232.8 0.6 dynamic_slice.45
  233.4 0.6 dynamic_slice.46
  234.0 0.6 dynamic_slice.47
  234.7 0.6 dynamic_slice.51
  235.3 0.6 dynamic_slice.40
  235.9 0.6 dynamic_slice.39
  236.6 0.7 dynamic_slice.49
  237.2 93.4 %all-reduce.2.cloned.1.call-done = bf16[384,4608]{1,0:T(8,128)(2,1)} async-done(((bf16[384,4608]{1,0:T(8,128)(2,1)}), bf16[384,4608]{1,0:T(8,128)(2,1)}) %all-reduce.2.cloned.1.call-update) | async-done | bytes 3538960 | tf_op jit(solution)/shard_map/psum | solution.py:355
  330.6 2.9 convert_multiply_fusion
  333.6 2.0 fusion
  335.6 1.7 copy-done
  337.4 1.4 copy.37
  338.8 2.4 constant_dynamic-slice_fusion
  341.1 1.0 constant_dynamic-slice_fusion.2
  342.1 0.7 constant_dynamic-slice_fusion.1
  (43 shorter events, 0.6 us)
Async XLA Ops:
  7.2 74.0 %copy-start.4 = (bf16[192,384]{1,0:T(8,128)(2,1)S(1)}, bf16[192,384]{1,0:T(8,128)(2,1)}, u32[]{:S(2)}) copy-start(bf16[192,384]{1,0:T(8,128)(2,1)} %param.22) | copy-start | bytes 442372
  7.2 80.1 %all-gather.3.cloned.1.call-start = ((), (), s32[]{:S(2)}) async-start(), calls=%async_computation | async-start | bytes 1769472 | tf_op jit(solution)/shard_map/all_gather | solution.py:335
  7.9 79.4 %all-gather.5.cloned.1.call-start = ((), (), s32[]{:S(2)}) async-start(), calls=%async_computation.1 | async-start | bytes 1769472 | tf_op jit(solution)/shard_map/all_gather | solution.py:335
  8.7 322.0 %all-reduce.2.cloned.1.call-start = ((), (), s32[]{:S(2)}) async-start(), calls=%async_computation.2 | async-start | bytes 7077888 | tf_op jit(solution)/shard_map/psum | solution.py:355
  141.6 45.9 %copy-start.1 = (bf16[384,1536]{1,0:T(8,128)(2,1)S(1)}, bf16[384,1536]{1,0:T(8,128)(2,1)}, u32[]{:S(2)}) copy-start(bf16[384,1536]{1,0:T(8,128)(2,1)} %get-tuple-element.39) | copy-start | bytes 3538948
  141.6 45.9 %copy-start.2 = (bf16[384,1536]{1,0:T(8,128)(2,1)S(1)}, bf16[384,1536]{1,0:T(8,128)(2,1)}, u32[]{:S(2)}) copy-start(bf16[384,1536]{1,0:T(8,128)(2,1)} %get-tuple-element.40) | copy-start | bytes 3538948
  141.6 45.9 %copy-start.3 = (bf16[384,384]{1,0:T(8,128)(2,1)S(1)}, bf16[384,384]{1,0:T(8,128)(2,1)}, u32[]{:S(2)}) copy-start(bf16[384,384]{1,0:T(8,128)(2,1)} %get-tuple-element.38) | copy-start | bytes 884740
  190.5 0.7 copy-start.7
  190.5 0.7 copy-start.6
  190.5 0.7 copy-start.5
  333.6 3.7 %copy-start = (f32[384,4608]{1,0:T(8,128)}, f32[384,4608]{1,0:T(8,128)S(1)}, u32[]{:S(2)}) copy-start(f32[384,4608]{1,0:T(8,128)S(1)} %convert_multiply_fusion) | copy-start | bytes 21233668
  337.3 3.8 %slice-start = ((f32[384,4608]{1,0:T(8,128)}), f32[384,1152]{1,0:T(8,128)S(1)}, s32[]{:S(2)}) async-start(f32[384,4608]{1,0:T(8,128)} %copy-done), calls=%async_computation.3 | async-start | bytes 3538944 | tf_op jit(solution)/shard_map/slice | solution.py:363
  337.4 4.7 %slice-start.1 = ((f32[384,4608]{1,0:T(8,128)}), f32[384,384]{1,0:T(8,128)S(1)}, s32[]{:S(2)}) async-start(f32[384,4608]{1,0:T(8,128)} %copy-done), calls=%async_computation.4 | async-start | bytes 1179648 | tf_op jit(solution)/shard_map/slice | solution.py:363
Sparse Core Ops, SparseCore 0:
  9.5 33.2 all-gather.2
  44.4 22.5 all-gather.4
  190.6 139.9 all-reduce.1

commit v2 on v1

v2 whole, which is shorter than its diff:
```python
import functools

import jax
import jax.numpy as jnp
from jax import lax
from jax.experimental import pallas as pl
from jax.experimental.pallas import tpu as pltpu
from jax.sharding import PartitionSpec as P

HEADS = 6
EPS = 1e-06
BF = jnp.bfloat16
F32 = jnp.float32
LOG2E = 1.4426950408889634
VMEM_LIMIT = 60 * 1024 * 1024
MESH = pl.DeviceIdType.MESH
LANES = 128
QUAD = 4


def dot(left, right):
    return jnp.dot(left, right, preferred_element_type=F32)


def dot_lt(left, right):
    return lax.dot_general(left, right, (((0,), (0,)), ((), ())), preferred_element_type=F32)


def dot_rt(left, right):
    return lax.dot_general(left, right, (((1,), (1,)), ((), ())), preferred_element_type=F32)


def row_stats(rows):
    centre = jnp.mean(rows, axis=-1, keepdims=True)
    centered = rows - centre
    inverse = lax.rsqrt(jnp.mean(centered * centered, axis=-1, keepdims=True) + EPS)
    return centered * inverse, inverse


def norm_back(grad_hidden, normed, inverse, gain):
    grad_normed = grad_hidden * gain
    one = jnp.mean(grad_normed, axis=-1, keepdims=True)
    two = jnp.mean(grad_normed * normed, axis=-1, keepdims=True)
    return inverse * (grad_normed - one - normed * two)


def col_sum(rows):
    return jnp.sum(rows, axis=0, keepdims=True)


def place():
    return lax.axis_index("replica"), lax.axis_index("group")


def greet(partners):
    barrier = pltpu.get_barrier_semaphore()
    for partner in partners:
        pl.semaphore_signal(barrier, inc=1, device_id=partner, device_id_type=MESH)
    pl.semaphore_wait(barrier, len(partners))


def remote(source, target, send, recv, device):
    return pltpu.make_async_remote_copy(
        src_ref=source, dst_ref=target, send_sem=send, recv_sem=recv, device_id=device, device_id_type=MESH
    )


class Gather:
    def __init__(self, shards, wholes, sends, recvs, passes, arrivals):
        self.replica, self.group = place()
        core = lax.rem(self.replica, 2)
        self.across = (self.replica, 1 - self.group)
        self.beside = (self.replica + 1 - 2 * core, self.group)
        self.first, self.second = [], []
        for k, (shard, whole_ref) in enumerate(zip(shards, wholes)):
            rows = shard.shape[0]
            half = rows // 2
            mine = pl.ds(pl.multiple_of(core * half, half), half)
            there = pl.ds(pl.multiple_of(self.group * rows + core * half, half), half)
            here = pl.ds(pl.multiple_of((1 - self.group) * rows + core * half, half), half)
            self.first.append(remote(shard.at[mine], whole_ref.at[there], sends.at[k], recvs.at[k], self.across))
            self.second.append(
                remote(whole_ref.at[here], whole_ref.at[here], passes.at[k], arrivals.at[k], self.beside)
            )


def attention_forward(
    length, pitch, count, late,
    x_ref, wq_hbm, wp_hbm, w1_hbm, w2_hbm, g1, s1, bq, bv, bp, g2, s2, b2, b1,
    packed_ref, probs_ref, att_ref, wq_out, wp_out, w1_out, w2_out, vec_out, b1_out,
    pad_ref, wq, wp, w1, w2, small, wide, vec, bias, b1_full,
    sends, recvs, passes, arrivals, vec_send, vec_recv, own_sem, out_sem,
):
    step = pl.program_id(0)
    width = x_ref.shape[2]
    head_dim = width // HEADS
    pair = 2 * head_dim
    factor = head_dim ** (-0.5) * LOG2E
    shards = (wq_hbm, wp_hbm, w1_hbm, w2_hbm)
    wholes = (wq, wp, w1, w2)
    outs = (wq_out, wp_out, w1_out, w2_out)
    move = Gather(shards, wholes, sends, recvs, passes, arrivals)
    group = move.group
    small_copy = remote(small.at[group], small.at[group], vec_send.at[0], vec_recv.at[0], move.across)
    wide_copy = remote(wide.at[group], wide.at[group], vec_send.at[1], vec_recv.at[1], move.across)
    owns = [
        pltpu.make_async_copy(
            shard, full.at[pl.ds(pl.multiple_of(group * shard.shape[0], shard.shape[0]), shard.shape[0])], own_sem.at[k]
        )
        for k, (shard, full) in enumerate(zip(shards, wholes))
    ]
    flush = [pltpu.make_async_copy(full, out, out_sem.at[k]) for k, (full, out) in enumerate(zip(wholes, outs))]
    last = pl.num_programs(0) - 1

    @pl.when(step == 0)
    def _():
        pad_ref[...] = jnp.zeros_like(pad_ref)
        share = g1.shape[0]
        for k, ref in enumerate((g1, s1, bq, bv, bp, g2, s2, b2)):
            small[group, k : k + 1, 0:share] = ref[...].reshape(1, share).astype(F32)
        wide[group, 0:1, :] = b1[...].reshape(1, b1.shape[0]).astype(F32)
        greet((move.across, move.beside))
        small_copy.start()
        for copy in move.first:
            copy.start()
        wide_copy.start()
        for copy in owns:
            copy.start()
        small_copy.wait()
        for side in range(2):
            vec[:, side * share : (side + 1) * share] = small[side, :, 0:share]
        bias[0:1, 0:width] = vec[2:3, :]
        bias[0:1, width : 2 * width] = jnp.zeros((1, width), F32)
        bias[0:1, 2 * width : 3 * width] = vec[3:4, :]
        vec_out[...] = vec[...]
        move.first[0].wait()
        move.second[0].start()
        owns[0].wait()
        move.second[0].wait()

    @pl.when(step == late)
    def _():
        for k in range(1, 4):
            move.first[k].wait()
            move.second[k].start()
        wide_copy.wait()
        for side in range(2):
            b1_full[0:1, side * b1.shape[0] : (side + 1) * b1.shape[0]] = wide[side, 0:1, :]
        b1_out[...] = b1_full[...]
        for k in range(1, 4):
            owns[k].wait()

    @pl.when(step == late + 2)
    def _():
        for k in range(1, 4):
            move.second[k].wait()
        for copy in flush:
            copy.start()

    gain = vec[0:1, :]
    shift = vec[1:2, :]
    for image in range(count):
        pad_ref[image * pitch : image * pitch + length, :] = x_ref[image]
    normed, _ = row_stats(pad_ref[...].astype(F32))
    hidden = (normed * gain + shift).astype(BF)
    packed = (dot(hidden, wq[...]) + bias[0:1, :]).astype(BF)
    for image in range(count):
        packed_ref[image] = packed[image * pitch : (image + 1) * pitch]
    lane = lax.broadcasted_iota(jnp.int32, (pitch, pair), 1)
    tail = length // 8 * 8
    row = lax.broadcasted_iota(jnp.int32, (pitch - tail, pitch), 0) + tail
    for image in range(count):
        for two in range(HEADS // 2):
            cols = slice(two * pair, (two + 1) * pair)
            query = packed_ref[image, :, two * pair : (two + 1) * pair]
            keys = packed_ref[image, :, width + two * pair : width + (two + 1) * pair]
            values = packed_ref[image, :, 2 * width + two * pair : 2 * width + (two + 1) * pair]
            values_t = values.T
            parts = []
            for side in range(2):
                own = (lane < head_dim) if side == 0 else (lane >= head_dim)
                scores = dot_rt(keys, jnp.where(own, query, jnp.zeros_like(query)))
                low = jnp.where(row < length, scores[tail:], -1e30)
                scores = jnp.concatenate([scores[:tail], low], axis=0)
                top = jnp.max(scores, axis=0, keepdims=True)
                raised = jnp.exp2((scores - top) * factor)
                total = jnp.sum(raised, axis=0, keepdims=True)
                probs = (raised * (1.0 / total)).astype(BF)
                probs_ref[image, 2 * two + side] = probs
                parts.append(dot(values_t[side * head_dim : (side + 1) * head_dim], probs))
            mixed = jnp.concatenate(parts, axis=0)
            att_ref[image, :, cols] = mixed.T.astype(BF)

    @pl.when(step == last)
    def _():
        for copy in flush:
            copy.wait()


def gelu_parts(values):
    half = 0.5 * (1.0 + lax.erf(values * 0.7071067811865476))
    slope = half + values * jnp.exp(-0.5 * values * values) * 0.3989422804014327
    return half, slope


def mlp_both(
    length, pitch, count, chunk,
    x_ref, ct_ref, att_ref, wp_ref, w1_ref, w2_ref, vec_ref, b1_ref,
    y_ref, gr_ref, ga_ref, unit_ref, strip_ref, dvec_ref,
    xpad, ctpad, act_ref, gp_ref, acc1, acc2, accp, accv, accb,
):
    step = pl.program_id(0)
    width = x_ref.shape[2]
    hidden_units = w1_ref.shape[1]

    @pl.when(step == 0)
    def _():
        for ref in (xpad, ctpad, acc1, acc2, accp, accv, accb):
            ref[...] = jnp.zeros_like(ref)

    for image in range(count):
        xpad[image * pitch : image * pitch + length, :] = x_ref[image]
        ctpad[image * pitch : image * pitch + length, :] = ct_ref[image]
    bias_p = vec_ref[4:5, :]
    gain = vec_ref[5:6, :]
    shift = vec_ref[6:7, :]
    bias_2 = vec_ref[7:8, :]
    ct = ctpad[...]
    att = att_ref[...].reshape(count * pitch, width)
    resid = xpad[...].astype(F32) + dot(att, wp_ref[...]) + bias_p
    normed, inverse = row_stats(resid)
    hidden = (normed * gain + shift).astype(BF)
    for start in range(0, hidden_units, chunk):
        cols = slice(start, start + chunk)
        pre = dot(hidden, w1_ref[:, cols]) + b1_ref[0:1, cols]
        half, slope = gelu_parts(pre)
        act_ref[:, cols] = (pre * half).astype(BF)
        grad_pre = dot_rt(ct, w2_ref[cols, :]) * slope
        accb[0:1, cols] += col_sum(grad_pre)
        gp_ref[:, cols] = grad_pre.astype(BF)
    out = resid + dot(act_ref[...], w2_ref[...]) + bias_2
    for image in range(count):
        y_ref[image] = out[image * pitch : image * pitch + length].astype(BF)
    grad_hidden = dot_rt(gp_ref[...], w1_ref[...])
    top = ct.astype(F32)
    grad_resid = top + norm_back(grad_hidden, normed, inverse, gain)
    accv[0:1, :] += col_sum(grad_resid)
    accv[1:2, :] += col_sum(grad_hidden * normed)
    accv[2:3, :] += col_sum(grad_hidden)
    accv[3:4, :] += col_sum(top)
    gr_ref[...] = grad_resid.reshape(gr_ref.shape)
    grad_resid_b = grad_resid.astype(BF)
    ga_ref[...] = dot_rt(grad_resid_b, wp_ref[...]).astype(BF).reshape(ga_ref.shape)
    acc1[...] += dot_lt(hidden, gp_ref[...])
    acc2[...] += dot_lt(ct, act_ref[...])
    accp[...] += dot_lt(att, grad_resid_b)

    @pl.when(step == pl.num_programs(0) - 1)
    def _():
        share = width // 2
        wide = hidden_units // 2
        for side in range(2):
            rows = slice(side * share, (side + 1) * share)
            for strip in range(hidden_units // LANES):
                unit, at = strip // QUAD, strip % QUAD * share
                unit_ref[unit, side, at : at + share, :] = acc1[rows, strip * LANES : (strip + 1) * LANES].astype(BF)
            for strip in range(wide // LANES):
                unit, at = strip // 2 + hidden_units // (QUAD * LANES), strip % 2 * width
                start = side * wide + strip * LANES
                unit_ref[unit, side, at : at + width, :] = acc2[:, start : start + LANES].astype(BF)
            for strip in range(width // LANES):
                strip_ref[strip, side] = accp[rows, strip * LANES : (strip + 1) * LANES].astype(BF)
        dvec_ref[...] = jnp.zeros_like(dvec_ref)
        dvec_ref[0:4, :] = accv[0:4, :]
        for k in range(hidden_units // width):
            dvec_ref[8 + k : 9 + k, :] = accb[0:1, k * width : (k + 1) * width]


def attention_backward(
    length, pitch, count,
    x_ref, gr_ref, ga_ref, q_ref, k_ref, v_ref, probs_ref, wq_ref, vec_ref, strip_ref, dvec_in,
    gx_ref, unit_ref, dvec_ref,
    pad_ref, hid_ref, gp_ref, acc, accv,
):
    phase, block = pl.program_id(0), pl.program_id(1)
    phases, blocks_ = pl.num_programs(0), pl.num_programs(1)
    width = x_ref.shape[2]
    head_dim = width // HEADS
    pair = 2 * head_dim
    factor = head_dim ** (-0.5)
    rows = count * pitch
    here = pl.ds(pl.multiple_of(block * rows, rows), rows)
    gain = vec_ref[0:1, :]
    shift = vec_ref[1:2, :]

    @pl.when(jnp.logical_and(phase == 0, block == 0))
    def _():
        pad_ref[...] = jnp.zeros_like(pad_ref)
        accv[...] = jnp.zeros_like(accv)

    def stats():
        for image in range(count):
            pad_ref[image * pitch : image * pitch + length, :] = x_ref[image]
        return row_stats(pad_ref[...].astype(F32))

    @pl.when(phase == 0)
    def _():
        normed, _ = stats()
        hid_ref[here, :] = (normed * gain + shift).astype(BF)

    @pl.when(phase < phases - 1)
    def _():
        @pl.when(block == 0)
        def _():
            acc[...] = jnp.zeros_like(acc)

        lane = lax.broadcasted_iota(jnp.int32, (pitch, pair), 1)
        sum_q = jnp.zeros((1, pair), F32)
        sum_v = jnp.zeros((1, pair), F32)
        pieces = []
        for image in range(count):
            query = q_ref[image]
            keys = k_ref[image]
            values = v_ref[image]
            grad_out = ga_ref[image]
            keys_t = keys.T
            grad_values = None
            grad_keys = None
            parts = []
            for side in range(2):
                own = (lane < head_dim) if side == 0 else (lane >= head_dim)
                zero = jnp.zeros_like(query)
                grad_side = jnp.where(own, grad_out, zero)
                probs_b = probs_ref[image, side]
                probs = probs_b.astype(F32)
                grad_probs = dot_rt(values, grad_side)
                delta = jnp.sum(probs * grad_probs, axis=0, keepdims=True)
                grad_scores = (probs * (grad_probs - delta)).astype(BF)
                piece_v = dot(probs_b, grad_side)
                piece_k = dot(grad_scores, jnp.where(own, query, zero))
                grad_values = piece_v if grad_values is None else grad_values + piece_v
                grad_keys = piece_k if grad_keys is None else grad_keys + piece_k
                parts.append(dot(keys_t[side * head_dim : (side + 1) * head_dim], grad_scores))
            grad_query = jnp.concatenate(parts, axis=0).T * factor
            grad_keys = grad_keys * factor
            sum_q += col_sum(grad_query)
            sum_v += col_sum(grad_values)
            pieces.append(
                jnp.concatenate([grad_query.astype(BF), grad_keys.astype(BF), grad_values.astype(BF)], axis=1)
            )
        grad_pair = jnp.concatenate(pieces, axis=0)
        gp_ref[phase, here, :] = grad_pair
        accv[phase, 0:1, :] += sum_q
        accv[phase, 1:2, :] += sum_v
        acc[...] += dot_lt(hid_ref[here, :], grad_pair)

        @pl.when(block == blocks_ - 1)
        def _():
            share = width // 2
            for side in range(2):
                for strip in range(3):
                    unit_ref[phase, side, strip * share : (strip + 1) * share, :] = acc[
                        side * share : (side + 1) * share, strip * pair : (strip + 1) * pair
                    ].astype(BF)
                unit_ref[phase, side, 3 * share :, :] = strip_ref[phase, side]

    @pl.when(phase == phases - 1)
    def _():
        @pl.when(block == 0)
        def _():
            dvec_ref[...] = dvec_in[...]
            for two in range(HEADS // 2):
                dvec_ref[4:6, two * pair : (two + 1) * pair] = accv[two, 0:2, :]

        normed, inverse = stats()
        grad_hidden = None
        for two in range(HEADS // 2):
            for third in range(3):
                cols = slice(third * width + two * pair, third * width + (two + 1) * pair)
                piece = (gp_ref[two, here, third * pair : (third + 1) * pair], wq_ref[:, cols])
                grad_hidden = piece if grad_hidden is None else tuple(
                    jnp.concatenate([a, b], axis=1) for a, b in zip(grad_hidden, piece)
                )
        grad_hidden = dot_rt(*grad_hidden)
        dvec_ref[6:7, :] += col_sum(grad_hidden * normed)
        dvec_ref[7:8, :] += col_sum(grad_hidden)
        grad_x = gr_ref[...].reshape(rows, width) + norm_back(grad_hidden, normed, inverse, gain)
        for image in range(count):
            gx_ref[image] = grad_x[image * pitch : image * pitch + length]


class Reduce:
    STAGES = 8

    def __init__(self, source, bufs, out, sends, recvs):
        self.replica, self.group = place()
        self.source, self.out = source, out
        self.r1, self.b1, self.r2, self.b2, self.rx, self.bx, self.rz, self.ez = bufs
        replicas = lax.axis_size("replica")
        self.extra = replicas // 16
        half = out.shape[1] // 2
        self.half, self.quarter, self.piece = half, half // 2, half // 8
        r = self.replica
        self.core = lax.rem(r, 2)
        self.x = lax.rem(r // 2, 2)
        self.z = lax.rem(r // 4, 4)
        self.e = r // 16
        self.sends, self.recvs = sends, recvs
        low = self.core * half
        self.at_core = pl.ds(pl.multiple_of(low, half), half)
        self.at_quarter = pl.ds(pl.multiple_of(low + self.x * self.quarter, self.quarter), self.quarter)
        self.at_piece = pl.ds(
            pl.multiple_of(low + self.x * self.quarter + self.z * self.piece, self.piece), self.piece
        )

    def partners(self):
        return [self.to_core(), self.to_group(), self.to_x()] + [self.to_z(d) for d in (1, 2, 3)] + [
            self.to_e(d) for d in range(1, self.extra)
        ]

    def to_core(self):
        return (self.replica + 1 - 2 * self.core, self.group)

    def to_group(self):
        return (self.replica, 1 - self.group)

    def to_x(self):
        return (self.replica + 2 - 4 * self.x, self.group)

    def z_at(self, hop):
        return lax.rem(self.z + hop, 4)

    def to_z(self, hop):
        return (self.replica + 4 * (self.z_at(hop) - self.z), self.group)

    def to_e(self, hop):
        return (self.replica + 16 * (lax.rem(self.e + hop, self.extra) - self.e), self.group)

    def copy(self, stage, source, target, device, hop=0):
        return remote(source, target, self.sends.at[stage, hop], self.recvs.at[stage, hop], device)

    def copies(self, stage):
        if stage == 0:
            other = pl.ds(pl.multiple_of((1 - self.core) * self.half, self.half), self.half)
            return [self.copy(0, self.source.at[:, :, other], self.r1, self.to_core())]
        if stage == 1:
            return [self.copy(1, self.b1.at[:, 1 - self.group], self.r2, self.to_group())]
        if stage == 2:
            other = pl.ds(pl.multiple_of((1 - self.x) * self.quarter, self.quarter), self.quarter)
            return [self.copy(2, self.b2.at[:, other], self.rx, self.to_x())]
        if stage == 3:
            out = []
            for hop in (1, 2, 3):
                theirs = pl.ds(pl.multiple_of(self.z_at(hop) * self.piece, self.piece), self.piece)
                out.append(self.copy(3, self.bx.at[:, theirs], self.rz.at[hop - 1], self.to_z(hop), hop))
            return out
        if stage == 4:
            return [
                self.copy(4, self.ez.at[self.e], self.ez.at[self.e], self.to_e(hop), hop) for hop in range(1, self.extra)
            ]
        if stage == 5:
            place_ = self.out.at[:, self.at_piece]
            return [self.copy(5, place_, place_, self.to_z(hop), hop) for hop in (1, 2, 3)]
        if stage == 6:
            place_ = self.out.at[:, self.at_quarter]
            return [self.copy(6, place_, place_, self.to_x())]
        place_ = self.out.at[:, self.at_core]
        return [self.copy(7, place_, place_, self.to_core())]

    def start(self, stage):
        for copy in self.copies(stage):
            copy.start()

    def finish(self, stage):
        for copy in self.copies(stage):
            copy.wait()
        if stage == 0:
            self.b1[...] = (self.source[:, :, self.at_core].astype(F32) + self.r1[...].astype(F32)).astype(BF)
        elif stage == 1:
            self.b2[...] = (self.b1[:, self.group].astype(F32) + self.r2[...].astype(F32)).astype(BF)
        elif stage == 2:
            mine = pl.ds(pl.multiple_of(self.x * self.quarter, self.quarter), self.quarter)
            self.bx[...] = (self.b2[:, mine].astype(F32) + self.rx[...].astype(F32)).astype(BF)
        elif stage == 3:
            mine = pl.ds(pl.multiple_of(self.z * self.piece, self.piece), self.piece)
            total = self.bx[:, mine].astype(F32)
            for hop in range(3):
                total = total + self.rz[hop].astype(F32)
            if self.extra > 1:
                self.ez[self.e] = total.astype(BF)
            else:
                self.out[:, self.at_piece] = total.astype(BF)
        elif stage == 4 and self.extra > 1:
            total = self.ez[0].astype(F32)
            for k in range(1, self.extra):
                total = total + self.ez[k].astype(F32)
            self.out[:, self.at_piece] = total.astype(BF)


def reduce_scratch(units, rows, replicas):
    half, extra = rows // 2, max(replicas // 16, 1)
    hops = max(4, extra)
    return [
        pltpu.VMEM((units, 2, half, LANES), BF), pltpu.VMEM((units, 2, half, LANES), BF),
        pltpu.VMEM((units, half, LANES), BF), pltpu.VMEM((units, half, LANES), BF),
        pltpu.VMEM((units, half // 2, LANES), BF), pltpu.VMEM((units, half // 2, LANES), BF),
        pltpu.VMEM((3, units, half // 8, LANES), BF), pltpu.VMEM((extra, units, half // 8, LANES), BF),
        pltpu.SemaphoreType.DMA((Reduce.STAGES, hops)), pltpu.SemaphoreType.DMA((Reduce.STAGES, hops)),
    ]


class ReduceVectors:
    def __init__(self, like, v1, v2, v3, slots_z, slots_e, got, sends, recvs):
        self.like = like
        self.vals, self.slots_z, self.slots_e, self.got, self.sends, self.recvs = (
            (v1, v2, v3), slots_z, slots_e, got, sends, recvs
        )

    def copies(self, stage):
        o = self.like
        if stage < 3:
            device = (o.to_core, o.to_group, o.to_x)[stage]()
            return [remote(self.vals[stage], self.got.at[stage], self.sends.at[stage, 0], self.recvs.at[stage, 0], device)]
        if stage == 3:
            mine = self.slots_z.at[o.z]
            return [
                remote(mine, mine, self.sends.at[3, hop], self.recvs.at[3, hop], o.to_z(hop)) for hop in (1, 2, 3)
            ]
        mine = self.slots_e.at[o.e]
        return [
            remote(mine, mine, self.sends.at[4, hop], self.recvs.at[4, hop], o.to_e(hop)) for hop in range(1, o.extra)
        ]

    def start(self, stage):
        for copy in self.copies(stage):
            copy.start()

    def finish(self, stage, out):
        o = self.like
        for copy in self.copies(stage):
            copy.wait()
        if stage < 2:
            self.vals[stage + 1][...] = self.vals[stage][...] + self.got[stage]
        elif stage == 2:
            self.slots_z[o.z] = self.vals[2][...] + self.got[2]
        elif stage == 3:
            total = self.slots_z[0] + self.slots_z[1] + self.slots_z[2] + self.slots_z[3]
            if o.extra > 1:
                self.slots_e[o.e] = total
            else:
                out[...] = total
        elif o.extra > 1:
            total = self.slots_e[0]
            for k in range(1, o.extra):
                total = total + self.slots_e[k]
            out[...] = total


def vector_scratch(shape, replicas):
    extra = max(replicas // 16, 1)
    hops = max(4, extra)
    return [
        pltpu.VMEM(shape, F32), pltpu.VMEM(shape, F32), pltpu.VMEM(shape, F32),
        pltpu.VMEM((4,) + shape, F32), pltpu.VMEM((extra,) + shape, F32), pltpu.VMEM((3,) + shape, F32),
        pltpu.SemaphoreType.DMA((5, hops)), pltpu.SemaphoreType.DMA((5, hops)),
    ]


REDUCE_REFS = 10


def reduce_all(a_ref, b_ref, vec_ref, a_out, b_out, vec_out, *scratch):
    parts = []
    half = a_ref.shape[0] // 2
    groups = [(a_ref.at[0:half], a_out.at[0:half]), (a_ref.at[half:], a_out.at[half:]), (b_ref, b_out)]
    for k, (source, out) in enumerate(groups):
        refs = scratch[k * REDUCE_REFS : (k + 1) * REDUCE_REFS]
        parts.append(Reduce(source, refs[:8], out, refs[8], refs[9]))
    refs = scratch[3 * REDUCE_REFS :]
    vectors = ReduceVectors(parts[0], *refs)
    refs[0][...] = vec_ref[...]
    greet(parts[0].partners())
    vectors.start(0)
    for part in parts[:1]:
        part.start(0)
    for tick in range(Reduce.STAGES + 2):
        if tick < 2:
            parts[tick + 1].start(0)
        for k in range(3):
            stage = tick - k
            if 0 <= stage < Reduce.STAGES:
                parts[k].finish(stage)
                if stage + 1 < Reduce.STAGES:
                    parts[k].start(stage + 1)
        if tick < 5:
            vectors.finish(tick, vec_out)
            if tick < 4:
                vectors.start(tick + 1)


def unpack(factor, fc_ref, qkv_ref, vec_ref, g1, s1, wq, bq, bv, wp, bp, g2, s2, w1, b1, w2, b2):
    share, width = wp.shape
    group = lax.axis_index("group")
    pair = LANES
    for two in range(qkv_ref.shape[0]):
        for third in range(3):
            wq[:, third * width + two * pair : third * width + (two + 1) * pair] = (
                qkv_ref[two, third * share : (third + 1) * share, :].astype(F32) * factor
            )
        wp[:, two * pair : (two + 1) * pair] = qkv_ref[two, 3 * share :, :].astype(F32) * factor
    strips = w1.shape[1] // LANES
    for strip in range(strips):
        unit, at = strip // QUAD, strip % QUAD * share
        w1[:, strip * LANES : (strip + 1) * LANES] = fc_ref[unit, at : at + share, :].astype(F32) * factor
    for strip in range(w2.shape[0] // LANES):
        unit, at = strip // 2 + strips // QUAD, strip % 2 * width
        w2[strip * LANES : (strip + 1) * LANES, :] = (fc_ref[unit, at : at + width, :].astype(F32) * factor).T
    rows = vec_ref[...] * factor
    mine = jnp.where(group == 0, rows[:, 0:share], rows[:, share:])
    for k, ref in enumerate((bp, g2, s2, b2, bq, bv, g1, s1)):
        ref[...] = mine[k : k + 1, :].reshape(share)
    per = b1.shape[0] // width
    for k in range(per):
        row = jnp.where(group == 0, rows[8 + k : 9 + k, :], rows[8 + per + k : 9 + per + k, :])
        b1[k * width : (k + 1) * width] = row.reshape(width)


def whole(array):
    return pl.BlockSpec(array.shape, lambda *_: (0,) * len(array.shape))


def blocks(count, *rest):
    return pl.BlockSpec((count,) + rest, lambda i: (i,) + (0,) * len(rest))


def fixed(*shape):
    return pl.BlockSpec(shape, lambda *_: (0,) * len(shape))


def params(axes=1, **kw):
    return pltpu.CompilerParams(vmem_limit_bytes=VMEM_LIMIT, dimension_semantics=("arbitrary",) * axes, **kw)


HBM = pl.BlockSpec(memory_space=pl.ANY)
sds = jax.ShapeDtypeStruct


def forward_part(inputs, weights, vectors, pitch, members):
    images, length, width = inputs.shape
    count = 2
    share, wide = vectors[0].shape[0], vectors[-1].shape[0]
    lanes = (share + LANES - 1) // LANES * LANES
    fulls = [(members * w.shape[0], w.shape[1]) for w in weights]
    return pl.pallas_call(
        functools.partial(attention_forward, length, pitch, count, 5),
        grid=(images // count,),
        in_specs=[blocks(count, length, width)] + [HBM] * 4 + [whole(v) for v in vectors],
        out_specs=[
            blocks(count, pitch, 3 * width), blocks(count, HEADS, pitch, pitch), blocks(count, pitch, width),
            HBM, HBM, HBM, HBM, fixed(8, width), fixed(8, members * wide),
        ],
        out_shape=[
            sds((images, pitch, 3 * width), BF), sds((images, HEADS, pitch, pitch), BF), sds((images, pitch, width), BF),
        ] + [sds(full, BF) for full in fulls] + [sds((8, width), F32), sds((8, members * wide), F32)],
        scratch_shapes=[pltpu.VMEM((count * pitch, width), BF)] + [pltpu.VMEM(full, BF) for full in fulls] + [
            pltpu.VMEM((members, 8, lanes), F32), pltpu.VMEM((members, 8, wide), F32),
            pltpu.VMEM((8, width), F32), pltpu.VMEM((8, 3 * width), F32), pltpu.VMEM((8, members * wide), F32),
            pltpu.SemaphoreType.DMA((4,)), pltpu.SemaphoreType.DMA((4,)), pltpu.SemaphoreType.DMA((4,)),
            pltpu.SemaphoreType.DMA((4,)), pltpu.SemaphoreType.DMA((2,)), pltpu.SemaphoreType.DMA((2,)),
            pltpu.SemaphoreType.DMA((4,)), pltpu.SemaphoreType.DMA((4,)),
        ],
        compiler_params=params(collective_id=0, has_side_effects=True),
        name="attention_forward",
    )(inputs, *weights, *vectors)


def middle_part(inputs, cotangent, attended, w_proj, w_fc1, w_fc2, vecs, bias_fc1, pitch):
    images, length, width = inputs.shape
    hidden_units = w_fc1.shape[1]
    count = 2
    rows = count * pitch
    units = 2 * hidden_units // (QUAD * LANES)
    unit_rows = QUAD * width // 2
    unit = (units, 2, unit_rows, LANES)
    strip = (width // LANES, 2, width // 2, LANES)
    return pl.pallas_call(
        functools.partial(mlp_both, length, pitch, count, 256),
        grid=(images // count,),
        in_specs=[blocks(count, length, width), blocks(count, length, width), blocks(count, pitch, width)] + [
            whole(w) for w in (w_proj, w_fc1, w_fc2, vecs, bias_fc1)
        ],
        out_specs=[
            blocks(count, length, width), blocks(count, pitch, width), blocks(count, pitch, width),
            fixed(*unit), fixed(*strip), fixed(16, width),
        ],
        out_shape=[
            sds((images, length, width), BF), sds((images, pitch, width), F32), sds((images, pitch, width), BF),
            sds(unit, BF), sds(strip, BF), sds((16, width), F32),
        ],
        scratch_shapes=[
            pltpu.VMEM((rows, width), BF), pltpu.VMEM((rows, width), BF),
            pltpu.VMEM((rows, hidden_units), BF), pltpu.VMEM((rows, hidden_units), BF),
            pltpu.VMEM((width, hidden_units), F32), pltpu.VMEM((width, hidden_units), F32),
            pltpu.VMEM((width, width), F32), pltpu.VMEM((8, width), F32), pltpu.VMEM((8, hidden_units), F32),
        ],
        compiler_params=params(),
        name="mlp_both",
    )(inputs, cotangent, attended, w_proj, w_fc1, w_fc2, vecs, bias_fc1)


def backward_part(inputs, grad_resid, grad_att, packed, probs, w_qkv, vecs, strips, dvec, pitch):
    images, length, width = inputs.shape
    count = 4
    rows = count * pitch
    steps = images // count
    pairs = HEADS // 2
    pair = width // pairs
    unit = (pairs, 2, QUAD * width // 2, LANES)

    def edge(p, i):
        return jnp.where(jnp.logical_or(p == 0, p == pairs), i, steps - 1)

    def tail(p, i):
        return jnp.where(p == pairs, i, 0)

    def core(p, i):
        return jnp.where(p == pairs, steps - 1, i), jnp.minimum(p, pairs - 1)

    def part(third):
        def index(p, i):
            at, col = core(p, i)
            return at, 0, third * pairs + col

        return pl.BlockSpec((count, pitch, pair), index)

    def probs_at(p, i):
        at, col = core(p, i)
        return at, col, 0, 0

    return pl.pallas_call(
        functools.partial(attention_backward, length, pitch, count),
        grid=(pairs + 1, steps),
        in_specs=[
            pl.BlockSpec((count, length, width), lambda p, i: (edge(p, i), 0, 0)),
            pl.BlockSpec((count, pitch, width), lambda p, i: (tail(p, i), 0, 0)),
            part(0), part(0), part(1), part(2),
            pl.BlockSpec((count, 2, pitch, pitch), probs_at),
            whole(w_qkv), whole(vecs), whole(strips), whole(dvec),
        ],
        out_specs=[
            pl.BlockSpec((count, length, width), lambda p, i: (tail(p, i), 0, 0)), fixed(*unit), fixed(16, width),
        ],
        out_shape=[sds((images, length, width), F32), sds(unit, BF), sds((16, width), F32)],
        scratch_shapes=[
            pltpu.VMEM((rows, width), BF), pltpu.VMEM((images * pitch, width), BF),
            pltpu.VMEM((pairs, images * pitch, 3 * pair), BF), pltpu.VMEM((width, 3 * pair), F32),
            pltpu.VMEM((pairs, 8, pair), F32),
        ],
        compiler_params=params(2),
        name="attention_backward",
    )(inputs, grad_resid, grad_att, packed, packed, packed, probs, w_qkv, vecs, strips, dvec)


def reduce_part(fc_units, qkv_units, dvec, replicas):
    vmem = pl.BlockSpec(memory_space=pltpu.VMEM)
    three, rows = fc_units.shape[0] // 2, fc_units.shape[2]
    scratch = []
    for units in (three, three, qkv_units.shape[0]):
        scratch += reduce_scratch(units, rows, replicas)
    scratch += vector_scratch(dvec.shape, replicas)
    return pl.pallas_call(
        reduce_all,
        in_specs=[vmem] * 3,
        out_specs=[vmem] * 3,
        out_shape=[
            sds((fc_units.shape[0], rows, LANES), BF), sds((qkv_units.shape[0], rows, LANES), BF), sds(dvec.shape, F32),
        ],
        scratch_shapes=scratch,
        compiler_params=pltpu.CompilerParams(vmem_limit_bytes=VMEM_LIMIT, collective_id=1, has_side_effects=True),
        name="reduce_all",
    )(fc_units, qkv_units, dvec)


def local(
    inputs, cotangent, gain_one, shift_one, w_qkv, b_query, b_value, w_proj, b_proj,
    gain_two, shift_two, w_fc1, b_fc1, w_fc2, b_fc2,
):
    images, length, width = inputs.shape
    members = lax.axis_size("group")
    replicas = lax.axis_size("replica")
    pitch = (length + 15) // 16 * 16
    packed, probs, attended, wq, wp, w1, w2, vecs, bias_fc1 = forward_part(
        inputs, (w_qkv, w_proj, w_fc1, w_fc2),
        (gain_one, shift_one, b_query, b_value, b_proj, gain_two, shift_two, b_fc2, b_fc1), pitch, members,
    )
    outputs, grad_resid, grad_att, fc_units, strips, dvec = middle_part(
        inputs, cotangent, attended, wp, w1, w2, vecs, bias_fc1, pitch
    )
    grad_inputs, qkv_units, dvec = backward_part(
        inputs, grad_resid, grad_att, packed, probs, wq, vecs, strips, dvec, pitch
    )
    fc_sum, qkv_sum, vec_sum = reduce_part(fc_units, qkv_units, dvec, replicas)
    factor = float(images * length * replicas * members) ** (-0.5)
    weights = (gain_one, shift_one, w_qkv, b_query, b_value, w_proj, b_proj, gain_two, shift_two, w_fc1, b_fc1, w_fc2, b_fc2)
    grads = pl.pallas_call(
        functools.partial(unpack, factor),
        out_shape=[sds(w.shape, F32) for w in weights],
        compiler_params=pltpu.CompilerParams(vmem_limit_bytes=VMEM_LIMIT),
        name="unpack",
    )(fc_sum, qkv_sum, vec_sum)
    return (outputs, grad_inputs) + tuple(grads)


def solution(mesh):
    images = P(("replica", "group"), None, None)
    line, table = P("group"), P("group", None)
    specs = (line, line, table, line, line, table, line, line, line, table, line, table, line)
    return jax.shard_map(
        local, mesh=mesh, in_specs=(images, images) + specs, out_specs=(images, images) + specs, check_vma=False
    )
```

time: 350 us -> 225 us (0.64)
  waiting for transfers between devices: 94.8 us -> 0 us
  Pallas kernels: 137 us -> 224 us
  blocking collectives: 73.7 us -> 0 us
  local copies, waits for them, and re-layouts: 24.1 us -> 0 us
  between operations: 13.9 us -> 0.84 us
  other arithmetic: 5.89 us -> 0 us
    psum x1 -> x0, waiting for transfers between devices: 93.4 us -> none  [local(): big, flat = lax.psum((big, flat), ('replica', 'group'))]
    pallas_call x3 -> x5, Pallas kernels: 137 us -> 224 us  [the longest x1 57.8 us: middle_part(): pl.pallas_call(functools.partial(mlp_both, length, pitch, count, 256), gr...]
    psum x1 -> x0, blocking collectives: 40.2 us -> none  [local(): big, flat = lax.psum((big, flat), ('replica', 'group'))]
    all_gather x3 -> x0, blocking collectives: 33.5 us -> none  [the longest x2 28.2 us: gather(): return lax.all_gather(piece, 'group', axis=0, tiled=True)]
    dynamic_slice x13 -> x0, local copies, waits for them, and re-layouts: 9.88 us -> none  [rows(): lax.dynamic_slice_in_dim(block, position * (block.shape[0] // members), b...]
    concatenate x1 -> x0, local copies, waits for them, and re-layouts: 6.1 us -> none  [local(): jnp.concatenate([gain_one, shift_one, b_query, b_value, b_proj, gain_two,...]
    unnamed x17 -> x0, local copies, waits for them, and re-layouts: 3.8 us -> none
  transfers between devices with their start and end apart: 3 -> 0, of which waited for: 1 -> 0; matrix products, arithmetic and copies ran while one was open for 4% -> 0% of each run, Pallas kernels for 11% -> 0%
where the time goes in v2:
time: 225 us
  Pallas kernels  224 us (100%)
    pallas_call x1, Pallas kernels, middle_part(): pl.pallas_call(functools.partial(mlp_both, length, pitch, count, 256), gr...  57.8 us
    pallas_call x1, Pallas kernels, backward_part(): pl.pallas_call(functools.partial(attention_backward, length, pitch, count...  57.4 us
    pallas_call x1, Pallas kernels, reduce_part(): pl.pallas_call(reduce_all, in_specs=[vmem] * 3, out_specs=[vmem] * 3, out...  57.1 us
    pallas_call x1, Pallas kernels, forward_part(): pl.pallas_call(functools.partial(attention_forward, length, pitch, count,...  48.5 us

profile of v2, /device:TPU:0, one launch (start us, length us, event | category | flops | bytes accessed | tf_op | source)
XLA Modules:
  0.0 225.2 jit_solution(7160198679640619958)
XLA Ops:
  0.7 48.5 %attention_forward.1 = (bf16[20,208,1152]{2,1,0:T(8,128)(2,1)}, bf16[20,6,208,208]{3,2,1,0:T(8,128)(2,1)}, bf16[20,208,384]{2,1,0:T(8,128)(2,1)}, bf16[384,1152]...) custom-call(bf16[20,197,384]{2,1,0:T(8,128)(2,1)} %x_ref.5, ...), custom_call_target="tpu_custom_call" | custom-call | tf_op jit(solution)/shard_map/attention_forward/pallas_call | solution.py:654
  49.1 57.8 %mlp_both.1 = (bf16[20,197,384]{2,1,0:T(8,128)(2,1)}, f32[20,208,384]{2,1,0:T(8,128)}, bf16[20,208,384]{2,1,0:T(8,128)(2,1)}, bf16[6,2,768,128]{3,2,1,0:T(8,128)...) custom-call(bf16[20,197,384]{2,1,0:T(8,128)(2,1)} %x_ref.5, bf16[20,197,384]{2,1,0:T(8,128)(2,1)} %ct_ref.1, ...), custom_call_target="tpu_custom_call" | custom-call | tf_op jit(solution)/shard_map/mlp_both/pallas_call | solution.py:686
  106.9 57.4 %attention_backward.1 = (f32[20,197,384]{2,1,0:T(8,128)}, bf16[3,2,768,128]{3,2,1,0:T(8,128)(2,1)}, f32[16,384]{1,0:T(8,128)}) custom-call(bf16[20,197,384]{2,1,0:T(8,128)(2,1)} %x_ref.5, f32[20,208,384]{2,1,0:T(8,128)} %get-tuple-element.56.gr_ref, bf16[20,208,384]{2,1,0:T(8,128)(2,1)} %get-tuple-element.57.ga_ref, ...), custom_call_target="tpu_custom_call" | custom-call | tf_op jit(solution)/shard_map/attention_backward/pallas_call | solution.py:740
  164.3 57.1 %reduce_all.1 = (bf16[6,768,128]{2,1,0:T(8,128)(2,1)}, bf16[3,768,128]{2,1,0:T(8,128)(2,1)}, f32[16,384]{1,0:T(8,128)}) custom-call(bf16[6,2,768,128]{3,2,1,0:T(8,128)(2,1)} %get-tuple-element.64.a_ref, bf16[3,2,768,128]{3,2,1,0:T(8,128)(2,1)} %get-tuple-element.65.b_ref, f32[16,384]{1,0:T(8,128)} %get-tuple-element.66.vec_ref), custom_call_target="tpu_custom_call" | custom-call | tf_op jit(solution)/shard_map/reduce_all/pallas_call | solution.py:771
  221.4 3.6 %unpack.1 = (f32[192]{0:T(256)}, f32[192]{0:T(256)}, f32[192,1152]{1,0:T(8,128)}, f32[192]{0:T(256)}, f32[192]{0:T(256)}, /*index=5*/f32[192,384]{1,0:T(8,128)},...) custom-call(bf16[6,768,128]{2,1,0:T(8,128)(2,1)} %get-tuple-element., ...), custom_call_target="tpu_custom_call" | custom-call | tf_op jit(solution)/shard_map/unpack/pallas_call | solution.py:805

commit v3 on v2

--- a/solution.py
+++ b/solution.py
@@ -276,14 +276,105 @@
             dvec_ref[8 + k : 9 + k, :] = accb[0:1, k * width : (k + 1) * width]
 
 
+def phases_of(heads):
+    return heads // 2
+
+
+def schedule(total, steps):
+    plan = {}
+
+    def put(at, *work):
+        plan.setdefault(at if at < total else -1, []).append(work)
+
+    def chain(name, starts):
+        for k, at in enumerate(starts):
+            put(at, name, ORDER[k - 1] if k else None, ORDER[k] if k < len(ORDER) else None)
+
+    plan[0] = [("greet", None, None)]
+    chain("a", (0, 1, 4, 6, 8, 10, 12, 14))
+    chain("b", (0, 3, 7, 9, 11, 13, 15, 16))
+    chain(0, (steps, 7, 9, 10, 12, 13, 14, 15))
+    chain(1, (2 * steps, 11, 13, 14, 15, 16, 17, 18))
+    chain(2, (3 * steps, 16, 17, 18, 19, total, total, total))
+    return plan
+
+
+ORDER = (0, 1, 2, 3, 5, 6, 7)
+
+
+class Ticks:
+    def __init__(self, parts, vectors, vec_out, flushes, vec_flush):
+        self.parts, self.vectors, self.vec_out, self.flushes, self.vec_flush = parts, vectors, vec_out, flushes, vec_flush
+
+    def run(self, work):
+        for name, done, start in work:
+            if name == "greet":
+                greet(self.parts["a"].partners())
+                continue
+            part = self.parts[name]
+            if done is not None:
+                self.finish(name, part, done)
+            if start is not None:
+                part.start(start)
+
+    def finish(self, name, part, done):
+        part.finish(done)
+        if done == 3 and part.extra > 1:
+            part.start(4)
+            part.finish(4)
+        if done == ORDER[-1]:
+            self.flushes[name].start()
+
+    def close(self, work):
+        vectors, pending = self.vectors, list(work)
+        vectors.start(0)
+        for stage in range(5):
+            if pending:
+                self.run([pending.pop(0)])
+            vectors.finish(stage, self.vec_out)
+            if stage < 4:
+                vectors.start(stage + 1)
+        self.run(pending)
+        self.vec_flush.start()
+        for copy in list(self.flushes.values()) + [self.vec_flush]:
+            copy.wait()
+
+
+def make_ticks(fc_ref, unit_ref, dvec_ref, fc_out, qkv_out, vec_out, fc_hbm, qkv_hbm, vec_hbm, flush_sem, scratch):
+    three = fc_ref.shape[0] // 2
+    pairs = unit_ref.shape[0]
+    sources = {"a": (fc_ref, fc_out, fc_hbm, 0, three), "b": (fc_ref, fc_out, fc_hbm, three, three)}
+    for k in range(pairs):
+        sources[k] = (unit_ref, qkv_out, qkv_hbm, k, 1)
+    parts, flushes = {}, {}
+    for k, (name, (source, out, hbm, at, size)) in enumerate(sources.items()):
+        refs = scratch[k * REDUCE_REFS : (k + 1) * REDUCE_REFS]
+        mine = pl.ds(at, size)
+        parts[name] = Reduce(source.at[mine], refs[:8], out.at[mine], refs[8], refs[9])
+        flushes[name] = pltpu.make_async_copy(out.at[mine], hbm.at[mine], flush_sem.at[k])
+    vectors = ReduceVectors(parts["a"], *scratch[len(sources) * REDUCE_REFS :], first=dvec_ref)
+    vec_flush = pltpu.make_async_copy(vec_out, vec_hbm, flush_sem.at[len(sources)])
+    return Ticks(parts, vectors, vec_out, flushes, vec_flush)
+
+
 def attention_backward(
-    length, pitch, count,
-    x_ref, gr_ref, ga_ref, q_ref, k_ref, v_ref, probs_ref, wq_ref, vec_ref, strip_ref, dvec_in,
-    gx_ref, unit_ref, dvec_ref,
-    pad_ref, hid_ref, gp_ref, acc, accv,
+    length, pitch, count, steps,
+    x_ref, gr_ref, ga_ref, q_ref, k_ref, v_ref, probs_ref, wq_ref, vec_ref, strip_ref, dvec_in, fc_ref,
+    gx_ref, fc_hbm, qkv_hbm, vec_hbm,
+    pad_ref, hid_ref, gp_ref, acc, accv, unit_ref, dvec_ref, fc_out, qkv_out, vec_out, flush_sem, *scratch,
 ):
     phase, block = pl.program_id(0), pl.program_id(1)
     phases, blocks_ = pl.num_programs(0), pl.num_programs(1)
+    step = phase * blocks_ + block
+    ticks = make_ticks(
+        fc_ref, unit_ref, dvec_ref, fc_out, qkv_out, vec_out, fc_hbm, qkv_hbm, vec_hbm, flush_sem, scratch
+    )
+    plan = schedule((phases_of(HEADS) + 1) * steps, steps)
+    for at, work in plan.items():
+        if at >= 0:
+            @pl.when(step == at)
+            def _(work=work):
+                ticks.run(work)
     width = x_ref.shape[2]
     head_dim = width // HEADS
     pair = 2 * head_dim
@@ -388,6 +479,10 @@
         for image in range(count):
             gx_ref[image] = grad_x[image * pitch : image * pitch + length]
 
+        @pl.when(block == blocks_ - 1)
+        def _():
+            ticks.close(plan.get(-1, []))
+
 
 class Reduce:
     STAGES = 8
@@ -510,10 +605,10 @@
 
 
 class ReduceVectors:
-    def __init__(self, like, v1, v2, v3, slots_z, slots_e, got, sends, recvs):
+    def __init__(self, like, v2, v3, slots_z, slots_e, got, sends, recvs, first):
         self.like = like
         self.vals, self.slots_z, self.slots_e, self.got, self.sends, self.recvs = (
-            (v1, v2, v3), slots_z, slots_e, got, sends, recvs
+            (first, v2, v3), slots_z, slots_e, got, sends, recvs
         )
 
     def copies(self, stage):
@@ -560,42 +655,13 @@
     extra = max(replicas // 16, 1)
     hops = max(4, extra)
     return [
-        pltpu.VMEM(shape, F32), pltpu.VMEM(shape, F32), pltpu.VMEM(shape, F32),
+        pltpu.VMEM(shape, F32), pltpu.VMEM(shape, F32),
         pltpu.VMEM((4,) + shape, F32), pltpu.VMEM((extra,) + shape, F32), pltpu.VMEM((3,) + shape, F32),
         pltpu.SemaphoreType.DMA((5, hops)), pltpu.SemaphoreType.DMA((5, hops)),
     ]
 
 
 REDUCE_REFS = 10
-
-
-def reduce_all(a_ref, b_ref, vec_ref, a_out, b_out, vec_out, *scratch):
-    parts = []
-    half = a_ref.shape[0] // 2
-    groups = [(a_ref.at[0:half], a_out.at[0:half]), (a_ref.at[half:], a_out.at[half:]), (b_ref, b_out)]
-    for k, (source, out) in enumerate(groups):
-        refs = scratch[k * REDUCE_REFS : (k + 1) * REDUCE_REFS]
-        parts.append(Reduce(source, refs[:8], out, refs[8], refs[9]))
-    refs = scratch[3 * REDUCE_REFS :]
-    vectors = ReduceVectors(parts[0], *refs)
-    refs[0][...] = vec_ref[...]
-    greet(parts[0].partners())
-    vectors.start(0)
-    for part in parts[:1]:
-        part.start(0)
-    for tick in range(Reduce.STAGES + 2):
-        if tick < 2:
-            parts[tick + 1].start(0)
-        for k in range(3):
-            stage = tick - k
-            if 0 <= stage < Reduce.STAGES:
-                parts[k].finish(stage)
-                if stage + 1 < Reduce.STAGES:
-                    parts[k].start(stage + 1)
-        if tick < 5:
-            vectors.finish(tick, vec_out)
-            if tick < 4:
-                vectors.start(tick + 1)
 
 
 def unpack(factor, fc_ref, qkv_ref, vec_ref, g1, s1, wq, bq, bv, wp, bp, g2, s2, w1, b1, w2, b2):
@@ -708,14 +774,20 @@
     )(inputs, cotangent, attended, w_proj, w_fc1, w_fc2, vecs, bias_fc1)
 
 
-def backward_part(inputs, grad_resid, grad_att, packed, probs, w_qkv, vecs, strips, dvec, pitch):
+def backward_part(inputs, grad_resid, grad_att, packed, probs, w_qkv, vecs, strips, dvec, fc_units, pitch, replicas):
     images, length, width = inputs.shape
     count = 4
     rows = count * pitch
     steps = images // count
     pairs = HEADS // 2
     pair = width // pairs
-    unit = (pairs, 2, QUAD * width // 2, LANES)
+    unit_rows = QUAD * width // 2
+    unit = (pairs, 2, unit_rows, LANES)
+    fc_sum, qkv_sum = (fc_units.shape[0], unit_rows, LANES), (pairs, unit_rows, LANES)
+    scratch = []
+    for units in (fc_units.shape[0] // 2,) * 2 + (1,) * pairs:
+        scratch += reduce_scratch(units, unit_rows, replicas)
+    scratch += vector_scratch(dvec.shape, replicas)
 
     def edge(p, i):
         return jnp.where(jnp.logical_or(p == 0, p == pairs), i, steps - 1)
@@ -738,47 +810,27 @@
         return at, col, 0, 0
 
     return pl.pallas_call(
-        functools.partial(attention_backward, length, pitch, count),
+        functools.partial(attention_backward, length, pitch, count, steps),
         grid=(pairs + 1, steps),
         in_specs=[
             pl.BlockSpec((count, length, width), lambda p, i: (edge(p, i), 0, 0)),
             pl.BlockSpec((count, pitch, width), lambda p, i: (tail(p, i), 0, 0)),
             part(0), part(0), part(1), part(2),
             pl.BlockSpec((count, 2, pitch, pitch), probs_at),
-            whole(w_qkv), whole(vecs), whole(strips), whole(dvec),
+            whole(w_qkv), whole(vecs), whole(strips), whole(dvec), whole(fc_units),
         ],
-        out_specs=[
-            pl.BlockSpec((count, length, width), lambda p, i: (tail(p, i), 0, 0)), fixed(*unit), fixed(16, width),
-        ],
-        out_shape=[sds((images, length, width), F32), sds(unit, BF), sds((16, width), F32)],
+        out_specs=[pl.BlockSpec((count, length, width), lambda p, i: (tail(p, i), 0, 0)), HBM, HBM, HBM],
+        out_shape=[sds((images, length, width), F32), sds(fc_sum, BF), sds(qkv_sum, BF), sds(dvec.shape, F32)],
         scratch_shapes=[
             pltpu.VMEM((rows, width), BF), pltpu.VMEM((images * pitch, width), BF),
             pltpu.VMEM((pairs, images * pitch, 3 * pair), BF), pltpu.VMEM((width, 3 * pair), F32),
-            pltpu.VMEM((pairs, 8, pair), F32),
-        ],
-        compiler_params=params(2),
+            pltpu.VMEM((pairs, 8, pair), F32), pltpu.VMEM(unit, BF), pltpu.VMEM(dvec.shape, F32),
+            pltpu.VMEM(fc_sum, BF), pltpu.VMEM(qkv_sum, BF), pltpu.VMEM(dvec.shape, F32),
+            pltpu.SemaphoreType.DMA((pairs + 3,)),
+        ] + scratch,
+        compiler_params=params(2, collective_id=1, has_side_effects=True),
         name="attention_backward",
-    )(inputs, grad_resid, grad_att, packed, packed, packed, probs, w_qkv, vecs, strips, dvec)
-
-
-def reduce_part(fc_units, qkv_units, dvec, replicas):
-    vmem = pl.BlockSpec(memory_space=pltpu.VMEM)
-    three, rows = fc_units.shape[0] // 2, fc_units.shape[2]
-    scratch = []
-    for units in (three, three, qkv_units.shape[0]):
-        scratch += reduce_scratch(units, rows, replicas)
-    scratch += vector_scratch(dvec.shape, replicas)
-    return pl.pallas_call(
-        reduce_all,
-        in_specs=[vmem] * 3,
-        out_specs=[vmem] * 3,
-        out_shape=[
-            sds((fc_units.shape[0], rows, LANES), BF), sds((qkv_units.shape[0], rows, LANES), BF), sds(dvec.shape, F32),
-        ],
-        scratch_shapes=scratch,
-        compiler_params=pltpu.CompilerParams(vmem_limit_bytes=VMEM_LIMIT, collective_id=1, has_side_effects=True),
-        name="reduce_all",
-    )(fc_units, qkv_units, dvec)
+    )(inputs, grad_resid, grad_att, packed, packed, packed, probs, w_qkv, vecs, strips, dvec, fc_units)
 
 
 def local(
@@ -796,10 +848,9 @@
     outputs, grad_resid, grad_att, fc_units, strips, dvec = middle_part(
         inputs, cotangent, attended, wp, w1, w2, vecs, bias_fc1, pitch
     )
-    grad_inputs, qkv_units, dvec = backward_part(
-        inputs, grad_resid, grad_att, packed, probs, wq, vecs, strips, dvec, pitch
+    grad_inputs, fc_sum, qkv_sum, vec_sum = backward_part(
+        inputs, grad_resid, grad_att, packed, probs, wq, vecs, strips, dvec, fc_units, pitch, replicas
     )
-    fc_sum, qkv_sum, vec_sum = reduce_part(fc_units, qkv_units, dvec, replicas)
     factor = float(images * length * replicas * members) ** (-0.5)
     weights = (gain_one, shift_one, w_qkv, b_query, b_value, w_proj, b_proj, gain_two, shift_two, w_fc1, b_fc1, w_fc2, b_fc2)
     grads = pl.pallas_call(

time: 225 us -> 209 us (0.929)
  Pallas kernels: 224 us -> 202 us
  local copies, waits for them, and re-layouts: 0 us -> 5.79 us
    pallas_call x1 -> x0, Pallas kernels: 57.1 us -> none  [reduce_part(): pl.pallas_call(reduce_all, in_specs=[vmem] * 3, out_specs=[vmem] * 3, out...]
    pallas_call x1, Pallas kernels: 57.4 us -> 92.1 us  [backward_part(): pl.pallas_call(functools.partial(attention_backward, length, pitch, count...]
    unnamed x0 -> x1, local copies, waits for them, and re-layouts: none -> 5.79 us
where the time goes in v3:
time: 209 us; the launch traced here: 208 us
  Pallas kernels  202 us (97%)
  local copies, waits for them, and re-layouts  5.79 us (3%)
    pallas_call x1, Pallas kernels, backward_part(): pl.pallas_call(functools.partial(attention_backward, length, pitch, count...  92.1 us
    pallas_call x1, Pallas kernels, middle_part(): pl.pallas_call(functools.partial(mlp_both, length, pitch, count, 256), gr...  57.8 us
    pallas_call x1, Pallas kernels, forward_part(): pl.pallas_call(functools.partial(attention_forward, length, pitch, count,...  48.5 us
    unnamed x1, local copies, waits for them, and re-layouts  5.79 us

profile of v3, /device:TPU:0, one launch (start us, length us, event | category | flops | bytes accessed | tf_op | source)
XLA Modules:
  0.0 208.5 jit_solution(33075029377194572)
XLA Ops:
  0.7 48.5 %attention_forward.1 = (bf16[20,208,1152]{2,1,0:T(8,128)(2,1)}, bf16[20,6,208,208]{3,2,1,0:T(8,128)(2,1)}, bf16[20,208,384]{2,1,0:T(8,128)(2,1)}, bf16[384,1152]...) custom-call(bf16[20,197,384]{2,1,0:T(8,128)(2,1)} %x_ref.5, ...), custom_call_target="tpu_custom_call" | custom-call | tf_op jit(solution)/shard_map/attention_forward/pallas_call | solution.py:720
  49.1 57.8 %mlp_both.1 = (bf16[20,197,384]{2,1,0:T(8,128)(2,1)}, f32[20,208,384]{2,1,0:T(8,128)}, bf16[20,208,384]{2,1,0:T(8,128)(2,1)}, bf16[6,2,768,128]{3,2,1,0:T(8,128)...) custom-call(bf16[20,197,384]{2,1,0:T(8,128)(2,1)} %x_ref.5, bf16[20,197,384]{2,1,0:T(8,128)(2,1)} %ct_ref.1, ...), custom_call_target="tpu_custom_call" | custom-call | tf_op jit(solution)/shard_map/mlp_both/pallas_call | solution.py:752
  106.9 92.1 %attention_backward.1 = (f32[20,197,384]{2,1,0:T(8,128)}, bf16[6,768,128]{2,1,0:T(8,128)(2,1)}, bf16[3,768,128]{2,1,0:T(8,128)(2,1)}, f32[16,384]{1,0:T(8,128)}) custom-call(bf16[20,197,384]{2,1,0:T(8,128)(2,1)} %x_ref.5, f32[20,208,384]{2,1,0:T(8,128)} %get-tuple-element.54.gr_ref, bf16[20,208,384]{2,1,0:T(8,128)(2,1)} %get-tuple-element.55.ga_ref, ...), custom_call_target="tpu_custom_call" | custom-call | tf_op jit(solution)/shard_map/attention_backward/pallas_call | solution.py:812
  199.1 3.6 %unpack.1 = (f32[192]{0:T(256)}, f32[192]{0:T(256)}, f32[192,1152]{1,0:T(8,128)}, f32[192]{0:T(256)}, f32[192]{0:T(256)}, /*index=5*/f32[192,384]{1,0:T(8,128)},...) custom-call(bf16[6,768,128]{2,1,0:T(8,128)(2,1)} %get-tuple-element., ...), custom_call_target="tpu_custom_call" | custom-call | tf_op jit(solution)/shard_map/unpack/pallas_call | solution.py:856
  202.7 5.8 %copy.31 = f32[20,197,384]{2,1,0:T(8,128)} copy(f32[20,197,384]{2,1,0:T(8,128)} %get-tuple-element.95) | data formatting | bytes 12103680

commit v4 on v3

--- a/solution.py
+++ b/solution.py
@@ -84,17 +84,23 @@
             )
 
 
+def pipeline(items, *stages):
+    for tick in range(len(items) + len(stages) - 1):
+        for late, stage in enumerate(stages):
+            if 0 <= tick - late < len(items):
+                stage(items[tick - late])
+
+
 def attention_forward(
     length, pitch, count, late,
     x_ref, wq_hbm, wp_hbm, w1_hbm, w2_hbm, g1, s1, bq, bv, bp, g2, s2, b2, b1,
-    packed_ref, probs_ref, att_ref, wq_out, wp_out, w1_out, w2_out, vec_out, b1_out,
-    pad_ref, wq, wp, w1, w2, small, wide, vec, bias, b1_full,
+    qt_ref, kt_ref, v_ref, exp_ref, inv_ref, att_ref, wq_out, wp_out, w1_out, w2_out, vec_out, b1_out,
+    pad_ref, wq, wp, w1, w2, small, wide, vec, b1_full, wqt, bias_q, k_ref,
     sends, recvs, passes, arrivals, vec_send, vec_recv, own_sem, out_sem,
 ):
     step = pl.program_id(0)
     width = x_ref.shape[2]
     head_dim = width // HEADS
-    pair = 2 * head_dim
     factor = head_dim ** (-0.5) * LOG2E
     shards = (wq_hbm, wp_hbm, w1_hbm, w2_hbm)
     wholes = (wq, wp, w1, w2)
@@ -129,14 +135,13 @@
         small_copy.wait()
         for side in range(2):
             vec[:, side * share : (side + 1) * share] = small[side, :, 0:share]
-        bias[0:1, 0:width] = vec[2:3, :]
-        bias[0:1, width : 2 * width] = jnp.zeros((1, width), F32)
-        bias[0:1, 2 * width : 3 * width] = vec[3:4, :]
         vec_out[...] = vec[...]
+        bias_q[...] = jnp.broadcast_to(vec[...].T[:, 2:3], bias_q.shape)
         move.first[0].wait()
         move.second[0].start()
         owns[0].wait()
         move.second[0].wait()
+        wqt[...] = wq[:, 0:width].T
 
     @pl.when(step == late)
     def _():
@@ -150,7 +155,7 @@
         for k in range(1, 4):
             owns[k].wait()
 
-    @pl.when(step == late + 2)
+    @pl.when(step == late + 1)
     def _():
         for k in range(1, 4):
             move.second[k].wait()
@@ -163,33 +168,51 @@
         pad_ref[image * pitch : image * pitch + length, :] = x_ref[image]
     normed, _ = row_stats(pad_ref[...].astype(F32))
     hidden = (normed * gain + shift).astype(BF)
-    packed = (dot(hidden, wq[...]) + bias[0:1, :]).astype(BF)
+    keys_all = dot(hidden, wq[:, width : 2 * width]).astype(BF)
+    values_all = (dot(hidden, wq[:, 2 * width :]) + vec[3:4, :]).astype(BF)
     for image in range(count):
-        packed_ref[image] = packed[image * pitch : (image + 1) * pitch]
-    lane = lax.broadcasted_iota(jnp.int32, (pitch, pair), 1)
+        rows = slice(image * pitch, (image + 1) * pitch)
+        k_ref[image] = keys_all[rows]
+        v_ref[image] = values_all[rows]
+        qt_ref[image] = ((dot_rt(wqt[...], hidden[rows]) + bias_q[...]) * factor).astype(BF)
     tail = length // 8 * 8
     row = lax.broadcasted_iota(jnp.int32, (pitch - tail, pitch), 0) + tail
-    for image in range(count):
-        for two in range(HEADS // 2):
-            cols = slice(two * pair, (two + 1) * pair)
-            query = packed_ref[image, :, two * pair : (two + 1) * pair]
-            keys = packed_ref[image, :, width + two * pair : width + (two + 1) * pair]
-            values = packed_ref[image, :, 2 * width + two * pair : 2 * width + (two + 1) * pair]
-            values_t = values.T
-            parts = []
-            for side in range(2):
-                own = (lane < head_dim) if side == 0 else (lane >= head_dim)
-                scores = dot_rt(keys, jnp.where(own, query, jnp.zeros_like(query)))
-                low = jnp.where(row < length, scores[tail:], -1e30)
-                scores = jnp.concatenate([scores[:tail], low], axis=0)
-                top = jnp.max(scores, axis=0, keepdims=True)
-                raised = jnp.exp2((scores - top) * factor)
-                total = jnp.sum(raised, axis=0, keepdims=True)
-                probs = (raised * (1.0 / total)).astype(BF)
-                probs_ref[image, 2 * two + side] = probs
-                parts.append(dot(values_t[side * head_dim : (side + 1) * head_dim], probs))
-            mixed = jnp.concatenate(parts, axis=0)
-            att_ref[image, :, cols] = mixed.T.astype(BF)
+    zero = jnp.zeros((head_dim, pitch), BF)
+    ones = jnp.ones((16, pitch), BF)
+    kept = {}
+
+    def score(item):
+        image, two, side = item
+        cols = slice(two * LANES, (two + 1) * LANES)
+        if side == 0:
+            kt_ref[image, cols, :] = k_ref[image, :, cols].T
+            kept["vt", image, two] = v_ref[image, :, cols].T
+        at = two * LANES + side * head_dim
+        own = qt_ref[image, at : at + head_dim, :]
+        full = jnp.concatenate([own, zero] if side == 0 else [zero, own], axis=0)
+        kept[item] = dot(k_ref[image, :, cols], full)
+
+    def soften(item):
+        image, two, side = item
+        scores = kept.pop(item)
+        low = jnp.where(row < length, scores[tail:], -1e30)
+        scores = jnp.concatenate([scores[:tail], low], axis=0)
+        top = jnp.max(scores, axis=0, keepdims=True)
+        raised = jnp.exp2(scores - top).astype(BF)
+        exp_ref[image, 2 * two + side] = raised
+        kept[item] = raised
+
+    def mix(item):
+        image, two, side = item
+        own = kept["vt", image, two][side * head_dim : (side + 1) * head_dim]
+        mixed = dot(jnp.concatenate([own, ones], axis=0), kept.pop(item))
+        inverse = 1.0 / mixed[head_dim : head_dim + 1]
+        at = two * LANES + side * head_dim
+        inv_ref[image, 2 * two + side : 2 * two + side + 1, :] = inverse
+        att_ref[image, at : at + head_dim, :] = (mixed[:head_dim] * inverse).astype(BF)
+
+    items = [(image, two, side) for image in range(count) for two in range(HEADS // 2) for side in range(2)]
+    pipeline(items, score, soften, mix)
 
     @pl.when(step == last)
     def _():
@@ -207,7 +230,7 @@
     length, pitch, count, chunk,
     x_ref, ct_ref, att_ref, wp_ref, w1_ref, w2_ref, vec_ref, b1_ref,
     y_ref, gr_ref, ga_ref, unit_ref, strip_ref, dvec_ref,
-    xpad, ctpad, act_ref, gp_ref, acc1, acc2, accp, accv, accb,
+    xpad, ctpad, att_s, act_ref, gp_ref, w2t, acc1, acc2, accp, accv, accb,
 ):
     step = pl.program_id(0)
     width = x_ref.shape[2]
@@ -217,8 +240,10 @@
     def _():
         for ref in (xpad, ctpad, acc1, acc2, accp, accv, accb):
             ref[...] = jnp.zeros_like(ref)
+        w2t[...] = w2_ref[...].T
 
     for image in range(count):
+        att_s[image * pitch : (image + 1) * pitch, :] = att_ref[image].T
         xpad[image * pitch : image * pitch + length, :] = x_ref[image]
         ctpad[image * pitch : image * pitch + length, :] = ct_ref[image]
     bias_p = vec_ref[4:5, :]
@@ -226,7 +251,7 @@
     shift = vec_ref[6:7, :]
     bias_2 = vec_ref[7:8, :]
     ct = ctpad[...]
-    att = att_ref[...].reshape(count * pitch, width)
+    att = att_s[...]
     resid = xpad[...].astype(F32) + dot(att, wp_ref[...]) + bias_p
     normed, inverse = row_stats(resid)
     hidden = (normed * gain + shift).astype(BF)
@@ -238,19 +263,21 @@
         grad_pre = dot_rt(ct, w2_ref[cols, :]) * slope
         accb[0:1, cols] += col_sum(grad_pre)
         gp_ref[:, cols] = grad_pre.astype(BF)
-    out = resid + dot(act_ref[...], w2_ref[...]) + bias_2
+    out = resid + dot_rt(w2t[...], act_ref[...]).T + bias_2
     for image in range(count):
         y_ref[image] = out[image * pitch : image * pitch + length].astype(BF)
-    grad_hidden = dot_rt(gp_ref[...], w1_ref[...])
+    grad_hidden = dot_rt(w1_ref[...], gp_ref[...]).T
     top = ct.astype(F32)
     grad_resid = top + norm_back(grad_hidden, normed, inverse, gain)
     accv[0:1, :] += col_sum(grad_resid)
     accv[1:2, :] += col_sum(grad_hidden * normed)
     accv[2:3, :] += col_sum(grad_hidden)
     accv[3:4, :] += col_sum(top)
-    gr_ref[...] = grad_resid.reshape(gr_ref.shape)
     grad_resid_b = grad_resid.astype(BF)
-    ga_ref[...] = dot_rt(grad_resid_b, wp_ref[...]).astype(BF).reshape(ga_ref.shape)
+    for image in range(count):
+        rows = slice(image * pitch, (image + 1) * pitch)
+        gr_ref[image] = grad_resid[rows]
+        ga_ref[image] = dot_rt(wp_ref[...], grad_resid_b[rows]).astype(BF)
     acc1[...] += dot_lt(hidden, gp_ref[...])
     acc2[...] += dot_lt(ct, act_ref[...])
     accp[...] += dot_lt(att, grad_resid_b)
@@ -359,9 +386,9 @@
 
 def attention_backward(
     length, pitch, count, steps,
-    x_ref, gr_ref, ga_ref, q_ref, k_ref, v_ref, probs_ref, wq_ref, vec_ref, strip_ref, dvec_in, fc_ref,
+    x_ref, gr_ref, ga_ref, qt_ref, kt_ref, v_ref, exp_ref, inv_ref, wq_ref, vec_ref, strip_ref, dvec_in, fc_ref,
     gx_ref, fc_hbm, qkv_hbm, vec_hbm,
-    pad_ref, hid_ref, gp_ref, acc, accv, unit_ref, dvec_ref, fc_out, qkv_out, vec_out, flush_sem, *scratch,
+    pad_ref, hid_ref, gp_ref, wperm, acc, accv, unit_ref, dvec_ref, fc_out, qkv_out, vec_out, flush_sem, *scratch,
 ):
     phase, block = pl.program_id(0), pl.program_id(1)
     phases, blocks_ = pl.num_programs(0), pl.num_programs(1)
@@ -380,14 +407,17 @@
     pair = 2 * head_dim
     factor = head_dim ** (-0.5)
     rows = count * pitch
-    here = pl.ds(pl.multiple_of(block * rows, rows), rows)
+    first = block * count
     gain = vec_ref[0:1, :]
     shift = vec_ref[1:2, :]
 
     @pl.when(jnp.logical_and(phase == 0, block == 0))
     def _():
         pad_ref[...] = jnp.zeros_like(pad_ref)
-        accv[...] = jnp.zeros_like(accv)
+        for two in range(HEADS // 2):
+            for third in range(3):
+                to, at = (3 * two + third) * pair, third * width + two * pair
+                wperm[:, to : to + pair] = wq_ref[:, at : at + pair]
 
     def stats():
         for image in range(count):
@@ -397,7 +427,10 @@
     @pl.when(phase == 0)
     def _():
         normed, _ = stats()
-        hid_ref[here, :] = (normed * gain + shift).astype(BF)
+        hidden = (normed * gain + shift).astype(BF)
+        for image in range(count):
+            hid_ref[first + image, 0:width, :] = hidden[image * pitch : (image + 1) * pitch].T
+            hid_ref[first + image, width:, :] = jnp.ones((16, pitch), BF)
 
     @pl.when(phase < phases - 1)
     def _():
@@ -405,45 +438,42 @@
         def _():
             acc[...] = jnp.zeros_like(acc)
 
-        lane = lax.broadcasted_iota(jnp.int32, (pitch, pair), 1)
-        sum_q = jnp.zeros((1, pair), F32)
-        sum_v = jnp.zeros((1, pair), F32)
-        pieces = []
-        for image in range(count):
-            query = q_ref[image]
-            keys = k_ref[image]
-            values = v_ref[image]
-            grad_out = ga_ref[image]
-            keys_t = keys.T
-            grad_values = None
-            grad_keys = None
-            parts = []
-            for side in range(2):
-                own = (lane < head_dim) if side == 0 else (lane >= head_dim)
-                zero = jnp.zeros_like(query)
-                grad_side = jnp.where(own, grad_out, zero)
-                probs_b = probs_ref[image, side]
-                probs = probs_b.astype(F32)
-                grad_probs = dot_rt(values, grad_side)
-                delta = jnp.sum(probs * grad_probs, axis=0, keepdims=True)
-                grad_scores = (probs * (grad_probs - delta)).astype(BF)
-                piece_v = dot(probs_b, grad_side)
-                piece_k = dot(grad_scores, jnp.where(own, query, zero))
-                grad_values = piece_v if grad_values is None else grad_values + piece_v
-                grad_keys = piece_k if grad_keys is None else grad_keys + piece_k
-                parts.append(dot(keys_t[side * head_dim : (side + 1) * head_dim], grad_scores))
-            grad_query = jnp.concatenate(parts, axis=0).T * factor
-            grad_keys = grad_keys * factor
-            sum_q += col_sum(grad_query)
-            sum_v += col_sum(grad_values)
-            pieces.append(
-                jnp.concatenate([grad_query.astype(BF), grad_keys.astype(BF), grad_values.astype(BF)], axis=1)
-            )
-        grad_pair = jnp.concatenate(pieces, axis=0)
-        gp_ref[phase, here, :] = grad_pair
-        accv[phase, 0:1, :] += sum_q
-        accv[phase, 1:2, :] += sum_v
-        acc[...] += dot_lt(hid_ref[here, :], grad_pair)
+        zero = jnp.zeros((head_dim, pitch), BF)
+        kept = {}
+
+        def probe(item):
+            image, side = item
+            own = slice(side * head_dim, (side + 1) * head_dim)
+            inverse = inv_ref[image, pl.ds(2 * phase + side, 1), :]
+            grad_out = (ga_ref[image, own, :].astype(F32) * inverse).astype(BF)
+            full = jnp.concatenate([grad_out, zero] if side == 0 else [zero, grad_out], axis=0)
+            kept[item] = (dot(v_ref[image], full), grad_out, inverse)
+
+        def soften(item):
+            image, side = item
+            grad_probs, grad_out, inverse = kept[item]
+            raised = exp_ref[image, side].astype(F32)
+            delta = jnp.sum(raised * grad_probs, axis=0, keepdims=True) * inverse
+            kept[item] = ((raised * (grad_probs - delta)).astype(BF), grad_out)
+
+        def spread(item):
+            image, side = item
+            scores, grad_out = kept.pop(item)
+            own = slice(side * head_dim, (side + 1) * head_dim)
+            grad_q = dot(kt_ref[image, own, :], scores) * factor
+            grad_k = dot_rt(qt_ref[image, own, :], scores) * (1.0 / LOG2E)
+            grad_v = dot_rt(grad_out, exp_ref[image, side])
+            for third, part in enumerate((grad_q, grad_k, grad_v)):
+                at = third * pair + side * head_dim
+                gp_ref[phase, first + image, at : at + head_dim, :] = part.astype(BF)
+
+        def gather(item):
+            image, side = item
+            if side == 1:
+                acc[...] += dot_rt(hid_ref[first + image], gp_ref[phase, first + image])
+
+        items = [(image, side) for image in range(count) for side in range(2)]
+        pipeline(items, probe, soften, spread, gather)
 
         @pl.when(block == blocks_ - 1)
         def _():
@@ -454,6 +484,7 @@
                         side * share : (side + 1) * share, strip * pair : (strip + 1) * pair
                     ].astype(BF)
                 unit_ref[phase, side, 3 * share :, :] = strip_ref[phase, side]
+            accv[phase] = acc[width : width + 8, :]
 
     @pl.when(phase == phases - 1)
     def _():
@@ -461,23 +492,23 @@
         def _():
             dvec_ref[...] = dvec_in[...]
             for two in range(HEADS // 2):
-                dvec_ref[4:6, two * pair : (two + 1) * pair] = accv[two, 0:2, :]
+                cols = slice(two * pair, (two + 1) * pair)
+                dvec_ref[4:5, cols] = accv[two, 0:1, 0:pair]
+                dvec_ref[5:6, cols] = accv[two, 0:1, 2 * pair : 3 * pair]
 
         normed, inverse = stats()
-        grad_hidden = None
-        for two in range(HEADS // 2):
-            for third in range(3):
-                cols = slice(third * width + two * pair, third * width + (two + 1) * pair)
-                piece = (gp_ref[two, here, third * pair : (third + 1) * pair], wq_ref[:, cols])
-                grad_hidden = piece if grad_hidden is None else tuple(
-                    jnp.concatenate([a, b], axis=1) for a, b in zip(grad_hidden, piece)
-                )
-        grad_hidden = dot_rt(*grad_hidden)
-        dvec_ref[6:7, :] += col_sum(grad_hidden * normed)
-        dvec_ref[7:8, :] += col_sum(grad_hidden)
-        grad_x = gr_ref[...].reshape(rows, width) + norm_back(grad_hidden, normed, inverse, gain)
+        sum_n = jnp.zeros((1, width), F32)
+        sum_h = jnp.zeros((1, width), F32)
         for image in range(count):
-            gx_ref[image] = grad_x[image * pitch : image * pitch + length]
+            at = slice(image * pitch, (image + 1) * pitch)
+            packed = jnp.concatenate([gp_ref[two, first + image] for two in range(HEADS // 2)], axis=0)
+            grad_hidden = dot(wperm[...], packed).T
+            sum_n += col_sum(grad_hidden * normed[at])
+            sum_h += col_sum(grad_hidden)
+            grad_x = gr_ref[image] + norm_back(grad_hidden, normed[at], inverse[at], gain)
+            gx_ref[image] = grad_x[:length]
+        dvec_ref[6:7, :] += sum_n
+        dvec_ref[7:8, :] += sum_h
 
         @pl.when(block == blocks_ - 1)
         def _():
@@ -717,20 +748,24 @@
     share, wide = vectors[0].shape[0], vectors[-1].shape[0]
     lanes = (share + LANES - 1) // LANES * LANES
     fulls = [(members * w.shape[0], w.shape[1]) for w in weights]
+    turned = (images, width, pitch)
     return pl.pallas_call(
         functools.partial(attention_forward, length, pitch, count, 5),
         grid=(images // count,),
         in_specs=[blocks(count, length, width)] + [HBM] * 4 + [whole(v) for v in vectors],
         out_specs=[
-            blocks(count, pitch, 3 * width), blocks(count, HEADS, pitch, pitch), blocks(count, pitch, width),
+            blocks(count, width, pitch), blocks(count, width, pitch), blocks(count, pitch, width),
+            blocks(count, HEADS, pitch, pitch), blocks(count, 8, pitch), blocks(count, width, pitch),
             HBM, HBM, HBM, HBM, fixed(8, width), fixed(8, members * wide),
         ],
         out_shape=[
-            sds((images, pitch, 3 * width), BF), sds((images, HEADS, pitch, pitch), BF), sds((images, pitch, width), BF),
+            sds(turned, BF), sds(turned, BF), sds((images, pitch, width), BF),
+            sds((images, HEADS, pitch, pitch), BF), sds((images, 8, pitch), F32), sds(turned, BF),
         ] + [sds(full, BF) for full in fulls] + [sds((8, width), F32), sds((8, members * wide), F32)],
         scratch_shapes=[pltpu.VMEM((count * pitch, width), BF)] + [pltpu.VMEM(full, BF) for full in fulls] + [
             pltpu.VMEM((members, 8, lanes), F32), pltpu.VMEM((members, 8, wide), F32),
-            pltpu.VMEM((8, width), F32), pltpu.VMEM((8, 3 * width), F32), pltpu.VMEM((8, members * wide), F32),
+            pltpu.VMEM((8, width), F32), pltpu.VMEM((8, members * wide), F32),
+            pltpu.VMEM((width, width), BF), pltpu.VMEM((width, pitch), F32), pltpu.VMEM((count, pitch, width), BF),
             pltpu.SemaphoreType.DMA((4,)), pltpu.SemaphoreType.DMA((4,)), pltpu.SemaphoreType.DMA((4,)),
             pltpu.SemaphoreType.DMA((4,)), pltpu.SemaphoreType.DMA((2,)), pltpu.SemaphoreType.DMA((2,)),
             pltpu.SemaphoreType.DMA((4,)), pltpu.SemaphoreType.DMA((4,)),
@@ -743,7 +778,7 @@
 def middle_part(inputs, cotangent, attended, w_proj, w_fc1, w_fc2, vecs, bias_fc1, pitch):
     images, length, width = inputs.shape
     hidden_units = w_fc1.shape[1]
-    count = 2
+    count = 5
     rows = count * pitch
     units = 2 * hidden_units // (QUAD * LANES)
     unit_rows = QUAD * width // 2
@@ -752,20 +787,21 @@
     return pl.pallas_call(
         functools.partial(mlp_both, length, pitch, count, 256),
         grid=(images // count,),
-        in_specs=[blocks(count, length, width), blocks(count, length, width), blocks(count, pitch, width)] + [
+        in_specs=[blocks(count, length, width), blocks(count, length, width), blocks(count, width, pitch)] + [
             whole(w) for w in (w_proj, w_fc1, w_fc2, vecs, bias_fc1)
         ],
         out_specs=[
-            blocks(count, length, width), blocks(count, pitch, width), blocks(count, pitch, width),
+            blocks(count, length, width), blocks(count, pitch, width), blocks(count, width, pitch),
             fixed(*unit), fixed(*strip), fixed(16, width),
         ],
         out_shape=[
-            sds((images, length, width), BF), sds((images, pitch, width), F32), sds((images, pitch, width), BF),
+            sds((images, length, width), BF), sds((images, pitch, width), F32), sds((images, width, pitch), BF),
             sds(unit, BF), sds(strip, BF), sds((16, width), F32),
         ],
         scratch_shapes=[
-            pltpu.VMEM((rows, width), BF), pltpu.VMEM((rows, width), BF),
+            pltpu.VMEM((rows, width), BF), pltpu.VMEM((rows, width), BF), pltpu.VMEM((rows, width), BF),
             pltpu.VMEM((rows, hidden_units), BF), pltpu.VMEM((rows, hidden_units), BF),
+            pltpu.VMEM((width, hidden_units), BF),
             pltpu.VMEM((width, hidden_units), F32), pltpu.VMEM((width, hidden_units), F32),
             pltpu.VMEM((width, width), F32), pltpu.VMEM((8, width), F32), pltpu.VMEM((8, hidden_units), F32),
         ],
@@ -774,7 +810,7 @@
     )(inputs, cotangent, attended, w_proj, w_fc1, w_fc2, vecs, bias_fc1)
 
 
-def backward_part(inputs, grad_resid, grad_att, packed, probs, w_qkv, vecs, strips, dvec, fc_units, pitch, replicas):
+def backward_part(inputs, grad_resid, grad_att, qt, kt, values, raised, inverse, w_qkv, vecs, strips, dvec, fc_units, pitch, replicas):
     images, length, width = inputs.shape
     count = 4
     rows = count * pitch
@@ -798,39 +834,42 @@
     def core(p, i):
         return jnp.where(p == pairs, steps - 1, i), jnp.minimum(p, pairs - 1)
 
-    def part(third):
-        def index(p, i):
-            at, col = core(p, i)
-            return at, 0, third * pairs + col
-
-        return pl.BlockSpec((count, pitch, pair), index)
-
-    def probs_at(p, i):
+    def turned(p, i):
+        at, row = core(p, i)
+        return at, row, 0
+
+    def plain(p, i):
+        at, col = core(p, i)
+        return at, 0, col
+
+    def exp_at(p, i):
         at, col = core(p, i)
         return at, col, 0, 0
 
+    strip = pl.BlockSpec((count, pair, pitch), turned)
     return pl.pallas_call(
         functools.partial(attention_backward, length, pitch, count, steps),
         grid=(pairs + 1, steps),
         in_specs=[
             pl.BlockSpec((count, length, width), lambda p, i: (edge(p, i), 0, 0)),
             pl.BlockSpec((count, pitch, width), lambda p, i: (tail(p, i), 0, 0)),
-            part(0), part(0), part(1), part(2),
-            pl.BlockSpec((count, 2, pitch, pitch), probs_at),
+            strip, strip, strip, pl.BlockSpec((count, pitch, pair), plain),
+            pl.BlockSpec((count, 2, pitch, pitch), exp_at),
+            pl.BlockSpec((count, 8, pitch), lambda p, i: (core(p, i)[0], 0, 0)),
             whole(w_qkv), whole(vecs), whole(strips), whole(dvec), whole(fc_units),
         ],
         out_specs=[pl.BlockSpec((count, length, width), lambda p, i: (tail(p, i), 0, 0)), HBM, HBM, HBM],
         out_shape=[sds((images, length, width), F32), sds(fc_sum, BF), sds(qkv_sum, BF), sds(dvec.shape, F32)],
         scratch_shapes=[
-            pltpu.VMEM((rows, width), BF), pltpu.VMEM((images * pitch, width), BF),
-            pltpu.VMEM((pairs, images * pitch, 3 * pair), BF), pltpu.VMEM((width, 3 * pair), F32),
-            pltpu.VMEM((pairs, 8, pair), F32), pltpu.VMEM(unit, BF), pltpu.VMEM(dvec.shape, F32),
+            pltpu.VMEM((rows, width), BF), pltpu.VMEM((images, width + 16, pitch), BF),
+            pltpu.VMEM((pairs, images, 3 * pair, pitch), BF), pltpu.VMEM((width, 3 * width), BF),
+            pltpu.VMEM((width + 16, 3 * pair), F32), pltpu.VMEM((pairs, 8, 3 * pair), F32), pltpu.VMEM(unit, BF), pltpu.VMEM(dvec.shape, F32),
             pltpu.VMEM(fc_sum, BF), pltpu.VMEM(qkv_sum, BF), pltpu.VMEM(dvec.shape, F32),
             pltpu.SemaphoreType.DMA((pairs + 3,)),
         ] + scratch,
         compiler_params=params(2, collective_id=1, has_side_effects=True),
         name="attention_backward",
-    )(inputs, grad_resid, grad_att, packed, packed, packed, probs, w_qkv, vecs, strips, dvec, fc_units)
+    )(inputs, grad_resid, grad_att, qt, kt, values, raised, inverse, w_qkv, vecs, strips, dvec, fc_units)
 
 
 def local(
@@ -840,8 +879,8 @@
     images, length, width = inputs.shape
     members = lax.axis_size("group")
     replicas = lax.axis_size("replica")
-    pitch = (length + 15) // 16 * 16
-    packed, probs, attended, wq, wp, w1, w2, vecs, bias_fc1 = forward_part(
+    pitch = (length + 7) // 8 * 8
+    qt, kt, values, raised, inverse, attended, wq, wp, w1, w2, vecs, bias_fc1 = forward_part(
         inputs, (w_qkv, w_proj, w_fc1, w_fc2),
         (gain_one, shift_one, b_query, b_value, b_proj, gain_two, shift_two, b_fc2, b_fc1), pitch, members,
     )
@@ -849,7 +888,7 @@
         inputs, cotangent, attended, wp, w1, w2, vecs, bias_fc1, pitch
     )
     grad_inputs, fc_sum, qkv_sum, vec_sum = backward_part(
-        inputs, grad_resid, grad_att, packed, probs, wq, vecs, strips, dvec, fc_units, pitch, replicas
+        inputs, grad_resid, grad_att, qt, kt, values, raised, inverse, wq, vecs, strips, dvec, fc_units, pitch, replicas
     )
     factor = float(images * length * replicas * members) ** (-0.5)
     weights = (gain_one, shift_one, w_qkv, b_query, b_value, w_proj, b_proj, gain_two, shift_two, w_fc1, b_fc1, w_fc2, b_fc2)

time: 209 us -> 184 us (0.88)
  Pallas kernels: 202 us -> 177 us
    pallas_call x1, Pallas kernels: 48.5 us -> 38.8 us  [forward_part(): pl.pallas_call(functools.partial(attention_forward, length, pitch, count,...]
    pallas_call x1, Pallas kernels: 92.1 us -> 84 us  [backward_part(): pl.pallas_call(functools.partial(attention_backward, length, pitch, count...]
    pallas_call x1, Pallas kernels: 57.8 us -> 51 us  [middle_part(): pl.pallas_call(functools.partial(mlp_both, length, pitch, count, 256), gr...]
where the time goes in v4:
time: 184 us
  Pallas kernels  177 us (96%)
  local copies, waits for them, and re-layouts  5.79 us (3%)
    pallas_call x1, Pallas kernels, backward_part(): pl.pallas_call(functools.partial(attention_backward, length, pitch, count...  84 us
    pallas_call x1, Pallas kernels, middle_part(): pl.pallas_call(functools.partial(mlp_both, length, pitch, count, 256), gr...  51 us
    pallas_call x1, Pallas kernels, forward_part(): pl.pallas_call(functools.partial(attention_forward, length, pitch, count,...  38.8 us
    unnamed x1, local copies, waits for them, and re-layouts  5.79 us

profile of v4, /device:TPU:0, one launch (start us, length us, event | category | flops | bytes accessed | tf_op | source)
XLA Modules:
  0.0 183.9 jit_solution(6672234480973889295)
XLA Ops:
  0.7 38.8 %attention_forward.1 = (bf16[20,384,200]{2,1,0:T(8,128)(2,1)}, bf16[20,384,200]{2,1,0:T(8,128)(2,1)}, bf16[20,200,384]{2,1,0:T(8,128)(2,1)}, bf16[20,6,200,200]{...) custom-call(bf16[20,197,384]{2,1,0:T(8,128)(2,1)} %x_ref.5, ...), custom_call_target="tpu_custom_call" | custom-call | tf_op jit(solution)/shard_map/attention_forward/pallas_call | solution.py:752
  39.5 51.0 %mlp_both.1 = (bf16[20,197,384]{2,1,0:T(8,128)(2,1)}, f32[20,200,384]{2,1,0:T(8,128)}, bf16[20,384,200]{2,1,0:T(8,128)(2,1)}, bf16[6,2,768,128]{3,2,1,0:T(8,128)...) custom-call(bf16[20,197,384]{2,1,0:T(8,128)(2,1)} %x_ref.5, bf16[20,197,384]{2,1,0:T(8,128)(2,1)} %ct_ref.1, ...), custom_call_target="tpu_custom_call" | custom-call | tf_op jit(solution)/shard_map/mlp_both/pallas_call | solution.py:787
  90.4 84.0 %attention_backward.1 = (f32[20,197,384]{2,1,0:T(8,128)}, bf16[6,768,128]{2,1,0:T(8,128)(2,1)}, bf16[3,768,128]{2,1,0:T(8,128)(2,1)}, f32[16,384]{1,0:T(8,128)}) custom-call(bf16[20,197,384]{2,1,0:T(8,128)(2,1)} %x_ref.5, f32[20,200,384]{2,1,0:T(8,128)} %get-tuple-element.57.gr_ref, bf16[20,384,200]{2,1,0:T(8,128)(2,1)} %get-tuple-element.58.ga_ref, ...), custom_call_target="tpu_custom_call" | custom-call | tf_op jit(solution)/shard_map/attention_backward/pallas_call | solution.py:850
  174.4 3.6 %unpack.1 = (f32[192]{0:T(256)}, f32[192]{0:T(256)}, f32[192,1152]{1,0:T(8,128)}, f32[192]{0:T(256)}, f32[192]{0:T(256)}, /*index=5*/f32[192,384]{1,0:T(8,128)},...) custom-call(bf16[6,768,128]{2,1,0:T(8,128)(2,1)} %get-tuple-element., ...), custom_call_target="tpu_custom_call" | custom-call | tf_op jit(solution)/shard_map/unpack/pallas_call | solution.py:895
  178.1 5.8 %copy.31 = f32[20,197,384]{2,1,0:T(8,128)} copy(f32[20,197,384]{2,1,0:T(8,128)} %get-tuple-element.101) | data formatting | bytes 12103680

commit v5 on v4

--- a/solution.py
+++ b/solution.py
@@ -94,8 +94,8 @@
 def attention_forward(
     length, pitch, count, late,
     x_ref, wq_hbm, wp_hbm, w1_hbm, w2_hbm, g1, s1, bq, bv, bp, g2, s2, b2, b1,
-    qt_ref, kt_ref, v_ref, exp_ref, inv_ref, att_ref, wq_out, wp_out, w1_out, w2_out, vec_out, b1_out,
-    pad_ref, wq, wp, w1, w2, small, wide, vec, b1_full, wqt, bias_q, k_ref,
+    qt_ref, kt_ref, v_ref, exp_ref, inv_ref, att_ref, nt_ref, wq_out, wp_out, w1_out, w2_out, vec_out, b1_out,
+    normed_ref, wq, wp, w1, w2, small, wide, vec, b1_full, wqt, bias_q, k_ref,
     sends, recvs, passes, arrivals, vec_send, vec_recv, own_sem, out_sem,
 ):
     step = pl.program_id(0)
@@ -120,7 +120,6 @@
 
     @pl.when(step == 0)
     def _():
-        pad_ref[...] = jnp.zeros_like(pad_ref)
         share = g1.shape[0]
         for k, ref in enumerate((g1, s1, bq, bv, bp, g2, s2, b2)):
             small[group, k : k + 1, 0:share] = ref[...].reshape(1, share).astype(F32)
@@ -132,6 +131,13 @@
         wide_copy.start()
         for copy in owns:
             copy.start()
+        tail_ = length // 8 * 8
+
+        @pl.loop(0, x_ref.shape[0])
+        def _(image):
+            normed_ref[image, tail_:, :] = jnp.zeros((pitch - tail_, width), F32)
+            normed_ref[image, 0:length, :] = row_stats(x_ref[image].astype(F32))[0]
+
         small_copy.wait()
         for side in range(2):
             vec[:, side * share : (side + 1) * share] = small[side, :, 0:share]
@@ -164,14 +170,14 @@
 
     gain = vec[0:1, :]
     shift = vec[1:2, :]
-    for image in range(count):
-        pad_ref[image * pitch : image * pitch + length, :] = x_ref[image]
-    normed, _ = row_stats(pad_ref[...].astype(F32))
+    normed = normed_ref[pl.ds(step * count, count)].reshape(count * pitch, width)
     hidden = (normed * gain + shift).astype(BF)
     keys_all = dot(hidden, wq[:, width : 2 * width]).astype(BF)
     values_all = (dot(hidden, wq[:, 2 * width :]) + vec[3:4, :]).astype(BF)
     for image in range(count):
         rows = slice(image * pitch, (image + 1) * pitch)
+        nt_ref[image, 0:width, :] = normed[rows].astype(BF).T
+        nt_ref[image, width:, :] = jnp.ones((16, pitch), BF)
         k_ref[image] = keys_all[rows]
         v_ref[image] = values_all[rows]
         qt_ref[image] = ((dot_rt(wqt[...], hidden[rows]) + bias_q[...]) * factor).astype(BF)
@@ -303,35 +309,38 @@
             dvec_ref[8 + k : 9 + k, :] = accb[0:1, k * width : (k + 1) * width]
 
 
-def phases_of(heads):
-    return heads // 2
-
-
-def schedule(total, steps):
-    plan = {}
-
-    def put(at, *work):
-        plan.setdefault(at if at < total else -1, []).append(work)
-
-    def chain(name, starts):
+CHAINS = {
+    "a": (0, 1, 3, 5, 7, 9, 11, 12),
+    "b": (0, 1, 3, 5, 7, 9, 11, 12),
+    "c": (0, 3, 5, 7, 9, 11, 13, 14),
+    0: (4, 5, 8, 10, 12, 13, 14, 15),
+    1: (8, 9, 11, 13, 14, 15, 16, 16),
+    2: (12, 13, 14, 16, 16, 16),
+    "v": (12, 13, 14, 15, 16),
+}
+SWAPPED = ("b", 0)
+SHORT = (2,)
+
+
+def schedule(total):
+    plan = {0: [("greet", None, None)]}
+    for name, starts in CHAINS.items():
+        order = order_of(name)
         for k, at in enumerate(starts):
-            put(at, name, ORDER[k - 1] if k else None, ORDER[k] if k < len(ORDER) else None)
-
-    plan[0] = [("greet", None, None)]
-    chain("a", (0, 1, 4, 6, 8, 10, 12, 14))
-    chain("b", (0, 3, 7, 9, 11, 13, 15, 16))
-    chain(0, (steps, 7, 9, 10, 12, 13, 14, 15))
-    chain(1, (2 * steps, 11, 13, 14, 15, 16, 17, 18))
-    chain(2, (3 * steps, 16, 17, 18, 19, total, total, total))
+            work = (name, order[k - 1] if k else None, order[k] if k < len(order) else None)
+            plan.setdefault(at if at < total else -1, []).append(work)
     return plan
 
 
-ORDER = (0, 1, 2, 3, 5, 6, 7)
+def order_of(name):
+    if name == "v":
+        return (0, 1, 2, 3)
+    return (0, 1, 3, 5, 7) if name in SHORT else (0, 1, 2, 3, 5, 6, 7)
 
 
 class Ticks:
-    def __init__(self, parts, vectors, vec_out, flushes, vec_flush):
-        self.parts, self.vectors, self.vec_out, self.flushes, self.vec_flush = parts, vectors, vec_out, flushes, vec_flush
+    def __init__(self, parts, flushes):
+        self.parts, self.flushes = parts, flushes
 
     def run(self, work):
         for name, done, start in work:
@@ -340,55 +349,52 @@
                 continue
             part = self.parts[name]
             if done is not None:
-                self.finish(name, part, done)
+                part.finish(done)
+                if done == 3 and part.extra > 1:
+                    part.start(4)
+                    part.finish(4)
+                if done == order_of(name)[-1]:
+                    self.flushes[name].start()
             if start is not None:
                 part.start(start)
 
-    def finish(self, name, part, done):
-        part.finish(done)
-        if done == 3 and part.extra > 1:
-            part.start(4)
-            part.finish(4)
-        if done == ORDER[-1]:
-            self.flushes[name].start()
-
     def close(self, work):
-        vectors, pending = self.vectors, list(work)
-        vectors.start(0)
-        for stage in range(5):
-            if pending:
-                self.run([pending.pop(0)])
-            vectors.finish(stage, self.vec_out)
-            if stage < 4:
-                vectors.start(stage + 1)
-        self.run(pending)
-        self.vec_flush.start()
-        for copy in list(self.flushes.values()) + [self.vec_flush]:
+        pending = list(work)
+        while pending:
+            names, later = set(), []
+            for item in pending:
+                if item[0] in names:
+                    later.append(item)
+                else:
+                    names.add(item[0])
+                    self.run([item])
+            pending = later
+        for copy in self.flushes.values():
             copy.wait()
 
 
 def make_ticks(fc_ref, unit_ref, dvec_ref, fc_out, qkv_out, vec_out, fc_hbm, qkv_hbm, vec_hbm, flush_sem, scratch):
-    three = fc_ref.shape[0] // 2
+    third = fc_ref.shape[0] // 3
     pairs = unit_ref.shape[0]
-    sources = {"a": (fc_ref, fc_out, fc_hbm, 0, three), "b": (fc_ref, fc_out, fc_hbm, three, three)}
+    sources = {name: (fc_ref, fc_out, fc_hbm, k * third, third) for k, name in enumerate("abc")}
     for k in range(pairs):
         sources[k] = (unit_ref, qkv_out, qkv_hbm, k, 1)
     parts, flushes = {}, {}
     for k, (name, (source, out, hbm, at, size)) in enumerate(sources.items()):
         refs = scratch[k * REDUCE_REFS : (k + 1) * REDUCE_REFS]
         mine = pl.ds(at, size)
-        parts[name] = Reduce(source.at[mine], refs[:8], out.at[mine], refs[8], refs[9])
+        parts[name] = Reduce(source.at[mine], refs[:8], out.at[mine], refs[8], refs[9], name)
         flushes[name] = pltpu.make_async_copy(out.at[mine], hbm.at[mine], flush_sem.at[k])
-    vectors = ReduceVectors(parts["a"], *scratch[len(sources) * REDUCE_REFS :], first=dvec_ref)
-    vec_flush = pltpu.make_async_copy(vec_out, vec_hbm, flush_sem.at[len(sources)])
-    return Ticks(parts, vectors, vec_out, flushes, vec_flush)
+    parts["v"] = ReduceVectors(parts["a"], *scratch[len(sources) * REDUCE_REFS :], first=dvec_ref, out=vec_out)
+    flushes["v"] = pltpu.make_async_copy(vec_out, vec_hbm, flush_sem.at[len(sources)])
+    return Ticks(parts, flushes)
 
 
 def attention_backward(
     length, pitch, count, steps,
-    x_ref, gr_ref, ga_ref, qt_ref, kt_ref, v_ref, exp_ref, inv_ref, wq_ref, vec_ref, strip_ref, dvec_in, fc_ref,
+    x_ref, gr_ref, ga_ref, qt_ref, kt_ref, v_ref, exp_ref, inv_ref, nt_ref, wq_ref, vec_ref, strip_ref, dvec_in, fc_ref,
     gx_ref, fc_hbm, qkv_hbm, vec_hbm,
-    pad_ref, hid_ref, gp_ref, wperm, acc, accv, unit_ref, dvec_ref, fc_out, qkv_out, vec_out, flush_sem, *scratch,
+    pad_ref, gp_ref, wperm, acc, accv, unit_ref, dvec_ref, fc_out, qkv_out, vec_out, flush_sem, *scratch,
 ):
     phase, block = pl.program_id(0), pl.program_id(1)
     phases, blocks_ = pl.num_programs(0), pl.num_programs(1)
@@ -396,7 +402,7 @@
     ticks = make_ticks(
         fc_ref, unit_ref, dvec_ref, fc_out, qkv_out, vec_out, fc_hbm, qkv_hbm, vec_hbm, flush_sem, scratch
     )
-    plan = schedule((phases_of(HEADS) + 1) * steps, steps)
+    plan = schedule((HEADS // 2 + 1) * steps)
     for at, work in plan.items():
         if at >= 0:
             @pl.when(step == at)
@@ -409,7 +415,6 @@
     rows = count * pitch
     first = block * count
     gain = vec_ref[0:1, :]
-    shift = vec_ref[1:2, :]
 
     @pl.when(jnp.logical_and(phase == 0, block == 0))
     def _():
@@ -423,14 +428,6 @@
         for image in range(count):
             pad_ref[image * pitch : image * pitch + length, :] = x_ref[image]
         return row_stats(pad_ref[...].astype(F32))
-
-    @pl.when(phase == 0)
-    def _():
-        normed, _ = stats()
-        hidden = (normed * gain + shift).astype(BF)
-        for image in range(count):
-            hid_ref[first + image, 0:width, :] = hidden[image * pitch : (image + 1) * pitch].T
-            hid_ref[first + image, width:, :] = jnp.ones((16, pitch), BF)
 
     @pl.when(phase < phases - 1)
     def _():
@@ -470,7 +467,7 @@
         def gather(item):
             image, side = item
             if side == 1:
-                acc[...] += dot_rt(hid_ref[first + image], gp_ref[phase, first + image])
+                acc[...] += dot_rt(nt_ref[image], gp_ref[phase, first + image])
 
         items = [(image, side) for image in range(count) for side in range(2)]
         pipeline(items, probe, soften, spread, gather)
@@ -486,40 +483,37 @@
                 unit_ref[phase, side, 3 * share :, :] = strip_ref[phase, side]
             accv[phase] = acc[width : width + 8, :]
 
+            @pl.when(phase == phases - 2)
+            def _():
+                dvec_ref[...] = dvec_in[...]
+                for two in range(HEADS // 2):
+                    for third in range(3):
+                        dvec_ref[4 + third : 5 + third, two * pair : (two + 1) * pair] = accv[
+                            two, 0:1, third * pair : (third + 1) * pair
+                        ]
+
     @pl.when(phase == phases - 1)
     def _():
-        @pl.when(block == 0)
-        def _():
-            dvec_ref[...] = dvec_in[...]
-            for two in range(HEADS // 2):
-                cols = slice(two * pair, (two + 1) * pair)
-                dvec_ref[4:5, cols] = accv[two, 0:1, 0:pair]
-                dvec_ref[5:6, cols] = accv[two, 0:1, 2 * pair : 3 * pair]
-
         normed, inverse = stats()
-        sum_n = jnp.zeros((1, width), F32)
-        sum_h = jnp.zeros((1, width), F32)
         for image in range(count):
             at = slice(image * pitch, (image + 1) * pitch)
             packed = jnp.concatenate([gp_ref[two, first + image] for two in range(HEADS // 2)], axis=0)
             grad_hidden = dot(wperm[...], packed).T
-            sum_n += col_sum(grad_hidden * normed[at])
-            sum_h += col_sum(grad_hidden)
             grad_x = gr_ref[image] + norm_back(grad_hidden, normed[at], inverse[at], gain)
-            gx_ref[image] = grad_x[:length]
-        dvec_ref[6:7, :] += sum_n
-        dvec_ref[7:8, :] += sum_h
+            gx_ref[image] = grad_x[:length].astype(BF)
 
         @pl.when(block == blocks_ - 1)
         def _():
             ticks.close(plan.get(-1, []))
 
 
+SLOTS = {False: (0, 1, 2, 3, 11, 6, 9, 10), True: (0, 1, 0, 2, 17, 9, 0, 16)}
+
+
 class Reduce:
-    STAGES = 8
-
-    def __init__(self, source, bufs, out, sends, recvs):
+    def __init__(self, source, bufs, out, sends, recvs, name):
         self.replica, self.group = place()
+        self.swapped, self.short = name in SWAPPED, name in SHORT
         self.source, self.out = source, out
         self.r1, self.b1, self.r2, self.b2, self.rx, self.bx, self.rz, self.ez = bufs
         replicas = lax.axis_size("replica")
@@ -531,6 +525,7 @@
         self.x = lax.rem(r // 2, 2)
         self.z = lax.rem(r // 4, 4)
         self.e = r // 16
+        self.m = lax.rem(r // 2, 8)
         self.sends, self.recvs = sends, recvs
         low = self.core * half
         self.at_core = pl.ds(pl.multiple_of(low, half), half)
@@ -540,7 +535,7 @@
         )
 
     def partners(self):
-        return [self.to_core(), self.to_group(), self.to_x()] + [self.to_z(d) for d in (1, 2, 3)] + [
+        return [self.to_core(), self.to_group()] + [self.to_m(d) for d in range(1, 8)] + [
             self.to_e(d) for d in range(1, self.extra)
         ]
 
@@ -559,21 +554,45 @@
     def to_z(self, hop):
         return (self.replica + 4 * (self.z_at(hop) - self.z), self.group)
 
+    def m_at(self, hop):
+        return lax.rem(self.m + hop, 8)
+
+    def to_m(self, hop):
+        return (self.replica + 2 * (self.m_at(hop) - self.m), self.group)
+
+    def row_of(self, m):
+        start = lax.rem(m, 2) * self.quarter + m // 2 * self.piece
+        return pl.ds(pl.multiple_of(start, self.piece), self.piece)
+
     def to_e(self, hop):
         return (self.replica + 16 * (lax.rem(self.e + hop, self.extra) - self.e), self.group)
 
     def copy(self, stage, source, target, device, hop=0):
-        return remote(source, target, self.sends.at[stage, hop], self.recvs.at[stage, hop], device)
+        at = SLOTS[self.short][stage] + hop - (stage in (3, 5)) - (stage == 4)
+        return remote(source, target, self.sends.at[at], self.recvs.at[at], device)
 
     def copies(self, stage):
         if stage == 0:
             other = pl.ds(pl.multiple_of((1 - self.core) * self.half, self.half), self.half)
             return [self.copy(0, self.source.at[:, :, other], self.r1, self.to_core())]
+        if stage == 1 and self.swapped:
+            other = pl.ds(pl.multiple_of((1 - self.x) * self.quarter, self.quarter), self.quarter)
+            return [self.copy(1, self.b1.at[:, :, other], self.r2, self.to_x())]
+        if stage == 2 and self.swapped:
+            return [self.copy(2, self.b2.at[:, 1 - self.group], self.rx, self.to_group())]
         if stage == 1:
             return [self.copy(1, self.b1.at[:, 1 - self.group], self.r2, self.to_group())]
         if stage == 2:
             other = pl.ds(pl.multiple_of((1 - self.x) * self.quarter, self.quarter), self.quarter)
             return [self.copy(2, self.b2.at[:, other], self.rx, self.to_x())]
+        if stage == 3 and self.short:
+            return [
+                self.copy(3, self.b2.at[:, self.row_of(self.m_at(hop))], self.rz.at[hop - 1], self.to_m(hop), hop)
+                for hop in range(1, 8)
+            ]
+        if stage == 5 and self.short:
+            place_ = self.out.at[:, self.at_piece]
+            return [self.copy(5, place_, place_, self.to_m(hop), hop) for hop in range(1, 8)]
         if stage == 3:
             out = []
             for hop in (1, 2, 3):
@@ -601,16 +620,22 @@
         for copy in self.copies(stage):
             copy.wait()
         if stage == 0:
-            self.b1[...] = (self.source[:, :, self.at_core].astype(F32) + self.r1[...].astype(F32)).astype(BF)
+            self.b1[...] = self.source[:, :, self.at_core] + self.r1[...]
+        elif stage == 1 and self.swapped:
+            mine = pl.ds(pl.multiple_of(self.x * self.quarter, self.quarter), self.quarter)
+            self.b2[...] = self.b1[:, :, mine] + self.r2[...]
+        elif stage == 2 and self.swapped:
+            self.bx[...] = self.b2[:, self.group] + self.rx[...]
         elif stage == 1:
-            self.b2[...] = (self.b1[:, self.group].astype(F32) + self.r2[...].astype(F32)).astype(BF)
+            self.b2[...] = self.b1[:, self.group] + self.r2[...]
         elif stage == 2:
             mine = pl.ds(pl.multiple_of(self.x * self.quarter, self.quarter), self.quarter)
-            self.bx[...] = (self.b2[:, mine].astype(F32) + self.rx[...].astype(F32)).astype(BF)
+            self.bx[...] = self.b2[:, mine] + self.rx[...]
         elif stage == 3:
             mine = pl.ds(pl.multiple_of(self.z * self.piece, self.piece), self.piece)
-            total = self.bx[:, mine].astype(F32)
-            for hop in range(3):
+            own = self.b2.at[:, self.row_of(self.m)] if self.short else self.bx.at[:, mine]
+            total = own[...].astype(F32)
+            for hop in range(self.rz.shape[0]):
                 total = total + self.rz[hop].astype(F32)
             if self.extra > 1:
                 self.ez[self.e] = total.astype(BF)
@@ -623,21 +648,22 @@
             self.out[:, self.at_piece] = total.astype(BF)
 
 
-def reduce_scratch(units, rows, replicas):
+def reduce_scratch(units, rows, replicas, name):
     half, extra = rows // 2, max(replicas // 16, 1)
-    hops = max(4, extra)
+    sems = SLOTS[name in SHORT][4] + extra - 1
+    second = (units, 2, half // 2, LANES) if name in SWAPPED else (units, half, LANES)
     return [
         pltpu.VMEM((units, 2, half, LANES), BF), pltpu.VMEM((units, 2, half, LANES), BF),
-        pltpu.VMEM((units, half, LANES), BF), pltpu.VMEM((units, half, LANES), BF),
+        pltpu.VMEM(second, BF), pltpu.VMEM(second, BF),
         pltpu.VMEM((units, half // 2, LANES), BF), pltpu.VMEM((units, half // 2, LANES), BF),
-        pltpu.VMEM((3, units, half // 8, LANES), BF), pltpu.VMEM((extra, units, half // 8, LANES), BF),
-        pltpu.SemaphoreType.DMA((Reduce.STAGES, hops)), pltpu.SemaphoreType.DMA((Reduce.STAGES, hops)),
+        pltpu.VMEM((7 if name in SHORT else 3, units, half // 8, LANES), BF), pltpu.VMEM((extra, units, half // 8, LANES), BF),
+        pltpu.SemaphoreType.DMA((sems,)), pltpu.SemaphoreType.DMA((sems,)),
     ]
 
 
 class ReduceVectors:
-    def __init__(self, like, v2, v3, slots_z, slots_e, got, sends, recvs, first):
-        self.like = like
+    def __init__(self, like, v2, v3, slots_z, slots_e, got, sends, recvs, first, out):
+        self.like, self.out, self.extra = like, out, like.extra
         self.vals, self.slots_z, self.slots_e, self.got, self.sends, self.recvs = (
             (first, v2, v3), slots_z, slots_e, got, sends, recvs
         )
@@ -646,23 +672,23 @@
         o = self.like
         if stage < 3:
             device = (o.to_core, o.to_group, o.to_x)[stage]()
-            return [remote(self.vals[stage], self.got.at[stage], self.sends.at[stage, 0], self.recvs.at[stage, 0], device)]
+            return [remote(self.vals[stage], self.got.at[stage], self.sends.at[stage], self.recvs.at[stage], device)]
         if stage == 3:
             mine = self.slots_z.at[o.z]
             return [
-                remote(mine, mine, self.sends.at[3, hop], self.recvs.at[3, hop], o.to_z(hop)) for hop in (1, 2, 3)
+                remote(mine, mine, self.sends.at[2 + hop], self.recvs.at[2 + hop], o.to_z(hop)) for hop in (1, 2, 3)
             ]
         mine = self.slots_e.at[o.e]
         return [
-            remote(mine, mine, self.sends.at[4, hop], self.recvs.at[4, hop], o.to_e(hop)) for hop in range(1, o.extra)
+            remote(mine, mine, self.sends.at[5 + hop], self.recvs.at[5 + hop], o.to_e(hop)) for hop in range(1, o.extra)
         ]
 
     def start(self, stage):
         for copy in self.copies(stage):
             copy.start()
 
-    def finish(self, stage, out):
-        o = self.like
+    def finish(self, stage):
+        o, out = self.like, self.out
         for copy in self.copies(stage):
             copy.wait()
         if stage < 2:
@@ -684,42 +710,57 @@
 
 def vector_scratch(shape, replicas):
     extra = max(replicas // 16, 1)
-    hops = max(4, extra)
     return [
         pltpu.VMEM(shape, F32), pltpu.VMEM(shape, F32),
         pltpu.VMEM((4,) + shape, F32), pltpu.VMEM((extra,) + shape, F32), pltpu.VMEM((3,) + shape, F32),
-        pltpu.SemaphoreType.DMA((5, hops)), pltpu.SemaphoreType.DMA((5, hops)),
+        pltpu.SemaphoreType.DMA((5 + extra,)), pltpu.SemaphoreType.DMA((5 + extra,)),
     ]
 
 
 REDUCE_REFS = 10
 
 
-def unpack(factor, fc_ref, qkv_ref, vec_ref, g1, s1, wq, bq, bv, wp, bp, g2, s2, w1, b1, w2, b2):
-    share, width = wp.shape
-    group = lax.axis_index("group")
-    pair = LANES
-    for two in range(qkv_ref.shape[0]):
-        for third in range(3):
-            wq[:, third * width + two * pair : third * width + (two + 1) * pair] = (
-                qkv_ref[two, third * share : (third + 1) * share, :].astype(F32) * factor
-            )
-        wp[:, two * pair : (two + 1) * pair] = qkv_ref[two, 3 * share :, :].astype(F32) * factor
-    strips = w1.shape[1] // LANES
-    for strip in range(strips):
-        unit, at = strip // QUAD, strip % QUAD * share
-        w1[:, strip * LANES : (strip + 1) * LANES] = fc_ref[unit, at : at + share, :].astype(F32) * factor
-    for strip in range(w2.shape[0] // LANES):
-        unit, at = strip // 2 + strips // QUAD, strip % 2 * width
-        w2[strip * LANES : (strip + 1) * LANES, :] = (fc_ref[unit, at : at + width, :].astype(F32) * factor).T
-    rows = vec_ref[...] * factor
-    mine = jnp.where(group == 0, rows[:, 0:share], rows[:, share:])
-    for k, ref in enumerate((bp, g2, s2, b2, bq, bv, g1, s1)):
-        ref[...] = mine[k : k + 1, :].reshape(share)
-    per = b1.shape[0] // width
-    for k in range(per):
-        row = jnp.where(group == 0, rows[8 + k : 9 + k, :], rows[8 + per + k : 9 + per + k, :])
-        b1[k * width : (k + 1) * width] = row.reshape(width)
+def unpack(factor, gx_in, fc_ref, qkv_ref, vec_ref, w_ref, gain_ref, shift_ref, gx_out, g1, s1, wq, bq, bv, wp, bp, g2, s2, w1, b1, w2, b2):
+    gx_out[...] = gx_in[...].astype(F32)
+
+    @pl.when(pl.program_id(0) == 0)
+    def _():
+        share, width = wp.shape
+        group = lax.axis_index("group")
+        pair = LANES
+        column = [
+            jnp.broadcast_to(ref[...].reshape(1, share).astype(F32), (8, share)).T[:, 0:1] for ref in (gain_ref, shift_ref)
+        ]
+        sum_g = jnp.zeros((share, pair), F32)
+        sum_s = jnp.zeros((share, pair), F32)
+        for two in range(qkv_ref.shape[0]):
+            for third in range(3):
+                cols = slice(third * width + two * pair, third * width + (two + 1) * pair)
+                cross = qkv_ref[two, third * share : (third + 1) * share, :].astype(F32)
+                total = vec_ref[4 + third : 5 + third, two * pair : (two + 1) * pair]
+                weight = w_ref[:, cols].astype(F32)
+                sum_g += weight * cross
+                sum_s += weight * total
+                wq[:, cols] = (column[0] * cross + column[1] * total) * factor
+            wp[:, two * pair : (two + 1) * pair] = qkv_ref[two, 3 * share :, :].astype(F32) * factor
+        for ref, total in ((g1, sum_g), (s1, sum_s)):
+            ref[...] = (col_sum(total.T) * factor).reshape(share)
+        strips = w1.shape[1] // LANES
+        for strip in range(strips):
+            unit, at = strip // QUAD, strip % QUAD * share
+            w1[:, strip * LANES : (strip + 1) * LANES] = fc_ref[unit, at : at + share, :].astype(F32) * factor
+        for strip in range(w2.shape[0] // LANES):
+            unit, at = strip // 2 + strips // QUAD, strip % 2 * width
+            w2[strip * LANES : (strip + 1) * LANES, :] = (fc_ref[unit, at : at + width, :].astype(F32) * factor).T
+        rows = vec_ref[...] * factor
+        mine = jnp.where(group == 0, rows[:, 0:share], rows[:, share:])
+        for k, ref in enumerate((bp, g2, s2, b2, bq, None, bv)):
+            if ref is not None:
+                ref[...] = mine[k : k + 1, :].reshape(share)
+        per = b1.shape[0] // width
+        for k in range(per):
+            row = jnp.where(group == 0, rows[8 + k : 9 + k, :], rows[8 + per + k : 9 + per + k, :])
+            b1[k * width : (k + 1) * width] = row.reshape(width)
 
 
 def whole(array):
@@ -744,25 +785,26 @@
 
 def forward_part(inputs, weights, vectors, pitch, members):
     images, length, width = inputs.shape
-    count = 2
+    count = 4
     share, wide = vectors[0].shape[0], vectors[-1].shape[0]
     lanes = (share + LANES - 1) // LANES * LANES
     fulls = [(members * w.shape[0], w.shape[1]) for w in weights]
     turned = (images, width, pitch)
     return pl.pallas_call(
-        functools.partial(attention_forward, length, pitch, count, 5),
+        functools.partial(attention_forward, length, pitch, count, 2),
         grid=(images // count,),
-        in_specs=[blocks(count, length, width)] + [HBM] * 4 + [whole(v) for v in vectors],
+        in_specs=[whole(inputs)] + [HBM] * 4 + [whole(v) for v in vectors],
         out_specs=[
             blocks(count, width, pitch), blocks(count, width, pitch), blocks(count, pitch, width),
             blocks(count, HEADS, pitch, pitch), blocks(count, 8, pitch), blocks(count, width, pitch),
-            HBM, HBM, HBM, HBM, fixed(8, width), fixed(8, members * wide),
+            blocks(count, width + 16, pitch), HBM, HBM, HBM, HBM, fixed(8, width), fixed(8, members * wide),
         ],
         out_shape=[
             sds(turned, BF), sds(turned, BF), sds((images, pitch, width), BF),
             sds((images, HEADS, pitch, pitch), BF), sds((images, 8, pitch), F32), sds(turned, BF),
+            sds((images, width + 16, pitch), BF),
         ] + [sds(full, BF) for full in fulls] + [sds((8, width), F32), sds((8, members * wide), F32)],
-        scratch_shapes=[pltpu.VMEM((count * pitch, width), BF)] + [pltpu.VMEM(full, BF) for full in fulls] + [
+        scratch_shapes=[pltpu.VMEM((images, pitch, width), F32)] + [pltpu.VMEM(full, BF) for full in fulls] + [
             pltpu.VMEM((members, 8, lanes), F32), pltpu.VMEM((members, 8, wide), F32),
             pltpu.VMEM((8, width), F32), pltpu.VMEM((8, members * wide), F32),
             pltpu.VMEM((width, width), BF), pltpu.VMEM((width, pitch), F32), pltpu.VMEM((count, pitch, width), BF),
@@ -810,9 +852,9 @@
     )(inputs, cotangent, attended, w_proj, w_fc1, w_fc2, vecs, bias_fc1)
 
 
-def backward_part(inputs, grad_resid, grad_att, qt, kt, values, raised, inverse, w_qkv, vecs, strips, dvec, fc_units, pitch, replicas):
+def backward_part(inputs, grad_resid, grad_att, qt, kt, values, raised, inverse, turned_x, w_qkv, vecs, strips, dvec, fc_units, pitch, replicas):
     images, length, width = inputs.shape
-    count = 4
+    count = 5
     rows = count * pitch
     steps = images // count
     pairs = HEADS // 2
@@ -821,12 +863,13 @@
     unit = (pairs, 2, unit_rows, LANES)
     fc_sum, qkv_sum = (fc_units.shape[0], unit_rows, LANES), (pairs, unit_rows, LANES)
     scratch = []
-    for units in (fc_units.shape[0] // 2,) * 2 + (1,) * pairs:
-        scratch += reduce_scratch(units, unit_rows, replicas)
+    for name in [name for name in CHAINS if name != "v"]:
+        units = 1 if name in range(pairs) else fc_units.shape[0] // 3
+        scratch += reduce_scratch(units, unit_rows, replicas, name)
     scratch += vector_scratch(dvec.shape, replicas)
 
     def edge(p, i):
-        return jnp.where(jnp.logical_or(p == 0, p == pairs), i, steps - 1)
+        return jnp.where(p == pairs, i, 0)
 
     def tail(p, i):
         return jnp.where(p == pairs, i, 0)
@@ -856,20 +899,21 @@
             strip, strip, strip, pl.BlockSpec((count, pitch, pair), plain),
             pl.BlockSpec((count, 2, pitch, pitch), exp_at),
             pl.BlockSpec((count, 8, pitch), lambda p, i: (core(p, i)[0], 0, 0)),
+            pl.BlockSpec((count, width + 16, pitch), lambda p, i: (core(p, i)[0], 0, 0)),
             whole(w_qkv), whole(vecs), whole(strips), whole(dvec), whole(fc_units),
         ],
         out_specs=[pl.BlockSpec((count, length, width), lambda p, i: (tail(p, i), 0, 0)), HBM, HBM, HBM],
-        out_shape=[sds((images, length, width), F32), sds(fc_sum, BF), sds(qkv_sum, BF), sds(dvec.shape, F32)],
+        out_shape=[sds((images, length, width), BF), sds(fc_sum, BF), sds(qkv_sum, BF), sds(dvec.shape, F32)],
         scratch_shapes=[
-            pltpu.VMEM((rows, width), BF), pltpu.VMEM((images, width + 16, pitch), BF),
+            pltpu.VMEM((rows, width), BF),
             pltpu.VMEM((pairs, images, 3 * pair, pitch), BF), pltpu.VMEM((width, 3 * width), BF),
             pltpu.VMEM((width + 16, 3 * pair), F32), pltpu.VMEM((pairs, 8, 3 * pair), F32), pltpu.VMEM(unit, BF), pltpu.VMEM(dvec.shape, F32),
             pltpu.VMEM(fc_sum, BF), pltpu.VMEM(qkv_sum, BF), pltpu.VMEM(dvec.shape, F32),
-            pltpu.SemaphoreType.DMA((pairs + 3,)),
+            pltpu.SemaphoreType.DMA((len(CHAINS) + 1,)),
         ] + scratch,
         compiler_params=params(2, collective_id=1, has_side_effects=True),
         name="attention_backward",
-    )(inputs, grad_resid, grad_att, qt, kt, values, raised, inverse, w_qkv, vecs, strips, dvec, fc_units)
+    )(inputs, grad_resid, grad_att, qt, kt, values, raised, inverse, turned_x, w_qkv, vecs, strips, dvec, fc_units)
 
 
 def local(
@@ -880,7 +924,7 @@
     members = lax.axis_size("group")
     replicas = lax.axis_size("replica")
     pitch = (length + 7) // 8 * 8
-    qt, kt, values, raised, inverse, attended, wq, wp, w1, w2, vecs, bias_fc1 = forward_part(
+    qt, kt, values, raised, inverse, attended, turned_x, wq, wp, w1, w2, vecs, bias_fc1 = forward_part(
         inputs, (w_qkv, w_proj, w_fc1, w_fc2),
         (gain_one, shift_one, b_query, b_value, b_proj, gain_two, shift_two, b_fc2, b_fc1), pitch, members,
     )
@@ -888,16 +932,22 @@
         inputs, cotangent, attended, wp, w1, w2, vecs, bias_fc1, pitch
     )
     grad_inputs, fc_sum, qkv_sum, vec_sum = backward_part(
-        inputs, grad_resid, grad_att, qt, kt, values, raised, inverse, wq, vecs, strips, dvec, fc_units, pitch, replicas
+        inputs, grad_resid, grad_att, qt, kt, values, raised, inverse, turned_x, wq, vecs, strips, dvec, fc_units,
+        pitch, replicas
     )
     factor = float(images * length * replicas * members) ** (-0.5)
     weights = (gain_one, shift_one, w_qkv, b_query, b_value, w_proj, b_proj, gain_two, shift_two, w_fc1, b_fc1, w_fc2, b_fc2)
-    grads = pl.pallas_call(
+    grad_inputs, *grads = pl.pallas_call(
         functools.partial(unpack, factor),
-        out_shape=[sds(w.shape, F32) for w in weights],
-        compiler_params=pltpu.CompilerParams(vmem_limit_bytes=VMEM_LIMIT),
+        grid=(4,),
+        in_specs=[blocks(images // 4, length, width), whole(fc_sum), whole(qkv_sum), whole(vec_sum)] + [
+            whole(w) for w in (w_qkv, gain_one, shift_one)
+        ],
+        out_specs=[blocks(images // 4, length, width)] + [whole(w) for w in weights],
+        out_shape=[sds(inputs.shape, F32)] + [sds(w.shape, F32) for w in weights],
+        compiler_params=params(),
         name="unpack",
-    )(fc_sum, qkv_sum, vec_sum)
+    )(grad_inputs, fc_sum, qkv_sum, vec_sum, w_qkv, gain_one, shift_one)
     return (outputs, grad_inputs) + tuple(grads)
 
 

time: 184 us -> 166 us (0.902)
  Pallas kernels: 177 us -> 165 us
  local copies, waits for them, and re-layouts: 5.79 us -> 0 us
    pallas_call x1, Pallas kernels: 84 us -> 65.7 us  [backward_part(): pl.pallas_call(functools.partial(attention_backward, length, pitch, count...]
    unnamed x1 -> x0, local copies, waits for them, and re-layouts: 5.79 us -> none
    pallas_call x1, Pallas kernels: 3.62 us -> 7.87 us  [local(): pl.pallas_call(functools.partial(unpack, factor), grid=(4,), in_specs=[bl...]
    pallas_call x1, Pallas kernels: 38.8 us -> 40.9 us  [forward_part(): pl.pallas_call(functools.partial(attention_forward, length, pitch, count,...]
where the time goes in v5:
time: 166 us
  Pallas kernels  165 us (99%)
    pallas_call x1, Pallas kernels, backward_part(): pl.pallas_call(functools.partial(attention_backward, length, pitch, count...  65.7 us
    pallas_call x1, Pallas kernels, middle_part(): pl.pallas_call(functools.partial(mlp_both, length, pitch, count, 256), gr...  51 us
    pallas_call x1, Pallas kernels, forward_part(): pl.pallas_call(functools.partial(attention_forward, length, pitch, count,...  40.9 us
    pallas_call x1, Pallas kernels, local(): pl.pallas_call(functools.partial(unpack, factor), grid=(4,), in_specs=[bl...  7.87 us

profile of v5, /device:TPU:0, one launch (start us, length us, event | category | flops | bytes accessed | tf_op | source)
XLA Modules:
  0.0 166.3 jit_solution(10048388935034921081)
XLA Ops:
  0.6 40.9 %attention_forward.1 = (bf16[20,384,200]{2,1,0:T(8,128)(2,1)}, bf16[20,384,200]{2,1,0:T(8,128)(2,1)}, bf16[20,200,384]{2,1,0:T(8,128)(2,1)}, bf16[20,6,200,200]{...) custom-call(bf16[20,197,384]{2,1,0:T(8,128)(2,1)} %x_ref.5, ...), custom_call_target="tpu_custom_call" | custom-call | tf_op jit(solution)/shard_map/attention_forward/pallas_call | solution.py:793
  41.5 51.0 %mlp_both.1 = (bf16[20,197,384]{2,1,0:T(8,128)(2,1)}, f32[20,200,384]{2,1,0:T(8,128)}, bf16[20,384,200]{2,1,0:T(8,128)(2,1)}, bf16[6,2,768,128]{3,2,1,0:T(8,128)...) custom-call(bf16[20,197,384]{2,1,0:T(8,128)(2,1)} %x_ref.5, bf16[20,197,384]{2,1,0:T(8,128)(2,1)} %ct_ref.1, ...), custom_call_target="tpu_custom_call" | custom-call | tf_op jit(solution)/shard_map/mlp_both/pallas_call | solution.py:829
  92.5 65.7 %attention_backward.1 = (bf16[20,197,384]{2,1,0:T(8,128)(2,1)}, bf16[6,768,128]{2,1,0:T(8,128)(2,1)}, bf16[3,768,128]{2,1,0:T(8,128)(2,1)}, f32[16,384]{1,0:T(8,128)}) custom-call(bf16[20,197,384]{2,1,0:T(8,128)(2,1)} %x_ref.5, f32[20,200,384]{2,1,0:T(8,128)} %get-tuple-element.59.gr_ref, bf16[20,384,200]{2,1,0:T(8,128)(2,1)} %get-tuple-element.60.ga_ref, ...), custom_call_target="tpu_custom_call" | custom-call | tf_op jit(solution)/shard_map/attention_backward/pallas_call | solution.py:893
  158.2 7.9 %unpack.1 = (f32[20,197,384]{2,1,0:T(8,128)}, f32[192]{0:T(256)}, f32[192]{0:T(256)}, f32[192,1152]{1,0:T(8,128)}, f32[192]{0:T(256)}, /*index=5*/f32[192]{0:T(2...) custom-call(bf16[20,197,384]{2,1,0:T(8,128)(2,1)} %get-tuple-element, ...), custom_call_target="tpu_custom_call" | custom-call | tf_op jit(solution)/shard_map/unpack/pallas_call | solution.py:940

commit v6 on v5

--- a/solution.py
+++ b/solution.py
@@ -310,9 +310,9 @@
 
 
 CHAINS = {
-    "a": (0, 1, 3, 5, 7, 9, 11, 12),
-    "b": (0, 1, 3, 5, 7, 9, 11, 12),
-    "c": (0, 3, 5, 7, 9, 11, 13, 14),
+    "a": (0, 1, 4, 6, 8, 11, 13, 14),
+    "b": (0, 1, 4, 6, 8, 11, 13, 14),
+    "c": (0, 4, 7, 9, 11, 13, 15, 16),
     0: (4, 5, 8, 10, 12, 13, 14, 15),
     1: (8, 9, 11, 13, 14, 15, 16, 16),
     2: (12, 13, 14, 16, 16, 16),
@@ -791,7 +791,7 @@
     fulls = [(members * w.shape[0], w.shape[1]) for w in weights]
     turned = (images, width, pitch)
     return pl.pallas_call(
-        functools.partial(attention_forward, length, pitch, count, 2),
+        functools.partial(attention_forward, length, pitch, count, 3),
         grid=(images // count,),
         in_specs=[whole(inputs)] + [HBM] * 4 + [whole(v) for v in vectors],
         out_specs=[
@@ -939,11 +939,11 @@
     weights = (gain_one, shift_one, w_qkv, b_query, b_value, w_proj, b_proj, gain_two, shift_two, w_fc1, b_fc1, w_fc2, b_fc2)
     grad_inputs, *grads = pl.pallas_call(
         functools.partial(unpack, factor),
-        grid=(4,),
-        in_specs=[blocks(images // 4, length, width), whole(fc_sum), whole(qkv_sum), whole(vec_sum)] + [
+        grid=(1,),
+        in_specs=[blocks(images, length, width), whole(fc_sum), whole(qkv_sum), whole(vec_sum)] + [
             whole(w) for w in (w_qkv, gain_one, shift_one)
         ],
-        out_specs=[blocks(images // 4, length, width)] + [whole(w) for w in weights],
+        out_specs=[blocks(images, length, width)] + [whole(w) for w in weights],
         out_shape=[sds(inputs.shape, F32)] + [sds(w.shape, F32) for w in weights],
         compiler_params=params(),
         name="unpack",

time: 166 us -> 158 us (0.952)
  Pallas kernels: 165 us -> 157 us
    pallas_call x1, Pallas kernels: 40.9 us -> 37 us  [forward_part(): pl.pallas_call(functools.partial(attention_forward, length, pitch, count,...]
    pallas_call x1, Pallas kernels: 65.7 us -> 62.2 us  [backward_part(): pl.pallas_call(functools.partial(attention_backward, length, pitch, count...]
where the time goes in v6:
time: 158 us
  Pallas kernels  157 us (99%)
    pallas_call x1, Pallas kernels, backward_part(): pl.pallas_call(functools.partial(attention_backward, length, pitch, count...  62.2 us
    pallas_call x1, Pallas kernels, middle_part(): pl.pallas_call(functools.partial(mlp_both, length, pitch, count, 256), gr...  51 us
    pallas_call x1, Pallas kernels, forward_part(): pl.pallas_call(functools.partial(attention_forward, length, pitch, count,...  37 us
    pallas_call x1, Pallas kernels, local(): pl.pallas_call(functools.partial(unpack, factor), grid=(1,), in_specs=[bl...  6.87 us

profile of v6, /device:TPU:0, one launch (start us, length us, event | category | flops | bytes accessed | tf_op | source)
XLA Modules:
  0.0 157.8 jit_solution(7509959190434306459)
XLA Ops:
  0.6 37.0 %attention_forward.1 = (bf16[20,384,200]{2,1,0:T(8,128)(2,1)}, bf16[20,384,200]{2,1,0:T(8,128)(2,1)}, bf16[20,200,384]{2,1,0:T(8,128)(2,1)}, bf16[20,6,200,200]{...) custom-call(bf16[20,197,384]{2,1,0:T(8,128)(2,1)} %x_ref.5, ...), custom_call_target="tpu_custom_call" | custom-call | tf_op jit(solution)/shard_map/attention_forward/pallas_call | solution.py:793
  37.6 51.0 %mlp_both.1 = (bf16[20,197,384]{2,1,0:T(8,128)(2,1)}, f32[20,200,384]{2,1,0:T(8,128)}, bf16[20,384,200]{2,1,0:T(8,128)(2,1)}, bf16[6,2,768,128]{3,2,1,0:T(8,128)...) custom-call(bf16[20,197,384]{2,1,0:T(8,128)(2,1)} %x_ref.5, bf16[20,197,384]{2,1,0:T(8,128)(2,1)} %ct_ref.1, ...), custom_call_target="tpu_custom_call" | custom-call | tf_op jit(solution)/shard_map/mlp_both/pallas_call | solution.py:829
  88.6 62.2 %attention_backward.1 = (bf16[20,197,384]{2,1,0:T(8,128)(2,1)}, bf16[6,768,128]{2,1,0:T(8,128)(2,1)}, bf16[3,768,128]{2,1,0:T(8,128)(2,1)}, f32[16,384]{1,0:T(8,128)}) custom-call(bf16[20,197,384]{2,1,0:T(8,128)(2,1)} %x_ref.5, f32[20,200,384]{2,1,0:T(8,128)} %get-tuple-element.59.gr_ref, bf16[20,384,200]{2,1,0:T(8,128)(2,1)} %get-tuple-element.60.ga_ref, ...), custom_call_target="tpu_custom_call" | custom-call | tf_op jit(solution)/shard_map/attention_backward/pallas_call | solution.py:893
  150.8 6.9 %unpack.1 = (f32[20,197,384]{2,1,0:T(8,128)}, f32[192]{0:T(256)}, f32[192]{0:T(256)}, f32[192,1152]{1,0:T(8,128)}, f32[192]{0:T(256)}, /*index=5*/f32[192]{0:T(2...) custom-call(bf16[20,197,384]{2,1,0:T(8,128)(2,1)} %get-tuple-element, ...), custom_call_target="tpu_custom_call" | custom-call | tf_op jit(solution)/shard_map/unpack/pallas_call | solution.py:940

commit v7 on v6

--- a/solution.py
+++ b/solution.py
@@ -314,12 +314,12 @@
     "b": (0, 1, 4, 6, 8, 11, 13, 14),
     "c": (0, 4, 7, 9, 11, 13, 15, 16),
     0: (4, 5, 8, 10, 12, 13, 14, 15),
-    1: (8, 9, 11, 13, 14, 15, 16, 16),
+    1: (8, 9, 12, 14, 16, 16),
     2: (12, 13, 14, 16, 16, 16),
     "v": (12, 13, 14, 15, 16),
 }
 SWAPPED = ("b", 0)
-SHORT = (2,)
+SHORT = (1, 2)
 
 
 def schedule(total):

time: 158 us -> 157 us (level)
  no operation moved by 1% of the time
where the time goes in v7:
time: 157 us
  Pallas kernels  156 us (99%)
    pallas_call x1, Pallas kernels, backward_part(): pl.pallas_call(functools.partial(attention_backward, length, pitch, count...  61.5 us
    pallas_call x1, Pallas kernels, middle_part(): pl.pallas_call(functools.partial(mlp_both, length, pitch, count, 256), gr...  51 us
    pallas_call x1, Pallas kernels, forward_part(): pl.pallas_call(functools.partial(attention_forward, length, pitch, count,...  37 us
    pallas_call x1, Pallas kernels, local(): pl.pallas_call(functools.partial(unpack, factor), grid=(1,), in_specs=[bl...  6.87 us

profile of v7, /device:TPU:0, one launch (start us, length us, event | category | flops | bytes accessed | tf_op | source)
XLA Modules:
  0.0 157.0 jit_solution(4456611864092140908)
XLA Ops:
  0.6 37.0 %attention_forward.1 = (bf16[20,384,200]{2,1,0:T(8,128)(2,1)}, bf16[20,384,200]{2,1,0:T(8,128)(2,1)}, bf16[20,200,384]{2,1,0:T(8,128)(2,1)}, bf16[20,6,200,200]{...) custom-call(bf16[20,197,384]{2,1,0:T(8,128)(2,1)} %x_ref.5, ...), custom_call_target="tpu_custom_call" | custom-call | tf_op jit(solution)/shard_map/attention_forward/pallas_call | solution.py:793
  37.6 51.0 %mlp_both.1 = (bf16[20,197,384]{2,1,0:T(8,128)(2,1)}, f32[20,200,384]{2,1,0:T(8,128)}, bf16[20,384,200]{2,1,0:T(8,128)(2,1)}, bf16[6,2,768,128]{3,2,1,0:T(8,128)...) custom-call(bf16[20,197,384]{2,1,0:T(8,128)(2,1)} %x_ref.5, bf16[20,197,384]{2,1,0:T(8,128)(2,1)} %ct_ref.1, ...), custom_call_target="tpu_custom_call" | custom-call | tf_op jit(solution)/shard_map/mlp_both/pallas_call | solution.py:829
  88.6 61.5 %attention_backward.1 = (bf16[20,197,384]{2,1,0:T(8,128)(2,1)}, bf16[6,768,128]{2,1,0:T(8,128)(2,1)}, bf16[3,768,128]{2,1,0:T(8,128)(2,1)}, f32[16,384]{1,0:T(8,128)}) custom-call(bf16[20,197,384]{2,1,0:T(8,128)(2,1)} %x_ref.5, f32[20,200,384]{2,1,0:T(8,128)} %get-tuple-element.59.gr_ref, bf16[20,384,200]{2,1,0:T(8,128)(2,1)} %get-tuple-element.60.ga_ref, ...), custom_call_target="tpu_custom_call" | custom-call | tf_op jit(solution)/shard_map/attention_backward/pallas_call | solution.py:893
  150.1 6.9 %unpack.1 = (f32[20,197,384]{2,1,0:T(8,128)}, f32[192]{0:T(256)}, f32[192]{0:T(256)}, f32[192,1152]{1,0:T(8,128)}, f32[192]{0:T(256)}, /*index=5*/f32[192]{0:T(2...) custom-call(bf16[20,197,384]{2,1,0:T(8,128)(2,1)} %get-tuple-element, ...), custom_call_target="tpu_custom_call" | custom-call | tf_op jit(solution)/shard_map/unpack/pallas_call | solution.py:940
